TPU v7x, 512 devices: a whole 4x8x8 slice. The times are simulated.
512 devices in a mesh: gx: 16 (over y, core), gy: 8 (over z), gz: 4 (over x).
Axes of the slice: x: 4, y: 8, z: 8, core: 2. Of those that a mesh axis runs over, the one named last changes fastest.
Arguments:
- charges: float32 [256, 256, 512], P('gx', 'gy', 'gz'), may hold values from -6 to 6
- term_width: float32 [2, 4], replicated, may hold values from 0.8 to 3.5
- term_weight: float32 [2, 4], replicated, may hold values from 0.5 to 2
Outputs:
- potential: float32 [256, 256, 512], P('gx', 'gy', 'gz')
All inputs are finite; a program needn't handle non-finite values.
Results may differ from a plain program's by a relative error of at most 0.00025.
Values sent between devices are 32-bit elements; how exact they have to be, the bound alone decides.
No kernel may reach another device: no remote copies, remote signals or barrier semaphores. Data moves between devices by JAX's collectives and lax.ppermute only.
A program may use at most 64 MiB of HBM per device.

v0:
```python
import math

import jax
import jax.numpy as jnp
from jax import lax
from jax.sharding import PartitionSpec as P

TERMS = 4
RADIUS = 8


HIGHEST = lax.Precision.HIGHEST
screening = 0.01
strength = 4.0


def extended(block, sides, width):
    for axis, dim in sides:
        count = lax.axis_size(axis)
        forward = [(i, i + 1) for i in range(count - 1)]
        forward.append((count - 1, 0))
        backward = [(target, source) for source, target in forward]
        low = lax.ppermute(
            lax.slice_in_dim(block, block.shape[dim] - width, None, axis=dim), axis, forward
        )
        high = lax.ppermute(lax.slice_in_dim(block, 0, width, axis=dim), axis, backward)
        block = jnp.concatenate([low, block, high], axis=dim)
    return block


def gaussian_taps(widths):
    offsets = jnp.arange(-RADIUS, RADIUS + 1).astype(widths.dtype)
    values = jnp.exp(-offsets[None, :] ** 2 / (2.0 * widths[:, None] ** 2))
    return values / jnp.sum(values, axis=1, keepdims=True)


def convolve(padded, taps, axis, length):
    total = taps[0] * lax.slice_in_dim(padded, 0, length, axis=axis)
    for offset in range(1, 2 * RADIUS + 1):
        total = total + taps[offset] * lax.slice_in_dim(padded, offset, offset + length, axis=axis)
    return total


def convolve_terms(padded, taps, axis, length):
    total = taps[:, 0][:, None, None, None] * lax.slice_in_dim(padded, 0, length, axis=axis)
    for offset in range(1, 2 * RADIUS + 1):
        total = total + taps[:, offset][:, None, None, None] * lax.slice_in_dim(
            padded, offset, offset + length, axis=axis
        )
    return total


def smooth_level(field, widths, weights):
    taps = gaussian_taps(widths)
    shape = field.shape
    result = None
    padded_x = extended(field, (("gx", 0),), RADIUS)
    first_pass = jnp.stack(
        [convolve(padded_x, taps[term_index], 0, shape[0]) for term_index in range(TERMS)]
    )
    padded_y = extended(first_pass, (("gy", 2),), RADIUS)
    second_pass = convolve_terms(padded_y, taps, 2, shape[1])
    padded_z = extended(second_pass, (("gz", 3),), RADIUS)
    third_pass = convolve_terms(padded_z, taps, 3, shape[2])
    for term_index in range(TERMS):
        contrib = weights[term_index] * third_pass[term_index]
        result = contrib if result is None else result + contrib
    return result


def restrict(field):
    shape = field.shape
    return field.reshape(shape[0] // 2, 2, shape[1] // 2, 2, shape[2] // 2, 2).mean(axis=(1, 3, 5))


def expand(field):
    return jnp.repeat(jnp.repeat(jnp.repeat(field, 2, axis=0), 2, axis=1), 2, axis=2)


def dft_tables(count):
    modes = jnp.arange(count, dtype=jnp.int32)
    product = modes[:, None] * modes[None, :] % count
    angles = 2.0 * math.pi / count * product.astype(jnp.float32)
    return (jnp.cos(angles), jnp.sin(angles))


def lam_modes(modes, count):
    return 2.0 - 2.0 * jnp.cos(2.0 * math.pi / count * modes.astype(jnp.float32))


def forward_axis(real_part, imag_part, cosine, sine, form):
    new_real = jnp.einsum(form, cosine, real_part, precision=HIGHEST) + jnp.einsum(
        form, sine, imag_part, precision=HIGHEST
    )
    new_imag = jnp.einsum(form, cosine, imag_part, precision=HIGHEST) - jnp.einsum(
        form, sine, real_part, precision=HIGHEST
    )
    return (new_real, new_imag)


def inverse_axis(real_part, imag_part, cosine, sine, form):
    new_real = jnp.einsum(form, cosine, real_part, precision=HIGHEST) - jnp.einsum(
        form, sine, imag_part, precision=HIGHEST
    )
    new_imag = jnp.einsum(form, cosine, imag_part, precision=HIGHEST) + jnp.einsum(
        form, sine, real_part, precision=HIGHEST
    )
    return (new_real, new_imag)


def solve_top(coarse):
    block_x, block_y, block_z = coarse.shape
    count_x = block_x * lax.axis_size("gx")
    count_y = block_y * lax.axis_size("gy")
    count_z = block_z * lax.axis_size("gz")
    column = lax.all_gather(coarse, "gx", axis=0, tiled=True)
    cos_x, sin_x = dft_tables(count_x)
    real_x = jnp.einsum("mx,xyz->myz", cos_x, column, precision=HIGHEST)
    imag_x = -jnp.einsum("mx,xyz->myz", sin_x, column, precision=HIGHEST)
    pencil = lax.all_to_all(
        lax.all_to_all(jnp.stack([real_x, imag_x]), "gy", split_axis=1, concat_axis=2, tiled=True),
        "gz",
        split_axis=1,
        concat_axis=3,
        tiled=True,
    )
    cos_y, sin_y = dft_tables(count_y)
    cos_z, sin_z = dft_tables(count_z)
    real_part, imag_part = forward_axis(pencil[0], pencil[1], cos_y, sin_y, "my,xyz->xmz")
    real_part, imag_part = forward_axis(real_part, imag_part, cos_z, sin_z, "mz,xyz->xym")
    rows_y = count_x // lax.axis_size("gy")
    rows_here = rows_y // lax.axis_size("gz")
    start = lax.axis_index("gy") * rows_y + lax.axis_index("gz") * rows_here
    modes_x = start + jnp.arange(rows_here, dtype=jnp.int32)
    lam = (
        lam_modes(modes_x, count_x)[:, None, None]
        + lam_modes(jnp.arange(count_y, dtype=jnp.int32), count_y)[None, :, None]
        + lam_modes(jnp.arange(count_z, dtype=jnp.int32), count_z)[None, None, :]
    )
    zeroed = lam <= 0.0
    mult = jnp.where(zeroed, 0.0, strength * jnp.exp(-lam) / (lam + screening))
    real_part = real_part * mult
    imag_part = imag_part * mult
    real_part, imag_part = inverse_axis(real_part, imag_part, cos_z, sin_z, "mz,xyz->xym")
    back_z = lax.all_to_all(
        jnp.stack([real_part, imag_part]), "gz", split_axis=3, concat_axis=1, tiled=True
    )
    real_part, imag_part = inverse_axis(back_z[0], back_z[1], cos_y, sin_y, "my,xyz->xmz")
    back_y = lax.all_to_all(
        jnp.stack([real_part, imag_part]), "gy", split_axis=2, concat_axis=1, tiled=True
    )
    whole = jnp.einsum("mx,xyz->myz", cos_x, back_y[0], precision=HIGHEST) - jnp.einsum(
        "mx,xyz->myz", sin_x, back_y[1], precision=HIGHEST
    )
    whole = whole / float(count_x * count_y * count_z)
    return lax.dynamic_slice_in_dim(whole, lax.axis_index("gx") * block_x, block_x, 0)


def shards(charges, term_width, term_weight):
    middle = restrict(charges)
    coarse = restrict(middle)
    distant = solve_top(coarse)
    near = smooth_level(charges, term_width[0], term_weight[0])
    between = smooth_level(middle, term_width[1], term_weight[1])
    return near + expand(between + expand(distant))


def solution(mesh):
    placed = (P("gx", "gy", "gz"), P(), P())
    return jax.shard_map(
        shards, mesh=mesh, in_specs=placed, out_specs=P("gx", "gy", "gz"), check_vma=False
    )
```

profile of v0, /device:TPU:6, one launch (start us, length us, event | category | flops | bytes accessed | tf_op | source)
XLA Modules:
  0.0 254.8 jit_solution(14744147205352669015)
XLA Ops:
  0.0 18.8 %reshape.481 = f32[8,2,16,2,64,2]{5,4,3,2,1,0:T(8,128)} reshape(f32[16,32,128]{2,1,0:T(8,128)} %param.3) | data formatting | bytes 524288 | tf_op jit(solution)/shard_map/reshape | solution.py:73
  18.8 7.0 %reduce_sum.38 = f32[8,16,64]{2,1,0:T(8,128)S(1)} reduce(f32[8,2,16,2,64,2]{5,4,3,2,1,0:T(8,128)} %reshape.481, f32[]{:T(128)} %constant.36.clone.1), dimensions={1,3,5}, to_apply=%region_2.3 | reduce | flops 57344 | bytes 294916 | tf_op jit(solution)/shard_map/reduce_sum | solution.py:73
  25.8 2.9 %collective-permute-start.7 = (f32[8,16,64]{2,1,0:T(8,128)S(1)}, f32[8,16,64]{2,1,0:T(8,128)S(1)}, u32[]{:S(2)}, u32[]{:S(2)}) collective-permute-start(f32[8,16,64]{2,1,0:T(8,128)S(1)} %broadcast_multiply_fusion), channel_id=1, source_target_pairs={{32,0},{64,32},{96,64},{128,96},{160,128},{192,160},{224,192},{256... | collective-permute-start | bytes 98312 | tf_op jit(solution)/shard_map/ppermute | solution.py:26
  28.8 2.1 div.76
  31.2 16.2 %all_gather.3 = f32[64,8,32]{2,1,0:T(8,128)S(1)} all-gather(f32[4,8,32]{2,1,0:T(8,128)S(1)} %broadcast_multiply_fusion.1), channel_id=1, replica_groups=mesh['gx'=16,'gy'=8,'gz'=4] {'gx'}, dimensions={0}, use_global_device_ids=true | all-gather | bytes 69632 | tf_op jit(solution)/shard_map/all_gather | solution.py:116
  47.3 0.6 fusion.2
  48.0 0.6 convolution_bitcast_fusion
  48.9 0.9 reshape.492
  49.8 10.3 %all-to-all-start = ((f32[8,1,4096]{2,1,0:T(1,128)}), f32[8,1,4096]{2,1,0:T(1,128)S(1)}, u32[]{:S(2)}, u32[]{:S(2)}) async-start(f32[8,1,4096]{2,1,0:T(1,128)} %reshape.492), calls=%async_computation | async-start | bytes 262144 | tf_op jit(solution)/shard_map/all_to_all | solution.py:121
  60.2 2.9 %collective-permute-start.1 = (f32[8,32,128]{2,1,0:T(8,128)S(1)}, f32[8,32,128]{2,1,0:T(8,128)S(1)}, u32[]{:S(2)}, u32[]{:S(2)}) collective-permute-start(f32[8,32,128]{2,1,0:T(8,128)S(1)} %get-tuple-element.31), channel_id=1, source_target_pairs={{32,0},{64,32},{96,64},{128,96},{160,128},{192,160},{224,192},{256... | collective-permute-start | bytes 393224 | tf_op jit(solution)/shard_map/ppermute | solution.py:26
  63.4 0.7 fusion.332
  64.1 0.7 fusion.330
  64.8 0.7 fusion.331
  65.6 0.7 fusion.326
  66.3 0.7 fusion.327
  67.0 0.7 fusion.328
  67.7 0.6 fusion.329
  68.4 0.6 slice_bitcast_fusion.33
  69.1 0.6 fusion.333
  72.3 9.9 %add_bitcast_fusion.7 = (f32[1,8,16,64]{3,2,1,0:T(8,128)S(1)}, f32[8,16,64]{2,1,0:T(8,128)S(1)}, f32[8,16,64]{2,1,0:T(8,128)S(1)}, f32[8,16,64]{2,1,0:T(8,128)S(...) fusion(f32[8,16,64]{2,1,0:T(8,128)S(1)} %collective-permute-don, ...), kind=kLoop, calls=%fused_computation.330 | loop fusion | flops 385024 | bytes 557124 | tf_op jit(solution)/shard_map/stack | solution.py:58
  82.2 10.1 %add_bitcast_fusion.4 = f32[1,8,16,64]{3,2,1,0:T(8,128)S(1)} fusion(f32[8,16,64]{2,1,0:T(8,128)S(1)} %collective-permute-done.7, f32[8,16,64]{2,1,0:T(8,128)S(1)} %get-tuple-element.19, f32[8,16,64]{2,1,0:T(8,128)S(1)} %get-tuple-element.18, f32[8,16,64]{2,1,0:T(8,128)S(1)} %get-tuple-element.17, f32[8,16,64]{2,1,0:T(8,128)S(1)} %get-tuple-element.16, ...), kind=kLoop, calls=%fused_computation.327 | loop fusion | flops 286720 | bytes 557124 | tf_op jit(solution)/shard_map/stack | solution.py:58
  92.4 10.1 %add_bitcast_fusion.5 = f32[1,8,16,64]{3,2,1,0:T(8,128)S(1)} fusion(f32[8,16,64]{2,1,0:T(8,128)S(1)} %collective-permute-done.7, f32[8,16,64]{2,1,0:T(8,128)S(1)} %get-tuple-element.19, f32[8,16,64]{2,1,0:T(8,128)S(1)} %get-tuple-element.18, f32[8,16,64]{2,1,0:T(8,128)S(1)} %get-tuple-element.17, f32[8,16,64]{2,1,0:T(8,128)S(1)} %get-tuple-element.16, ...), kind=kLoop, calls=%fused_computation.328 | loop fusion | flops 286720 | bytes 557124 | tf_op jit(solution)/shard_map/stack | solution.py:58
  102.4 9.9 %add_bitcast_fusion.6 = f32[1,8,16,64]{3,2,1,0:T(8,128)S(1)} fusion(f32[8,16,64]{2,1,0:T(8,128)S(1)} %collective-permute-done.7, f32[8,16,64]{2,1,0:T(8,128)S(1)} %get-tuple-element.19, f32[8,16,64]{2,1,0:T(8,128)S(1)} %get-tuple-element.18, f32[8,16,64]{2,1,0:T(8,128)S(1)} %get-tuple-element.17, f32[8,16,64]{2,1,0:T(8,128)S(1)} %get-tuple-element.16, ...), kind=kLoop, calls=%fused_computation.329 | loop fusion | flops 286720 | bytes 557124 | tf_op jit(solution)/shard_map/stack | solution.py:58
  112.4 3.9 %collective-permute-start.8 = (f32[4,8,8,64]{3,2,1,0:T(8,128)S(1)}, f32[4,8,8,64]{3,2,1,0:T(8,128)S(1)}, u32[]{:S(2)}, u32[]{:S(2)}) collective-permute-start(f32[4,8,8,64]{3,2,1,0:T(8,128)S(1)} %get-tuple-element.36), channel_id=1, source_target_pairs={{0,4},{4,8},{8,12},{12,16},{16,20},{20,24},{24,28},{28,0},{1,5},{5... | collective-permute-start | bytes 196616 | tf_op jit(solution)/shard_map/ppermute | solution.py:23
  116.4 3.1 %collective-permute-start.9 = (f32[4,8,8,64]{3,2,1,0:T(8,128)S(1)}, f32[4,8,8,64]{3,2,1,0:T(8,128)S(1)}, u32[]{:S(2)}, u32[]{:S(2)}) collective-permute-start(f32[4,8,8,64]{3,2,1,0:T(8,128)S(1)} %get-tuple-element.37), channel_id=1, source_target_pairs={{4,0},{8,4},{12,8},{16,12},{20,16},{24,20},{28,24},{0,28},{5,1},{9... | collective-permute-start | bytes 196616 | tf_op jit(solution)/shard_map/ppermute | solution.py:26
  119.5 0.7 fusion.334
  120.5 2.7 %collective-permute-done.9 = f32[4,8,8,64]{3,2,1,0:T(8,128)S(1)} collective-permute-done((f32[4,8,8,64]{3,2,1,0:T(8,128)S(1)}, f32[4,8,8,64]{3,2,1,0:T(8,128)S(1)}, u32[]{:S(2)}, u32[]{:S(2)}) %collective-permute-start.9) | collective-permute-done | bytes 65568 | tf_op jit(solution)/shard_map/ppermute | solution.py:26
  123.3 0.6 fusion.109
  124.0 2.7 %collective-permute-start.11 = (f32[4,8,16,8]{3,2,1,0:T(8,128)S(1)}, f32[4,8,16,8]{3,2,1,0:T(8,128)S(1)}, u32[]{:S(2)}, u32[]{:S(2)}) collective-permute-start(f32[4,8,16,8]{3,2,1,0:T(8,128)S(1)} %get-tuple-element.33), channel_id=1, source_target_pairs={{1,0},{2,1},{3,2},{0,3},{5,4},{6,5},{7,6},{4,7},{9,8},{10,9},{11,1... | collective-permute-start | bytes 49160 | tf_op jit(solution)/shard_map/ppermute | solution.py:26
  126.8 4.5 %collective-permute-start.10 = (f32[4,8,16,8]{3,2,1,0:T(8,128)S(1)}, f32[4,8,16,8]{3,2,1,0:T(8,128)S(1)}, u32[]{:S(2)}, u32[]{:S(2)}) collective-permute-start(f32[4,8,16,8]{3,2,1,0:T(8,128)S(1)} %get-tuple-element.32), channel_id=1, source_target_pairs={{0,1},{1,2},{2,3},{3,0},{4,5},{5,6},{6,7},{7,4},{8,9},{9,10},{10,1... | collective-permute-start | bytes 49160 | tf_op jit(solution)/shard_map/ppermute | solution.py:23
  131.3 2.2 collective-permute-done.11
  133.5 1.5 collective-permute-done.10
  135.0 2.2 fusion.72
  137.4 11.0 %add_bitcast_fusion = f32[1,16,32,128]{3,2,1,0:T(8,128)S(1)} fusion(f32[16,32,128]{2,1,0:T(8,128)S(1)} %copy-done, f32[24,32,128]{2,1,0:T(8,128)S(1)} %constant_dynamic-update-slice_fusion.2, f32[24,32,128]{2,1,0:T(8,128)S(1)} %get-tuple-element.28, f32[]{:T(128)} %bitcast.73, f32[]{:T(128)} %bitcast.72, f32[]{:T(128)} %bitcast.71, f32[]{:T(128)} %bitcast.70, ...), kind=kLoop, calls=%fused_computation.246 | loop fusion | flops 2162688 | bytes 4718660 | tf_op jit(solution)/shard_map/stack | solution.py:58
  148.4 10.8 %add_bitcast_fusion.1 = f32[1,16,32,128]{3,2,1,0:T(8,128)S(1)} fusion(f32[16,32,128]{2,1,0:T(8,128)S(1)} %copy-done, f32[24,32,128]{2,1,0:T(8,128)S(1)} %constant_dynamic-update-slice_fusion.2, f32[24,32,128]{2,1,0:T(8,128)S(1)} %get-tuple-element.28, f32[]{:T(128)} %bitcast.55, f32[]{:T(128)} %bitcast.54, f32[]{:T(128)} %bitcast.53, f32[]{:T(128)} %bitcast.52, ...), kind=kLoop, calls=%fused_computation.247 | loop fusion | flops 2162688 | bytes 4718660 | tf_op jit(solution)/shard_map/stack | solution.py:58
  159.1 10.7 %add_bitcast_fusion.2 = f32[1,16,32,128]{3,2,1,0:T(8,128)S(1)} fusion(f32[16,32,128]{2,1,0:T(8,128)S(1)} %copy-done, f32[24,32,128]{2,1,0:T(8,128)S(1)} %constant_dynamic-update-slice_fusion.2, f32[24,32,128]{2,1,0:T(8,128)S(1)} %get-tuple-element.28, f32[]{:T(128)} %bitcast.37, f32[]{:T(128)} %bitcast.36, f32[]{:T(128)} %bitcast.35, f32[]{:T(128)} %bitcast.34, ...), kind=kLoop, calls=%fused_computation.248 | loop fusion | flops 2162688 | bytes 4718660 | tf_op jit(solution)/shard_map/stack | solution.py:58
  169.9 10.9 %add_bitcast_fusion.3 = f32[1,16,32,128]{3,2,1,0:T(8,128)S(1)} fusion(f32[16,32,128]{2,1,0:T(8,128)S(1)} %copy-done, f32[24,32,128]{2,1,0:T(8,128)S(1)} %constant_dynamic-update-slice_fusion.2, f32[24,32,128]{2,1,0:T(8,128)S(1)} %get-tuple-element.28, f32[]{:T(128)} %bitcast.19, f32[]{:T(128)} %bitcast.18, f32[]{:T(128)} %bitcast.17, f32[]{:T(128)} %bitcast.16, ...), kind=kLoop, calls=%fused_computation.249 | loop fusion | flops 2162688 | bytes 4718660 | tf_op jit(solution)/shard_map/stack | solution.py:58
  181.3 0.9 reduce
  182.6 0.8 reshape.494
  183.4 6.9 %all-to-all-start.1 = ((f32[4,1,8192]{2,1,0:T(1,128)}), f32[4,1,8192]{2,1,0:T(1,128)S(1)}, u32[]{:S(2)}, u32[]{:S(2)}) async-start(f32[4,1,8192]{2,1,0:T(1,128)} %reshape.494), calls=%async_computation.1 | async-start | bytes 262144 | tf_op jit(solution)/shard_map/all_to_all | solution.py:120
  190.4 3.4 %collective-permute-start.2 = (f32[4,16,8,128]{3,2,1,0:T(8,128)S(1)}, f32[4,16,8,128]{3,2,1,0:T(8,128)S(1)}, u32[]{:S(2)}, u32[]{:S(2)}) collective-permute-start(f32[4,16,8,128]{3,2,1,0:T(8,128)S(1)} %get-tuple-element.24), channel_id=1, source_target_pairs={{0,4},{4,8},{8,12},{12,16},{16,20},{20,24},{24,28},{28,0},{1,5},{5... | collective-permute-start | bytes 786440 | tf_op jit(solution)/shard_map/ppermute | solution.py:23
  193.8 3.7 %collective-permute-start.3 = (f32[4,16,8,128]{3,2,1,0:T(8,128)S(1)}, f32[4,16,8,128]{3,2,1,0:T(8,128)S(1)}, u32[]{:S(2)}, u32[]{:S(2)}) collective-permute-start(f32[4,16,8,128]{3,2,1,0:T(8,128)S(1)} %get-tuple-element.25), channel_id=1, source_target_pairs={{4,0},{8,4},{12,8},{16,12},{20,16},{24,20},{28,24},{0,28},{5,1},{9... | collective-permute-start | bytes 786440 | tf_op jit(solution)/shard_map/ppermute | solution.py:26
  197.5 0.9 reduce.1
  201.1 0.5 fusion.5
  202.1 0.5 fusion.6
  203.2 0.5 fusion.3
  203.7 0.5 fusion.4
  204.4 0.9 reshape.496
  205.3 4.8 %all-to-all-start.2 = ((f32[4,1,8192]{2,1,0:T(1,128)}), f32[4,1,8192]{2,1,0:T(1,128)S(1)}, u32[]{:S(2)}, u32[]{:S(2)}) async-start(f32[4,1,8192]{2,1,0:T(1,128)} %reshape.496), calls=%async_computation.2 | async-start | bytes 262144 | tf_op jit(solution)/shard_map/all_to_all | solution.py:145
  210.9 2.4 fusion.55
  213.7 1.0 copy.259
  214.8 2.8 %collective-permute-start.5 = (f32[4,16,32,8]{2,3,1,0:T(8,128)}, f32[4,16,32,8]{2,3,1,0:T(8,128)S(1)}, u32[]{:S(2)}, u32[]{:S(2)}) collective-permute-start(f32[4,16,32,8]{2,3,1,0:T(8,128)} %copy.259), channel_id=1, source_target_pairs={{1,0},{2,1},{3,2},{0,3},{5,4},{6,5},{7,6},{4,7},{9,8},{10,9},{11,1... | collective-permute-start | bytes 196616 | tf_op jit(solution)/shard_map/ppermute | solution.py:26
  217.8 4.3 %collective-permute-start.4 = (f32[4,16,32,8]{2,3,1,0:T(8,128)S(1)}, f32[4,16,32,8]{2,3,1,0:T(8,128)}, u32[]{:S(2)}, u32[]{:S(2)}) collective-permute-start(f32[4,16,32,8]{2,3,1,0:T(8,128)S(1)} %copy.257), channel_id=1, source_target_pairs={{0,1},{1,2},{2,3},{3,0},{4,5},{5,6},{6,7},{7,4},{8,9},{9,10},{10,1... | collective-permute-start | bytes 196616 | tf_op jit(solution)/shard_map/ppermute | solution.py:23
  222.1 0.9 reduce.2
  225.3 0.9 reshape.498
  226.2 6.4 %all-to-all-start.3 = ((f32[8,1,4096]{2,1,0:T(1,128)}), f32[8,1,4096]{2,1,0:T(1,128)S(1)}, u32[]{:S(2)}, u32[]{:S(2)}) async-start(f32[8,1,4096]{2,1,0:T(1,128)} %reshape.498), calls=%async_computation.3 | async-start | bytes 262144 | tf_op jit(solution)/shard_map/all_to_all | solution.py:149
  233.0 1.3 copy.258
  234.3 10.2 %fusion.12 = f32[4,16,32,128]{3,2,1,0:T(8,128)} fusion(f32[4,16,32,128]{3,2,1,0:T(8,128)S(1)} %fusion.55, f32[4,16,32,8]{3,2,1,0:T(8,128)S(1)} %copy.260, f32[4,16,32,8]{3,2,1,0:T(8,128)S(1)} %copy.258, f32[4]{0:T(128)S(1)} %get-tuple-element.43, f32[4]{0:T(128)S(1)} %get-tuple-element.44, f32[4]{0:T(128)S(1)} %get-tuple-element.45, f32[4]{0:T(128)} %get-tuple-element.46, ...), kind=kLoop, calls=%fused_computation.52 | loop fusion | flops 12845056 | bytes 2228496 | tf_op jit(solution)/shard_map/add | solution.py:47
  244.5 0.9 reduce.3
  245.8 0.5 fusion.130
  246.3 0.5 fusion.132
  247.2 2.6 %fusion.157 = f32[8,16,64]{2,1,0:T(8,128)S(1)} fusion(f32[8,16,64]{2,1,0:T(8,128)S(1)} %copy.285, f32[4,8,16,64]{3,2,1,0:T(8,128)S(1)} %fusion.72, f32[]{:T(128)} %bitcast.188, f32[]{:T(128)} %bitcast.187, f32[]{:T(128)} %bitcast.186, f32[]{:T(128)} %bitcast.95), kind=kLoop, calls=%fused_computation.305 | loop fusion | flops 65536 | bytes 196624 | tf_op jit(solution)/shard_map/add | solution.py:165
  250.7 0.7 copy-done.1
  251.4 3.4 %fusion.127 = f32[16,32,128]{2,1,0:T(8,128)} fusion(f32[16,32,128]{2,1,0:T(8,128)S(1)} %copy.288, f32[4,16,32,128]{3,2,1,0:T(8,128)S(1)} %copy-done.1, f32[]{:T(128)} %bitcast.93, f32[]{:T(128)} %bitcast.92, f32[]{:T(128)} %bitcast.91, f32[]{:T(128)} %bitcast), kind=kLoop, calls=%fused_computation.233 | loop fusion | flops 524288 | bytes 1572880 | tf_op jit(solution)/shard_map/add | solution.py:165
  (123 shorter events, 12.1 us)
Async XLA Ops:
  25.8 46.4 %collective-permute-start.7 = (f32[8,16,64]{2,1,0:T(8,128)S(1)}, f32[8,16,64]{2,1,0:T(8,128)S(1)}, u32[]{:S(2)}, u32[]{:S(2)}) collective-permute-start(f32[8,16,64]{2,1,0:T(8,128)S(1)} %broadcast_multiply_fusion), channel_id=1, source_target_pairs={{32,0},{64,32},{96,64},{128,96},{160,128},{192,160},{224,192},{256... | collective-permute-start | bytes 98312 | tf_op jit(solution)/shard_map/ppermute | solution.py:26
  28.8 43.5 %collective-permute-start.6 = (f32[8,16,64]{2,1,0:T(8,128)S(1)}, f32[8,16,64]{2,1,0:T(8,128)S(1)}, u32[]{:S(2)}, u32[]{:S(2)}) collective-permute-start(f32[8,16,64]{2,1,0:T(8,128)S(1)} %broadcast_multiply_fusion), channel_id=1, source_target_pairs={{0,32},{32,64},{64,96},{96,128},{128,160},{160,192},{192,224},{224... | collective-permute-start | bytes 98312 | tf_op jit(solution)/shard_map/ppermute | solution.py:23
  47.9 12.2 %copy-start = (f32[16,32,128]{2,1,0:T(8,128)S(1)}, f32[16,32,128]{2,1,0:T(8,128)}, u32[]{:S(2)}) copy-start(f32[16,32,128]{2,1,0:T(8,128)} %param.3) | copy-start | bytes 786436
  48.5 14.6 %copy-start.16 = (f32[2,4]{1,0:T(2,128)S(1)}, f32[2,4]{1,0:T(2,128)}, u32[]{:S(2)}) copy-start(f32[2,4]{1,0:T(2,128)} %param.4) | copy-start | bytes 100
  49.8 131.0 %all-to-all-start = ((f32[8,1,4096]{2,1,0:T(1,128)}), f32[8,1,4096]{2,1,0:T(1,128)S(1)}, u32[]{:S(2)}, u32[]{:S(2)}) async-start(f32[8,1,4096]{2,1,0:T(1,128)} %reshape.492), calls=%async_computation | async-start | bytes 262144 | tf_op jit(solution)/shard_map/all_to_all | solution.py:121
  60.1 77.2 %collective-permute-start = (f32[8,32,128]{2,1,0:T(8,128)S(1)}, f32[8,32,128]{2,1,0:T(8,128)S(1)}, u32[]{:S(2)}, u32[]{:S(2)}) collective-permute-start(f32[8,32,128]{2,1,0:T(8,128)S(1)} %get-tuple-element.30), channel_id=1, source_target_pairs={{0,32},{32,64},{64,96},{96,128},{128,160},{160,192},{192,224},{224... | collective-permute-start | bytes 393224 | tf_op jit(solution)/shard_map/ppermute | solution.py:23
  60.2 77.2 %collective-permute-start.1 = (f32[8,32,128]{2,1,0:T(8,128)S(1)}, f32[8,32,128]{2,1,0:T(8,128)S(1)}, u32[]{:S(2)}, u32[]{:S(2)}) collective-permute-start(f32[8,32,128]{2,1,0:T(8,128)S(1)} %get-tuple-element.31), channel_id=1, source_target_pairs={{32,0},{64,32},{96,64},{128,96},{160,128},{192,160},{224,192},{256... | collective-permute-start | bytes 393224 | tf_op jit(solution)/shard_map/ppermute | solution.py:26
  102.4 17.1 %copy-start.2 = (f32[2,4]{1,0:T(2,128)S(1)}, f32[2,4]{1,0:T(2,128)}, u32[]{:S(2)}) copy-start(f32[2,4]{1,0:T(2,128)} %param.5) | copy-start | bytes 100
  112.4 8.1 %collective-permute-start.8 = (f32[4,8,8,64]{3,2,1,0:T(8,128)S(1)}, f32[4,8,8,64]{3,2,1,0:T(8,128)S(1)}, u32[]{:S(2)}, u32[]{:S(2)}) collective-permute-start(f32[4,8,8,64]{3,2,1,0:T(8,128)S(1)} %get-tuple-element.36), channel_id=1, source_target_pairs={{0,4},{4,8},{8,12},{12,16},{16,20},{20,24},{24,28},{28,0},{1,5},{5... | collective-permute-start | bytes 196616 | tf_op jit(solution)/shard_map/ppermute | solution.py:23
  116.4 6.9 %collective-permute-start.9 = (f32[4,8,8,64]{3,2,1,0:T(8,128)S(1)}, f32[4,8,8,64]{3,2,1,0:T(8,128)S(1)}, u32[]{:S(2)}, u32[]{:S(2)}) collective-permute-start(f32[4,8,8,64]{3,2,1,0:T(8,128)S(1)} %get-tuple-element.37), channel_id=1, source_target_pairs={{4,0},{8,4},{12,8},{16,12},{20,16},{24,20},{28,24},{0,28},{5,1},{9... | collective-permute-start | bytes 196616 | tf_op jit(solution)/shard_map/ppermute | solution.py:26
  124.0 9.5 %collective-permute-start.11 = (f32[4,8,16,8]{3,2,1,0:T(8,128)S(1)}, f32[4,8,16,8]{3,2,1,0:T(8,128)S(1)}, u32[]{:S(2)}, u32[]{:S(2)}) collective-permute-start(f32[4,8,16,8]{3,2,1,0:T(8,128)S(1)} %get-tuple-element.33), channel_id=1, source_target_pairs={{1,0},{2,1},{3,2},{0,3},{5,4},{6,5},{7,6},{4,7},{9,8},{10,9},{11,1... | collective-permute-start | bytes 49160 | tf_op jit(solution)/shard_map/ppermute | solution.py:26
  126.8 8.3 %collective-permute-start.10 = (f32[4,8,16,8]{3,2,1,0:T(8,128)S(1)}, f32[4,8,16,8]{3,2,1,0:T(8,128)S(1)}, u32[]{:S(2)}, u32[]{:S(2)}) collective-permute-start(f32[4,8,16,8]{3,2,1,0:T(8,128)S(1)} %get-tuple-element.32), channel_id=1, source_target_pairs={{0,1},{1,2},{2,3},{3,0},{4,5},{5,6},{6,7},{7,4},{8,9},{9,10},{10,1... | collective-permute-start | bytes 49160 | tf_op jit(solution)/shard_map/ppermute | solution.py:23
  183.4 14.0 %all-to-all-start.1 = ((f32[4,1,8192]{2,1,0:T(1,128)}), f32[4,1,8192]{2,1,0:T(1,128)S(1)}, u32[]{:S(2)}, u32[]{:S(2)}) async-start(f32[4,1,8192]{2,1,0:T(1,128)} %reshape.494), calls=%async_computation.1 | async-start | bytes 262144 | tf_op jit(solution)/shard_map/all_to_all | solution.py:120
  190.4 19.8 %collective-permute-start.2 = (f32[4,16,8,128]{3,2,1,0:T(8,128)S(1)}, f32[4,16,8,128]{3,2,1,0:T(8,128)S(1)}, u32[]{:S(2)}, u32[]{:S(2)}) collective-permute-start(f32[4,16,8,128]{3,2,1,0:T(8,128)S(1)} %get-tuple-element.24), channel_id=1, source_target_pairs={{0,4},{4,8},{8,12},{12,16},{16,20},{20,24},{24,28},{28,0},{1,5},{5... | collective-permute-start | bytes 786440 | tf_op jit(solution)/shard_map/ppermute | solution.py:23
  193.8 16.5 %collective-permute-start.3 = (f32[4,16,8,128]{3,2,1,0:T(8,128)S(1)}, f32[4,16,8,128]{3,2,1,0:T(8,128)S(1)}, u32[]{:S(2)}, u32[]{:S(2)}) collective-permute-start(f32[4,16,8,128]{3,2,1,0:T(8,128)S(1)} %get-tuple-element.25), channel_id=1, source_target_pairs={{4,0},{8,4},{12,8},{16,12},{20,16},{24,20},{28,24},{0,28},{5,1},{9... | collective-permute-start | bytes 786440 | tf_op jit(solution)/shard_map/ppermute | solution.py:26
  205.3 16.8 %all-to-all-start.2 = ((f32[4,1,8192]{2,1,0:T(1,128)}), f32[4,1,8192]{2,1,0:T(1,128)S(1)}, u32[]{:S(2)}, u32[]{:S(2)}) async-start(f32[4,1,8192]{2,1,0:T(1,128)} %reshape.496), calls=%async_computation.2 | async-start | bytes 262144 | tf_op jit(solution)/shard_map/all_to_all | solution.py:145
  210.1 0.6 copy-start.3
  210.1 0.7 copy-start.4
  210.1 0.7 copy-start.5
  210.1 0.7 copy-start.6
  210.1 0.7 copy-start.7
  210.1 0.7 copy-start.8
  210.2 0.7 copy-start.9
  210.2 0.7 copy-start.10
  210.2 0.7 copy-start.11
  210.2 0.7 copy-start.12
  210.2 0.7 copy-start.13
  210.2 0.7 copy-start.14
  210.2 0.7 copy-start.15
  214.8 17.8 %collective-permute-start.5 = (f32[4,16,32,8]{2,3,1,0:T(8,128)}, f32[4,16,32,8]{2,3,1,0:T(8,128)S(1)}, u32[]{:S(2)}, u32[]{:S(2)}) collective-permute-start(f32[4,16,32,8]{2,3,1,0:T(8,128)} %copy.259), channel_id=1, source_target_pairs={{1,0},{2,1},{3,2},{0,3},{5,4},{6,5},{7,6},{4,7},{9,8},{10,9},{11,1... | collective-permute-start | bytes 196616 | tf_op jit(solution)/shard_map/ppermute | solution.py:26
  217.8 15.1 %collective-permute-start.4 = (f32[4,16,32,8]{2,3,1,0:T(8,128)S(1)}, f32[4,16,32,8]{2,3,1,0:T(8,128)}, u32[]{:S(2)}, u32[]{:S(2)}) collective-permute-start(f32[4,16,32,8]{2,3,1,0:T(8,128)S(1)} %copy.257), channel_id=1, source_target_pairs={{0,1},{1,2},{2,3},{3,0},{4,5},{5,6},{6,7},{7,4},{8,9},{9,10},{10,1... | collective-permute-start | bytes 196616 | tf_op jit(solution)/shard_map/ppermute | solution.py:23
  226.2 18.3 %all-to-all-start.3 = ((f32[8,1,4096]{2,1,0:T(1,128)}), f32[8,1,4096]{2,1,0:T(1,128)S(1)}, u32[]{:S(2)}, u32[]{:S(2)}) async-start(f32[8,1,4096]{2,1,0:T(1,128)} %reshape.498), calls=%async_computation.3 | async-start | bytes 262144 | tf_op jit(solution)/shard_map/all_to_all | solution.py:149
  250.2 1.2 copy-start.1
where the time goes:
time: 257 us; the launch traced here: 255 us
  other arithmetic  116 us (45%)
  starting transfers between devices  62.7 us (24%)
  local copies, waits for them, and re-layouts  40.1 us (16%)
  blocking collectives  16.2 us (6%)
  matrix products  9.32 us (4%)
  waiting for transfers between devices  6.77 us (3%)
  between operations  3.4 us (1%)
    another operation x10, other arithmetic, smooth_level(): jnp.stack([convolve(padded_x, taps[term_index], 0, shape[0]) for term_ind...  83.5 us
    reshape x1, local copies, waits for them, and re-layouts, restrict(): field.reshape(shape[0] // 2, 2, shape[1] // 2, 2, shape[2] // 2, 2)  18.8 us
    ppermute x6, starting transfers between devices, extended(): lax.ppermute(lax.slice_in_dim(block, 0, width, axis=dim), axis, backward)  18.1 us
    all_gather x1, blocking collectives, solve_top(): column = lax.all_gather(coarse, 'gx', axis=0, tiled=True)  16.2 us
    ppermute x6, starting transfers between devices, extended(): lax.ppermute(lax.slice_in_dim(block, block.shape[dim] - width, None, axis...  16.2 us
    add x4, other arithmetic, convolve_terms(): total + taps[:, offset][:, None, None, None] * lax.slice_in_dim(padded, o...  15.5 us
    all_to_all x1, starting transfers between devices, solve_top(): lax.all_to_all(jnp.stack([real_x, imag_x]), 'gy', split_axis=1, concat_ax...  10.3 us
    reduce_sum x2, other arithmetic, restrict(): field.reshape(shape[0] // 2, 2, shape[1] // 2, 2, shape[2] // 2, 2)  7.22 us
  transfers between devices with their start and end apart: 16, of which 4 were waited for; matrix products, arithmetic and copies ran while one was open for 50% of the time, Pallas kernels for 0%

commit v1 on v0

v1 whole, which is shorter than its diff:
```python
import math

import jax
import jax.numpy as jnp
import numpy as np
from jax import lax
from jax.experimental import pallas as pl
from jax.experimental.pallas import tpu as pltpu
from jax.sharding import PartitionSpec as P

TERMS = 4
RADIUS = 8
TAPS = RADIUS + 1

HIGHEST = lax.Precision.HIGHEST
F32 = jnp.float32
BF16 = jnp.bfloat16
screening = 0.01
strength = 4.0

BX, BY, BZ = 16, 32, 128
MX, MY, MZ = 8, 16, 64
CX, CY, CZ = 64, 64, 128
EY, EMY = BY + 2 * RADIUS, MY + 2 * RADIUS
GX, GY, GZ = 16, 8, 4
YROWS = BX * 8 + 2 * 8 + 5 * 8
XROWS = 8 * EY + EY + 5 * EMY


def cas_table(count):
    modes = np.arange(count)
    angles = 2.0 * math.pi / count * (np.outer(modes, modes) % count)
    return np.cos(angles) + np.sin(angles)


def constant_tables():
    cas_y, cas_z = cas_table(CY), cas_table(CZ)

    def lam(count):
        return 2.0 - 2.0 * np.cos(2.0 * math.pi / count * np.arange(count))

    total = lam(CX)[:, None, None] + lam(CY)[None, :, None] + lam(CZ)[None, None, :]
    mult = strength * np.exp(-total) / (total + screening)
    mult[0, 0, 0] = 0.0
    shifts = np.arange(CX // 2 + 1)
    cosine = np.cos(2.0 * math.pi / CX * (np.outer(shifts, np.arange(CX)) % CX))
    along_x = np.einsum("dm,myz->dyz", cosine, mult) / (CX * CY * CZ)
    own_z = np.stack([np.tile(cas_z[:, 32 * g : 32 * g + 32], (1, 4)) for g in range(GZ)])
    fine = np.arange(BZ)
    pairs = np.zeros((BZ, BZ))
    pairs[fine, fine // 2] = 1.0 / 8.0
    pairs[fine, 64 + fine // 4] = 1.0 / 64.0
    spread = np.zeros((BZ, 4 * BZ))
    for block in range(4):
        spread[block * 32 + fine // 4, block * BZ + fine] = 1.0
    rows = np.zeros((MY, 8))
    rows[np.arange(MY), np.arange(MY) // 2] = 1.0
    return [np.asarray(t, np.float32) for t in (cas_y, cas_z, along_x, own_z, pairs, spread, rows)]


def lanes(shape):
    return lax.broadcasted_iota(jnp.int32, shape, len(shape) - 1)


def roll(value, shift):
    shift %= 128
    return pltpu.roll(value, shift, 1) if shift else value


def dot(a, b):
    return jnp.dot(a, b, preferred_element_type=F32)


def exact(a, b):
    return jnp.dot(a, b, preferred_element_type=F32, precision=HIGHEST)


def halves(value):
    high = value.astype(BF16)
    return high, (value - high.astype(F32)).astype(BF16)


def weights_kernel(width_ref, weight_ref, gy_ref, gzh_ref, gzl_ref, my_ref, mzh_ref, mzl_ref, cx_ref):
    def scale(level, term):
        width = jnp.full((8, 128), width_ref[level, term], F32)
        inverse = 1.0 / (2.0 * width * width)
        offset = lanes((8, 128)) - RADIUS
        values = jnp.exp(-(offset * offset).astype(F32) * inverse)
        values = jnp.where(offset <= RADIUS, values, 0.0)
        norm = 1.0 / jnp.sum(values, axis=1, keepdims=True)
        return inverse[0:1, 0:1], norm[0:1, 0:1]

    def taps(offset, inverse, norm):
        values = jnp.exp(-(offset * offset).astype(F32) * inverse) * norm
        return jnp.where(jnp.abs(offset) <= RADIUS, values, 0.0)

    def along_y(ref, term, inverse, norm, out, ext):
        shape = (out, 3 * ext)
        column = lanes(shape)
        row = lax.broadcasted_iota(jnp.int32, shape, 0)
        part = (column >= ext).astype(jnp.int32) + (column >= 2 * ext).astype(jnp.int32)
        high, low = halves(taps(column - part * ext - RADIUS - row, inverse, norm))
        ref[term * out : (term + 1) * out, :] = jnp.where(part < 2, high.astype(F32), low.astype(F32)).astype(BF16)

    for term in range(TERMS):
        inverse, norm = scale(0, term)
        along_y(gy_ref, term, inverse, norm, BY, EY)
        shape = (256, 128)
        row = lax.broadcasted_iota(jnp.int32, shape, 0)
        slot = row & 15
        place = jnp.where(row < BZ, row, jnp.where(slot < 8, slot - 8, BZ - 8 + slot))
        high, low = halves(taps(place - lanes(shape), inverse, norm))
        gzh_ref[term] = high
        gzl_ref[term] = low
        for offset in range(TAPS):
            value = jnp.exp(-float(offset * offset) * inverse) * norm * weight_ref[0, term]
            cx_ref[term * TAPS + offset] = jnp.broadcast_to(value, (8, 128))

        inverse, norm = scale(1, term)
        along_y(my_ref, term, inverse, norm, MY, EMY)
        shape = (128, 128)
        row = lax.broadcasted_iota(jnp.int32, shape, 0)
        place = jnp.where(row < MZ, row, jnp.where(row < MZ + 8, row - MZ - 8, row - 8))
        values = taps(place - (lanes(shape) >> 1), inverse, norm)
        high, low = halves(jnp.where(row < MZ + 16, values, 0.0))
        mzh_ref[term] = high
        mzl_ref[term] = low
        for offset in range(TAPS):
            value = jnp.exp(-float(offset * offset) * inverse) * norm * weight_ref[1, term]
            cx_ref[(TERMS + term) * TAPS + offset] = jnp.broadcast_to(value, (8, 128))


def restrict_kernel(f_ref, pairs_ref, coarse_ref, mid_ref, zmsg_ref, half_ref):
    planes = []
    for x in range(MX):
        total = None
        for plane in (2 * x, 2 * x + 1):
            for odd in (0, 1):
                part = f_ref[plane, pl.ds(odd, MY, stride=2), :]
                total = part if total is None else total + part
        planes.append(total)
    half_ref[...] = exact(jnp.concatenate(planes, axis=0), pairs_ref[...])
    lane = lanes((8, 128))
    coarse = jnp.zeros((8, 128), F32)
    for x in range(4):
        part = None
        for row in (2 * x * MY, 2 * x * MY + 1, (2 * x + 1) * MY, (2 * x + 1) * MY + 1):
            piece = half_ref[pl.ds(row, 8, stride=2), :]
            part = piece if part is None else part + piece
        coarse = jnp.where((lane >> 5) == x, roll(part, x * 32 - 64), coarse)
    for target in range(GY * GZ):
        coarse_ref[target] = coarse

    me = lax.axis_index("gz")
    up, down = lax.rem(me + 1, GZ), lax.rem(me + GZ - 1, GZ)
    zmsg_ref[...] = jnp.zeros_like(zmsg_ref)
    slot = lanes((BY, 128)) >> 3
    for group in range(2):
        rising = jnp.zeros((BY, 128), F32)
        falling = jnp.zeros((BY, 128), F32)
        for x in range(8):
            plane = f_ref[group * 8 + x]
            rising = jnp.where(slot == 2 * x, roll(plane, x * 16 - 120), rising)
            falling = jnp.where(slot == 2 * x + 1, roll(plane, x * 16 + 8), falling)
        zmsg_ref[up, group * BY : (group + 1) * BY, :] = rising
        zmsg_ref[down, group * BY : (group + 1) * BY, :] = falling
    slot = lanes((MY, 128)) >> 3
    rising = jnp.zeros((MY, 128), F32)
    falling = jnp.zeros((MY, 128), F32)
    middle = []
    for x in range(MX):
        plane = half_ref[x * MY : (x + 1) * MY, :]
        middle.append(plane)
        rising = jnp.where(slot == 2 * x, roll(plane, x * 16 - 56), rising)
        falling = jnp.where(slot == 2 * x + 1, roll(plane, x * 16 + 8), falling)
    zmsg_ref[up, 2 * BY : 2 * BY + MY, :] = rising
    zmsg_ref[down, 2 * BY : 2 * BY + MY, :] = falling
    for x in range(4):
        mid_ref[x] = jnp.where(slot < 8, middle[x], roll(middle[x + 4], 64))


def modes_kernel(slab_ref, cas_y_ref, cas_z_ref, along_ref, own_z_ref, out_ref):
    rows = [jnp.concatenate([slab_ref[gy * GZ + gz] for gz in range(GZ)], axis=1) for gy in range(GY)]
    by_y = exact(cas_y_ref[...], jnp.concatenate(rows, axis=0))
    lane = lanes((CY, 128)) >> 5
    planes = []
    for x in range(4):
        plane = jnp.zeros((CY, 128), F32)
        for gz in range(GZ):
            plane = jnp.where(lane == gz, roll(by_y[:, gz * 128 : (gz + 1) * 128], (gz - x) * 32), plane)
        planes.append(plane)
    by_z = exact(jnp.concatenate(planes, axis=0), cas_z_ref[...])
    source = [by_z[x * CY : (x + 1) * CY, :] for x in range(4)]
    own_y = cas_y_ref[pl.ds(pl.multiple_of(lax.axis_index("gy") * 8, 8), 8), :]
    own_z = own_z_ref[lax.axis_index("gz")]
    me = lax.axis_index("gx")
    lane = lanes((8, 128)) >> 5
    for block in range(GX):
        outs = []
        for x in range(4):
            total = None
            for other in range(4):
                shift = (block * 4 + x - other) % CX
                part = along_ref[min(shift, CX - shift)] * source[other]
                total = part if total is None else total + part
            outs.append(total)
        back_y = exact(own_y, jnp.concatenate(outs, axis=1))
        back_z = exact(
            jnp.concatenate([back_y[:, x * 128 : (x + 1) * 128] for x in range(4)], axis=0), own_z
        )
        result = back_z[0:8]
        for x in range(1, 4):
            result = jnp.where(lane == x, back_z[x * 8 : (x + 1) * 8], result)
        out_ref[lax.rem(me + block, GX)] = result


def y_message_kernel(f_ref, mid_ref, zrecv_ref, halo_ref, up_ref, down_ref):
    me = lax.axis_index("gz")
    halo = zrecv_ref[lax.rem(me + GZ - 1, GZ)] + zrecv_ref[lax.rem(me + 1, GZ)]
    halo_ref[...] = halo
    for ref, fine, middle in ((up_ref, BY - 8, MY - 8), (down_ref, 0, 0)):
        for x in range(BX):
            ref[x * 8 : x * 8 + 8, :] = f_ref[x, fine : fine + 8, :]
        for group in range(2):
            ref[128 + group * 8 : 136 + group * 8, :] = halo[group * BY + fine : group * BY + fine + 8]
        for x in range(4):
            ref[144 + x * 8 : 152 + x * 8, :] = mid_ref[x, middle : middle + 8, :]
        ref[176:184, :] = halo[2 * BY + middle : 2 * BY + middle + 8]


def own_extended(f_ref, mid_ref, halo_ref, low_ref, high_ref):
    def joined(row, inner):
        return jnp.concatenate([low_ref[row : row + 8, :], inner, high_ref[row : row + 8, :]], axis=0)

    planes = [lambda x=x: joined(x * 8, f_ref[x]) for x in range(BX)]
    sides = [lambda g=g: joined(128 + g * 8, halo_ref[g * BY : (g + 1) * BY, :]) for g in range(2)]
    middle = [lambda x=x: joined(144 + x * 8, mid_ref[x]) for x in range(4)]
    edge = lambda: joined(176, halo_ref[2 * BY : 2 * BY + MY, :])
    return planes, sides, middle, edge


def x_message_kernel(f_ref, mid_ref, halo_ref, low_ref, high_ref, up_ref, down_ref):
    planes, sides, middle, edge = own_extended(f_ref, mid_ref, halo_ref, low_ref, high_ref)
    for ref, first, group in ((up_ref, 8, 1), (down_ref, 0, 0)):
        for x in range(8):
            ref[x * EY : (x + 1) * EY, :] = planes[first + x]()
        ref[8 * EY : 9 * EY, :] = sides[group]()
        for x in range(4):
            ref[9 * EY + x * EMY : 9 * EY + (x + 1) * EMY, :] = middle[x]()
        ref[9 * EY + 4 * EMY : 9 * EY + 5 * EMY, :] = edge()


def filter_yz(planes, sides, gy, gzh_ref, gzl_ref, out_ref, places):
    for group in range(2):
        data = jnp.concatenate([planes[group * 8 + x]() for x in range(8)] + [sides[group]()], axis=1)
        high, low = halves(data)
        by_y = dot(gy, jnp.concatenate([high, low, high], axis=0))
        slot = lanes((BY, 128)) >> 4
        for term in range(TERMS):
            rows = by_y[term * BY : (term + 1) * BY, :]
            side = rows[:, 8 * 128 :]
            left = jnp.concatenate([rows[:, x * 128 : (x + 1) * 128] for x in range(8)], axis=0)
            right = jnp.concatenate([jnp.where(slot == x, side, 0.0) for x in range(8)], axis=0)
            high, low = halves(jnp.concatenate([left, right], axis=1))
            gzh = gzh_ref[term]
            result = dot(high, gzh) + dot(low, gzh) + dot(high, gzl_ref[term])
            for x in range(8):
                out_ref[term, places[group * 8 + x]] = result[x * BY : (x + 1) * BY]


def filter_middle(middle, edge, my, mzh_ref, mzl_ref, out_ref, place):
    slot = lanes((EMY, 128)) >> 3
    rim = edge()
    planes = []
    for x in range(MX):
        plane = middle[x]() if x < 4 else roll(middle[x - 4](), 64)
        rolled = roll(rim, 64 - 16 * x)
        planes.append(jnp.where(slot < 8, plane, jnp.where(slot < 10, rolled, 0.0)))
    high, low = halves(jnp.concatenate(planes, axis=1))
    by_y = dot(my, jnp.concatenate([high, low, high], axis=0))
    for term in range(TERMS):
        rows = by_y[term * MY : (term + 1) * MY, :]
        left = jnp.concatenate([rows[:, x * 128 : (x + 1) * 128] for x in range(MX)], axis=0)
        high, low = halves(left)
        mzh = mzh_ref[term]
        result = dot(high, mzh) + dot(low, mzh) + dot(high, mzl_ref[term])
        for x in range(MX):
            out_ref[term, place + x] = result[x * MY : (x + 1) * MY]


def own_kernel(
    f_ref, mid_ref, halo_ref, low_ref, high_ref, gy_ref, gzh_ref, gzl_ref, my_ref, mzh_ref, mzl_ref, fine_ref, middle_ref
):
    planes, sides, middle, edge = own_extended(f_ref, mid_ref, halo_ref, low_ref, high_ref)
    filter_yz(planes, sides, gy_ref[...], gzh_ref, gzl_ref, fine_ref, list(range(BX)))
    filter_middle(middle, edge, my_ref[...], mzh_ref, mzl_ref, middle_ref, 0)


def final_kernel(
    low_ref, high_ref, fine_ref, middle_ref, top_ref, gy_ref, gzh_ref, gzl_ref, my_ref, mzh_ref, mzl_ref, cx_ref,
    spread_ref, rows_ref, out_ref, ring_ref, small_ref, add_ref,
):
    planes, sides = [], []
    for ref in (low_ref, high_ref):
        planes += [lambda ref=ref, x=x: ref[x * EY : (x + 1) * EY, :] for x in range(8)]
        sides.append(lambda ref=ref: ref[8 * EY : 9 * EY, :])
    filter_yz(planes, sides, gy_ref[...], gzh_ref, gzl_ref, ring_ref, list(range(16)))
    for index, ref in enumerate((low_ref, high_ref)):
        middle = [lambda ref=ref, x=x: ref[9 * EY + x * EMY : 9 * EY + (x + 1) * EMY, :] for x in range(4)]
        edge = lambda ref=ref: ref[9 * EY + 4 * EMY : 9 * EY + 5 * EMY, :]
        filter_middle(middle, edge, my_ref[...], mzh_ref, mzl_ref, small_ref, index * MX)

    top = top_ref[0]
    for source in range(1, GX):
        top = top + top_ref[source]
    top = exact(exact(rows_ref[...], top), spread_ref[...])

    for tile in range(MY // 8):
        sl = slice(tile * 8, tile * 8 + 8)
        acc = [top[sl, (x // 2) * 128 : (x // 2 + 1) * 128] for x in range(MX)]
        for term in range(TERMS):
            for place in range(3 * MX):
                if place < MX:
                    value = small_ref[term, place, sl, :]
                elif place < 2 * MX:
                    value = middle_ref[term, place - MX, sl, :]
                else:
                    value = small_ref[term, place - MX, sl, :]
                for x in range(MX):
                    offset = place - x - RADIUS
                    if abs(offset) <= RADIUS:
                        acc[x] = acc[x] + cx_ref[(TERMS + term) * TAPS + abs(offset)] * value
        for x in range(MX):
            add_ref[x, pl.ds(tile * 16, 8, stride=2), :] = acc[x]
            add_ref[x, pl.ds(tile * 16 + 1, 8, stride=2), :] = acc[x]

    def tile_step(tile, carry):
        sl = pl.ds(pl.multiple_of(tile * 8, 8), 8)
        acc = [add_ref[x // 2, sl, :] for x in range(BX)]
        for term in range(TERMS):
            for place in range(2 * BX):
                if place < 8:
                    value = ring_ref[term, place, sl, :]
                elif place < 24:
                    value = fine_ref[term, place - 8, sl, :]
                else:
                    value = ring_ref[term, place - 16, sl, :]
                for x in range(BX):
                    offset = place - x - RADIUS
                    if abs(offset) <= RADIUS:
                        acc[x] = acc[x] + cx_ref[term * TAPS + abs(offset)] * value
        for x in range(BX):
            out_ref[x, sl, :] = acc[x]
        return carry

    lax.fori_loop(0, BY // 8, tile_step, 0)


def call(kernel, outs, args, scratch=(), flops=0, smem=0):
    vmem = pl.BlockSpec(memory_space=pltpu.VMEM)
    specs = [pl.BlockSpec(memory_space=pltpu.SMEM)] * smem + [vmem] * (len(args) - smem)
    size = sum(a.size * a.dtype.itemsize for a in args)
    return pl.pallas_call(
        kernel,
        out_shape=[jax.ShapeDtypeStruct(shape, dtype) for shape, dtype in outs],
        in_specs=specs,
        out_specs=[vmem] * len(outs),
        scratch_shapes=list(scratch),
        cost_estimate=pl.CostEstimate(flops=flops, bytes_accessed=size, transcendentals=0),
        compiler_params=pltpu.CompilerParams(vmem_limit_bytes=32 * 1024 * 1024),
    )(*args)


def ring(value, axis, step):
    count = lax.axis_size(axis)
    return lax.ppermute(value, axis, [(i, (i + step) % count) for i in range(count)])


def shards(charges, term_width, term_weight):
    cas_y, cas_z, along_x, own_z, pairs, spread, rows = [jnp.asarray(t) for t in constant_tables()]
    coarse, mid, zmsg = call(
        restrict_kernel,
        [((GY * GZ, 8, 128), F32), ((4, MY, 128), F32), ((GZ, 2 * BY + MY, 128), F32)],
        [charges, pairs],
        [pltpu.VMEM((MX * MY, 128), F32)],
        flops=10**7,
    )
    slab = lax.all_to_all(coarse, ("gy", "gz"), 0, 0, tiled=True)
    zrecv = lax.all_to_all(zmsg, "gz", 0, 0, tiled=True)
    gy, gzh, gzl, my, mzh, mzl, cx = call(
        weights_kernel,
        [
            ((TERMS * BY, 3 * EY), BF16),
            ((TERMS, 256, 128), BF16),
            ((TERMS, 256, 128), BF16),
            ((TERMS * MY, 3 * EMY), BF16),
            ((TERMS, 128, 128), BF16),
            ((TERMS, 128, 128), BF16),
            ((2 * TERMS * TAPS, 8, 128), F32),
        ],
        [term_width, term_weight],
        flops=10**7,
        smem=2,
    )
    (partial,) = call(
        modes_kernel, [((GX, 8, 128), F32)], [slab, cas_y, cas_z, along_x, own_z], flops=5 * 10**7
    )
    top = lax.all_to_all(partial, "gx", 0, 0, tiled=True)
    halo, y_up, y_down = call(
        y_message_kernel,
        [((2 * BY + MY, 128), F32), ((YROWS, 128), F32), ((YROWS, 128), F32)],
        [charges, mid, zrecv],
        flops=10**6,
    )
    low, high = ring(y_up, "gy", 1), ring(y_down, "gy", -1)
    x_up, x_down = call(
        x_message_kernel,
        [((XROWS, 128), F32), ((XROWS, 128), F32)],
        [charges, mid, halo, low, high],
        flops=10**6,
    )
    x_low, x_high = ring(x_up, "gx", 1), ring(x_down, "gx", -1)
    fine, middle = call(
        own_kernel,
        [((TERMS, BX, BY, 128), F32), ((TERMS, MX, MY, 128), F32)],
        [charges, mid, halo, low, high, gy, gzh, gzl, my, mzh, mzl],
        flops=10**8,
    )
    (result,) = call(
        final_kernel,
        [((BX, BY, BZ), F32)],
        [x_low, x_high, fine, middle, top, gy, gzh, gzl, my, mzh, mzl, cx, spread, rows],
        [
            pltpu.VMEM((TERMS, 16, BY, 128), F32),
            pltpu.VMEM((TERMS, 16, MY, 128), F32),
            pltpu.VMEM((MX, BY, 128), F32),
        ],
        flops=10**8,
    )
    return result


def solution(mesh):
    placed = (P("gx", "gy", "gz"), P(), P())
    return jax.shard_map(
        shards, mesh=mesh, in_specs=placed, out_specs=P("gx", "gy", "gz"), check_vma=False
    )
```

time: 257 us -> 68.6 us (0.27)
  the two profiles are of different devices: /device:TPU:6 before, /device:TPU:1 now
where the time goes in v1:
time: 68.6 us; the launch traced here: 68.1 us
  starting transfers between devices  32.8 us (48%)
  Pallas kernels  12.2 us (18%)
  blocking collectives  9.62 us (14%)
  waiting for transfers between devices  8.93 us (13%)
  local copies, waits for them, and re-layouts  4.42 us (6%)
    ppermute x4, starting transfers between devices, ring(): lax.ppermute(value, axis, [(i, (i + step) % count) for i in range(count)])  16.5 us
    pallas_call x7, Pallas kernels, call(): pl.pallas_call(kernel, out_shape=[jax.ShapeDtypeStruct(shape, dtype) for...  12.2 us
    all_to_all x1, starting transfers between devices, shards(): top = lax.all_to_all(partial, 'gx', 0, 0, tiled=True)  11.2 us
    all_to_all x1, blocking collectives, shards(): zrecv = lax.all_to_all(zmsg, 'gz', 0, 0, tiled=True)  9.62 us
    all_to_all x1, starting transfers between devices, shards(): slab = lax.all_to_all(coarse, ('gy', 'gz'), 0, 0, tiled=True)  5.12 us
    all_to_all x1, waiting for transfers between devices, shards(): slab = lax.all_to_all(coarse, ('gy', 'gz'), 0, 0, tiled=True)  4.49 us
    all_to_all x1, waiting for transfers between devices, shards(): top = lax.all_to_all(partial, 'gx', 0, 0, tiled=True)  4.43 us
    unnamed x26, local copies, waits for them, and re-layouts  4.42 us
  transfers between devices with their start and end apart: 6, of which 2 were waited for; matrix products, arithmetic and copies ran while one was open for 0% of the time, Pallas kernels for 10%

profile of v1, /device:TPU:1, one launch (start us, length us, event | category | flops | bytes accessed | tf_op | source)
XLA Modules:
  0.0 68.1 jit_solution(2426835032334404614)
XLA Ops:
  0.0 0.0 copy-start
  0.0 0.9 %copy-done = f32[16,32,128]{2,1,0:T(8,128)S(1)} copy-done((f32[16,32,128]{2,1,0:T(8,128)S(1)}, f32[16,32,128]{2,1,0:T(8,128)}, u32[]{:S(2)}) %copy-start) | copy-done | bytes 262168
  1.0 0.0 copy-start.8
  1.0 0.8 %copy-done.8 = f32[128,128]{1,0:T(8,128)S(1)} copy-done((f32[128,128]{1,0:T(8,128)S(1)}, f32[128,128]{1,0:T(8,128)}, u32[]{:S(2)}) %copy-start.8) | copy-done | bytes 65560
  1.8 0.0 copy-start.1
  1.8 0.0 copy-start.2
  1.8 0.0 copy-start.6
  1.8 0.0 copy-start.7
  1.8 0.0 copy-start.9
  1.8 1.0 %shard_map.100 = (f32[32,8,128]{2,1,0:T(8,128)}, f32[4,16,128]{2,1,0:T(8,128)S(1)}, f32[4,80,128]{2,1,0:T(8,128)S(1)}) custom-call(f32[16,32,128]{2,1,0:T(8,128)S(1)} %copy-done, f32[128,128]{1,0:T(8,128)S(1)} %copy-done.8), custom_call_target="tpu_custom_call" | custom-call | flops 10000000 | bytes 327680 | tf_op jit(solution)/shard_map/pallas_call | solution.py:363
  2.8 9.6 %all_to_all.15.zrecv_ref = f32[4,80,128]{2,1,0:T(8,128)S(1)} all-to-all(f32[4,80,128]{2,1,0:T(8,128)S(1)} %get-tuple-element.23), channel_id=1, replica_groups=mesh['gx'=16,'gy'=8,'gz'=4] {'gz'}, dimensions={0} | all-to-all | bytes 327680 | tf_op jit(solution)/shard_map/all_to_all | solution.py:389
  12.4 4.0 %collective-permute-start = (f32[184,128]{1,0:T(8,128)S(1)}, f32[184,128]{1,0:T(8,128)S(1)}, u32[]{:S(2)}, u32[]{:S(2)}) collective-permute-start(f32[184,128]{1,0:T(8,128)S(1)} %get-tuple-element.25), channel_id=1, source_target_pairs={{0,4},{4,8},{8,12},{12,16},{16,20},{20,24},{24,28},{28,0},{1,5},{5... | collective-permute-start | bytes 282632 | tf_op jit(solution)/shard_map/ppermute | solution.py:376
  16.4 8.6 %collective-permute-start.1 = (f32[184,128]{1,0:T(8,128)S(1)}, f32[184,128]{1,0:T(8,128)S(1)}, u32[]{:S(2)}, u32[]{:S(2)}) collective-permute-start(f32[184,128]{1,0:T(8,128)S(1)} %get-tuple-element.26), channel_id=1, source_target_pairs={{0,28},{4,0},{8,4},{12,8},{16,12},{20,16},{24,20},{28,24},{1,29},{... | collective-permute-start | bytes 282632 | tf_op jit(solution)/shard_map/ppermute | solution.py:376
  25.0 5.1 %all-to-all-start.1 = ((f32[32,8,128]{2,1,0:T(8,128)}), f32[32,8,128]{2,1,0:T(8,128)S(1)}, u32[]{:S(2)}, u32[]{:S(2)}) async-start(f32[32,8,128]{2,1,0:T(8,128)} %get-tuple-element.37), calls=%async_computation.1 | async-start | bytes 262144 | tf_op jit(solution)/shard_map/all_to_all | solution.py:388
  30.2 0.0 collective-permute-done.low_ref
  30.2 0.0 collective-permute-done.1.high_ref
  30.2 0.0 copy-done.1
  30.2 0.0 copy-start.11
  30.2 0.0 copy-start.12
  30.2 0.9 %shard_map.102 = (f32[592,128]{1,0:T(8,128)}, f32[592,128]{1,0:T(8,128)}) custom-call(f32[16,32,128]{2,1,0:T(8,128)S(1)} %copy-done.1, f32[4,16,128]{2,1,0:T(8,128)S(1)} %get-tuple-element.22.mid_ref, f32[80,128]{1,0:T(8,128)S(1)} %get-tuple-element.24.halo_ref, f32[184,128]{1,0:T(8,128)S(1)} %collective-permute-done.low_ref, ...), custom_call_target="tpu_custom_call" | custom-call | flops 1000000 | bytes 524288 | tf_op jit(solution)/shard_map/pallas_call | solution.py:363
  31.1 3.9 %collective-permute-start.2 = (f32[592,128]{1,0:T(8,128)}, f32[592,128]{1,0:T(8,128)S(1)}, u32[]{:S(2)}, u32[]{:S(2)}) collective-permute-start(f32[592,128]{1,0:T(8,128)} %get-tuple-element.27), channel_id=1, source_target_pairs={{0,32},{32,64},{64,96},{96,128},{128,160},{160,192},{192,224},{224... | collective-permute-start | bytes 909320 | tf_op jit(solution)/shard_map/ppermute | solution.py:376
  35.0 0.0 collective-permute-start.3
  35.0 4.5 %all-to-all-done.1.slab_ref = f32[32,8,128]{2,1,0:T(8,128)S(1)} async-done(((f32[32,8,128]{2,1,0:T(8,128)}), f32[32,8,128]{2,1,0:T(8,128)S(1)}, u32[]{:S(2)}, u32[]{:S(2)}) %all-to-all-start.1) | async-done | bytes 131104 | tf_op jit(solution)/shard_map/all_to_all | solution.py:388
  39.5 0.0 copy-done.2
  39.5 0.0 copy-done.6
  39.5 0.0 copy-done.7
  39.5 0.0 copy-done.9
  39.5 3.4 %shard_map.105 = f32[16,8,128]{2,1,0:T(8,128)} custom-call(f32[32,8,128]{2,1,0:T(8,128)S(1)} %all-to-all-done.1.slab_ref, f32[64,64]{1,0:T(8,128)S(1)} %copy-done.9, f32[128,128]{1,0:T(8,128)S(1)} %copy-done.7, f32[33,64,128]{2,1,0:T(8,128)S(1)} %copy-done.2, f32[4,128,128]{2,1,0:T(8,128)S(1)} %copy-done.6), custom_call_target="tpu_custom_call" | custom-call | flops 50000000 | bytes 1556480 | tf_op jit(solution)/shard_map/pallas_call | solution.py:363
  43.0 0.0 copy-start.10
  43.0 11.2 %all-to-all-start.2 = ((f32[16,8,128]{2,1,0:T(8,128)}), f32[16,8,128]{2,1,0:T(8,128)S(1)}, u32[]{:S(2)}, u32[]{:S(2)}) async-start(f32[16,8,128]{2,1,0:T(8,128)} %shard_map.105), calls=%async_computation.2 | async-start | bytes 131072 | tf_op jit(solution)/shard_map/all_to_all | solution.py:408
  54.1 0.0 copy-done.11
  54.2 0.0 copy-done.12
  54.2 0.9 %shard_map.103 = (bf16[128,144]{1,0:T(8,128)(2,1)S(1)}, bf16[4,256,128]{2,1,0:T(8,128)(2,1)S(1)}, bf16[4,256,128]{2,1,0:T(8,128)(2,1)S(1)}, bf16[64,96]{1,0:T(8,...) custom-call(f32[2,4]{1,0:T(2,128)S(1)} %copy-done.11, ...), custom_call_target="tpu_custom_call" | custom-call | flops 10000000 | bytes 64 | tf_op jit(solution)/shard_map/pallas_call | solution.py:363
  55.1 1.7 %shard_map.104 = (f32[4,16,32,128]{3,2,1,0:T(8,128)S(1)}, f32[4,8,16,128]{3,2,1,0:T(8,128)S(1)}) custom-call(f32[16,32,128]{2,1,0:T(8,128)S(1)} %copy-done.1, f32[4,16,128]{2,1,0:T(8,128)S(1)} %get-tuple-element.22.mid_ref, f32[80,128]{1,0:T(8,128)S(1)} %get-tuple-element.24.halo_ref, f32[184,128]{1,0:T(8,128)S(1)} %collective-permute-done.low_ref, ...), custom_call_target="tpu_custom_call" | custom-call | flops 100000000 | bytes 1359872 | tf_op jit(solution)/shard_map/pallas_call | solution.py:363
  56.8 0.0 copy-start.4
  56.8 0.7 %copy-done.4 = f32[4,8,16,128]{3,2,1,0:T(8,128)} copy-done((f32[4,8,16,128]{3,2,1,0:T(8,128)}, f32[4,8,16,128]{3,2,1,0:T(8,128)S(1)}, u32[]{:S(2)}) %copy-start.4) | copy-done | bytes 262168
  57.5 4.4 %all-to-all-done.2.top_ref = f32[16,8,128]{2,1,0:T(8,128)S(1)} async-done(((f32[16,8,128]{2,1,0:T(8,128)}), f32[16,8,128]{2,1,0:T(8,128)S(1)}, u32[]{:S(2)}, u32[]{:S(2)}) %all-to-all-start.2) | async-done | bytes 65568 | tf_op jit(solution)/shard_map/all_to_all | solution.py:408
  61.9 0.0 collective-permute-done.2.low_ref
  61.9 0.0 collective-permute-done.3.high_ref
  61.9 0.0 copy-done.10
  61.9 0.0 copy-start.3
  61.9 0.9 %copy-done.3 = f32[128,512]{1,0:T(8,128)S(1)} copy-done((f32[128,512]{1,0:T(8,128)S(1)}, f32[128,512]{1,0:T(8,128)}, u32[]{:S(2)}) %copy-start.3) | copy-done | bytes 262168
  62.9 0.0 copy-start.5
  62.9 0.9 %copy-done.5 = f32[4,8,16,128]{3,2,1,0:T(8,128)S(1)} copy-done((f32[4,8,16,128]{3,2,1,0:T(8,128)S(1)}, f32[4,8,16,128]{3,2,1,0:T(8,128)}, u32[]{:S(2)}) %copy-start.5) | copy-done | bytes 262168
  63.8 4.3 %shard_map.106 = f32[16,32,128]{2,1,0:T(8,128)} custom-call(f32[592,128]{1,0:T(8,128)S(1)} %collective-permute-done.2.low_ref, f32[592,128]{1,0:T(8,128)S(1)} %collective-permute-done.3.high_ref, f32[4,16,32,128]{3,2,1,0:T(8,128)S(1)} %get-tuple-element.35.fine_ref, f32[4,8,16,128]{3,2,1,0:T(8,128)S(1)} %copy-done.5, ...), custom_call_target="tpu_custom_call" | custom-call | flops 100000000 | bytes 3375616 | tf_op jit(solution)/shard_map/pallas_call | solution.py:363
  (1 shorter events, 0.0 us)
Async XLA Ops:
  0.0 0.9 %copy-start = (f32[16,32,128]{2,1,0:T(8,128)S(1)}, f32[16,32,128]{2,1,0:T(8,128)}, u32[]{:S(2)}) copy-start(f32[16,32,128]{2,1,0:T(8,128)} %f_ref.7) | copy-start | bytes 786436
  1.0 0.8 %copy-start.8 = (f32[128,128]{1,0:T(8,128)S(1)}, f32[128,128]{1,0:T(8,128)}, u32[]{:S(2)}) copy-start(f32[128,128]{1,0:T(8,128)} %constant.18.clone.pairs_ref) | copy-start | bytes 196612
  1.8 28.4 %copy-start.1 = (f32[16,32,128]{2,1,0:T(8,128)S(1)}, f32[16,32,128]{2,1,0:T(8,128)}, u32[]{:S(2)}) copy-start(f32[16,32,128]{2,1,0:T(8,128)} %f_ref.7) | copy-start | bytes 786436
  1.8 37.7 %copy-start.2 = (f32[33,64,128]{2,1,0:T(8,128)S(1)}, f32[33,64,128]{2,1,0:T(8,128)}, u32[]{:S(2)}) copy-start(f32[33,64,128]{2,1,0:T(8,128)} %constant.16.clone.along_ref) | copy-start | bytes 3244036
  1.8 37.7 %copy-start.6 = (f32[4,128,128]{2,1,0:T(8,128)S(1)}, f32[4,128,128]{2,1,0:T(8,128)}, u32[]{:S(2)}) copy-start(f32[4,128,128]{2,1,0:T(8,128)} %constant.17.clone.own_z_ref) | copy-start | bytes 786436
  1.8 37.7 %copy-start.7 = (f32[128,128]{1,0:T(8,128)S(1)}, f32[128,128]{1,0:T(8,128)}, u32[]{:S(2)}) copy-start(f32[128,128]{1,0:T(8,128)} %constant.15.clone.cas_z_ref) | copy-start | bytes 196612
  1.8 37.7 %copy-start.9 = (f32[64,64]{1,0:T(8,128)S(1)}, f32[64,64]{1,0:T(8,128)}, u32[]{:S(2)}) copy-start(f32[64,64]{1,0:T(8,128)} %constant.14.clone.cas_y_ref) | copy-start | bytes 49156
  12.4 17.7 %collective-permute-start = (f32[184,128]{1,0:T(8,128)S(1)}, f32[184,128]{1,0:T(8,128)S(1)}, u32[]{:S(2)}, u32[]{:S(2)}) collective-permute-start(f32[184,128]{1,0:T(8,128)S(1)} %get-tuple-element.25), channel_id=1, source_target_pairs={{0,4},{4,8},{8,12},{12,16},{16,20},{20,24},{24,28},{28,0},{1,5},{5... | collective-permute-start | bytes 282632 | tf_op jit(solution)/shard_map/ppermute | solution.py:376
  16.4 13.7 %collective-permute-start.1 = (f32[184,128]{1,0:T(8,128)S(1)}, f32[184,128]{1,0:T(8,128)S(1)}, u32[]{:S(2)}, u32[]{:S(2)}) collective-permute-start(f32[184,128]{1,0:T(8,128)S(1)} %get-tuple-element.26), channel_id=1, source_target_pairs={{0,28},{4,0},{8,4},{12,8},{16,12},{20,16},{24,20},{28,24},{1,29},{... | collective-permute-start | bytes 282632 | tf_op jit(solution)/shard_map/ppermute | solution.py:376
  25.0 14.5 %all-to-all-start.1 = ((f32[32,8,128]{2,1,0:T(8,128)}), f32[32,8,128]{2,1,0:T(8,128)S(1)}, u32[]{:S(2)}, u32[]{:S(2)}) async-start(f32[32,8,128]{2,1,0:T(8,128)} %get-tuple-element.37), calls=%async_computation.1 | async-start | bytes 262144 | tf_op jit(solution)/shard_map/all_to_all | solution.py:388
  30.2 24.0 %copy-start.11 = (f32[2,4]{1,0:T(2,128)S(1)}, f32[2,4]{1,0:T(2,128)}, u32[]{:S(2)}) copy-start(f32[2,4]{1,0:T(2,128)} %width_ref.1) | copy-start | bytes 100
  30.2 23.9 %copy-start.12 = (f32[2,4]{1,0:T(2,128)S(1)}, f32[2,4]{1,0:T(2,128)}, u32[]{:S(2)}) copy-start(f32[2,4]{1,0:T(2,128)} %weight_ref.1) | copy-start | bytes 100
  31.1 30.8 %collective-permute-start.2 = (f32[592,128]{1,0:T(8,128)}, f32[592,128]{1,0:T(8,128)S(1)}, u32[]{:S(2)}, u32[]{:S(2)}) collective-permute-start(f32[592,128]{1,0:T(8,128)} %get-tuple-element.27), channel_id=1, source_target_pairs={{0,32},{32,64},{64,96},{96,128},{128,160},{160,192},{192,224},{224... | collective-permute-start | bytes 909320 | tf_op jit(solution)/shard_map/ppermute | solution.py:376
  35.0 26.9 %collective-permute-start.3 = (f32[592,128]{1,0:T(8,128)}, f32[592,128]{1,0:T(8,128)S(1)}, u32[]{:S(2)}, u32[]{:S(2)}) collective-permute-start(f32[592,128]{1,0:T(8,128)} %get-tuple-element.28), channel_id=1, source_target_pairs={{0,480},{32,0},{64,32},{96,64},{128,96},{160,128},{192,160},{224,1... | collective-permute-start | bytes 909320 | tf_op jit(solution)/shard_map/ppermute | solution.py:376
  43.0 19.0 %copy-start.10 = (f32[16,8]{1,0:T(8,128)S(1)}, f32[16,8]{1,0:T(8,128)}, u32[]{:S(2)}) copy-start(f32[16,8]{1,0:T(8,128)} %constant.20.clone.rows_ref) | copy-start | bytes 1540
  43.0 18.9 %all-to-all-start.2 = ((f32[16,8,128]{2,1,0:T(8,128)}), f32[16,8,128]{2,1,0:T(8,128)S(1)}, u32[]{:S(2)}, u32[]{:S(2)}) async-start(f32[16,8,128]{2,1,0:T(8,128)} %shard_map.105), calls=%async_computation.2 | async-start | bytes 131072 | tf_op jit(solution)/shard_map/all_to_all | solution.py:408
  56.8 0.7 %copy-start.4 = (f32[4,8,16,128]{3,2,1,0:T(8,128)}, f32[4,8,16,128]{3,2,1,0:T(8,128)S(1)}, u32[]{:S(2)}) copy-start(f32[4,8,16,128]{3,2,1,0:T(8,128)S(1)} %get-tuple-element.36.middle_ref) | copy-start | bytes 786436
  61.9 1.0 %copy-start.3 = (f32[128,512]{1,0:T(8,128)S(1)}, f32[128,512]{1,0:T(8,128)}, u32[]{:S(2)}) copy-start(f32[128,512]{1,0:T(8,128)} %constant.19.clone.spread_ref) | copy-start | bytes 786436
  62.9 0.9 %copy-start.5 = (f32[4,8,16,128]{3,2,1,0:T(8,128)S(1)}, f32[4,8,16,128]{3,2,1,0:T(8,128)}, u32[]{:S(2)}) copy-start(f32[4,8,16,128]{3,2,1,0:T(8,128)} %copy-done.4) | copy-start | bytes 786436

commit v2 on v1

--- a/solution.py
+++ b/solution.py
@@ -8,6 +8,7 @@
 from jax.experimental.pallas import tpu as pltpu
 from jax.sharding import PartitionSpec as P
 
+
 TERMS = 4
 RADIUS = 8
 TAPS = RADIUS + 1
@@ -23,6 +24,8 @@
 CX, CY, CZ = 64, 64, 128
 EY, EMY = BY + 2 * RADIUS, MY + 2 * RADIUS
 GX, GY, GZ = 16, 8, 4
+FETCHED = 7
+ZROWS = 2 * BY + MY
 YROWS = BX * 8 + 2 * 8 + 5 * 8
 XROWS = 8 * EY + EY + 5 * EMY
 
@@ -46,16 +49,7 @@
     cosine = np.cos(2.0 * math.pi / CX * (np.outer(shifts, np.arange(CX)) % CX))
     along_x = np.einsum("dm,myz->dyz", cosine, mult) / (CX * CY * CZ)
     own_z = np.stack([np.tile(cas_z[:, 32 * g : 32 * g + 32], (1, 4)) for g in range(GZ)])
-    fine = np.arange(BZ)
-    pairs = np.zeros((BZ, BZ))
-    pairs[fine, fine // 2] = 1.0 / 8.0
-    pairs[fine, 64 + fine // 4] = 1.0 / 64.0
-    spread = np.zeros((BZ, 4 * BZ))
-    for block in range(4):
-        spread[block * 32 + fine // 4, block * BZ + fine] = 1.0
-    rows = np.zeros((MY, 8))
-    rows[np.arange(MY), np.arange(MY) // 2] = 1.0
-    return [np.asarray(t, np.float32) for t in (cas_y, cas_z, along_x, own_z, pairs, spread, rows)]
+    return [np.asarray(t, np.float32) for t in (cas_y, cas_z, along_x, own_z)]
 
 
 def lanes(shape):
@@ -82,7 +76,7 @@
 
 def weights_kernel(width_ref, weight_ref, gy_ref, gzh_ref, gzl_ref, my_ref, mzh_ref, mzl_ref, cx_ref):
     def scale(level, term):
-        width = jnp.full((8, 128), width_ref[level, term], F32)
+        width = jnp.broadcast_to(width_ref[level : level + 1, term : term + 1], (8, 128))
         inverse = 1.0 / (2.0 * width * width)
         offset = lanes((8, 128)) - RADIUS
         values = jnp.exp(-(offset * offset).astype(F32) * inverse)
@@ -113,7 +107,7 @@
         gzh_ref[term] = high
         gzl_ref[term] = low
         for offset in range(TAPS):
-            value = jnp.exp(-float(offset * offset) * inverse) * norm * weight_ref[0, term]
+            value = jnp.exp(-float(offset * offset) * inverse) * norm * weight_ref[0:1, term : term + 1]
             cx_ref[term * TAPS + offset] = jnp.broadcast_to(value, (8, 128))
 
         inverse, norm = scale(1, term)
@@ -126,11 +120,18 @@
         mzh_ref[term] = high
         mzl_ref[term] = low
         for offset in range(TAPS):
-            value = jnp.exp(-float(offset * offset) * inverse) * norm * weight_ref[1, term]
+            value = jnp.exp(-float(offset * offset) * inverse) * norm * weight_ref[1:2, term : term + 1]
             cx_ref[(TERMS + term) * TAPS + offset] = jnp.broadcast_to(value, (8, 128))
 
 
-def restrict_kernel(f_ref, pairs_ref, coarse_ref, mid_ref, zmsg_ref, half_ref):
+def restrict_kernel(*refs):
+    sources, (coarse_ref, mid_ref, up_ref, down_ref), copies = refs[:FETCHED], refs[FETCHED : FETCHED + 4], refs[FETCHED + 4 :]
+    copies, half_ref, sems = copies[:FETCHED], copies[FETCHED], copies[FETCHED + 1]
+    fetches = [pltpu.make_async_copy(a, b, sems.at[i]) for i, (a, b) in enumerate(zip(sources, copies))]
+    for fetch in fetches:
+        fetch.start()
+    f_ref = copies[0]
+    fetches[0].wait()
     planes = []
     for x in range(MX):
         total = None
@@ -139,7 +140,9 @@
                 part = f_ref[plane, pl.ds(odd, MY, stride=2), :]
                 total = part if total is None else total + part
         planes.append(total)
-    half_ref[...] = exact(jnp.concatenate(planes, axis=0), pairs_ref[...])
+    row, column = lax.broadcasted_iota(jnp.int32, (BZ, 128), 0), lanes((BZ, 128))
+    pairs = jnp.where((row >> 1) == column, 1.0 / 8.0, jnp.where((row >> 2) == column - 64, 1.0 / 64.0, 0.0))
+    half_ref[...] = exact(jnp.concatenate(planes, axis=0), pairs)
     lane = lanes((8, 128))
     coarse = jnp.zeros((8, 128), F32)
     for x in range(4):
@@ -151,9 +154,6 @@
     for target in range(GY * GZ):
         coarse_ref[target] = coarse
 
-    me = lax.axis_index("gz")
-    up, down = lax.rem(me + 1, GZ), lax.rem(me + GZ - 1, GZ)
-    zmsg_ref[...] = jnp.zeros_like(zmsg_ref)
     slot = lanes((BY, 128)) >> 3
     for group in range(2):
         rising = jnp.zeros((BY, 128), F32)
@@ -162,8 +162,8 @@
             plane = f_ref[group * 8 + x]
             rising = jnp.where(slot == 2 * x, roll(plane, x * 16 - 120), rising)
             falling = jnp.where(slot == 2 * x + 1, roll(plane, x * 16 + 8), falling)
-        zmsg_ref[up, group * BY : (group + 1) * BY, :] = rising
-        zmsg_ref[down, group * BY : (group + 1) * BY, :] = falling
+        up_ref[group * BY : (group + 1) * BY, :] = rising
+        down_ref[group * BY : (group + 1) * BY, :] = falling
     slot = lanes((MY, 128)) >> 3
     rising = jnp.zeros((MY, 128), F32)
     falling = jnp.zeros((MY, 128), F32)
@@ -173,10 +173,12 @@
         middle.append(plane)
         rising = jnp.where(slot == 2 * x, roll(plane, x * 16 - 56), rising)
         falling = jnp.where(slot == 2 * x + 1, roll(plane, x * 16 + 8), falling)
-    zmsg_ref[up, 2 * BY : 2 * BY + MY, :] = rising
-    zmsg_ref[down, 2 * BY : 2 * BY + MY, :] = falling
+    up_ref[2 * BY : 2 * BY + MY, :] = rising
+    down_ref[2 * BY : 2 * BY + MY, :] = falling
     for x in range(4):
         mid_ref[x] = jnp.where(slot < 8, middle[x], roll(middle[x + 4], 64))
+    for fetch in fetches[1:]:
+        fetch.wait()
 
 
 def modes_kernel(slab_ref, cas_y_ref, cas_z_ref, along_ref, own_z_ref, out_ref):
@@ -214,9 +216,8 @@
         out_ref[lax.rem(me + block, GX)] = result
 
 
-def y_message_kernel(f_ref, mid_ref, zrecv_ref, halo_ref, up_ref, down_ref):
-    me = lax.axis_index("gz")
-    halo = zrecv_ref[lax.rem(me + GZ - 1, GZ)] + zrecv_ref[lax.rem(me + 1, GZ)]
+def y_message_kernel(f_ref, mid_ref, zlow_ref, zhigh_ref, halo_ref, up_ref, down_ref):
+    halo = zlow_ref[...] + zhigh_ref[...]
     halo_ref[...] = halo
     for ref, fine, middle in ((up_ref, BY - 8, MY - 8), (down_ref, 0, 0)):
         for x in range(BX):
@@ -296,9 +297,9 @@
     filter_middle(middle, edge, my_ref[...], mzh_ref, mzl_ref, middle_ref, 0)
 
 
-def final_kernel(
-    low_ref, high_ref, fine_ref, middle_ref, top_ref, gy_ref, gzh_ref, gzl_ref, my_ref, mzh_ref, mzl_ref, cx_ref,
-    spread_ref, rows_ref, out_ref, ring_ref, small_ref, add_ref,
+def near_kernel(
+    low_ref, high_ref, fine_ref, middle_ref, gy_ref, gzh_ref, gzl_ref, my_ref, mzh_ref, mzl_ref, cx_ref,
+    out_ref, ring_ref, small_ref, add_ref,
 ):
     planes, sides = [], []
     for ref in (low_ref, high_ref):
@@ -310,14 +311,9 @@
         edge = lambda ref=ref: ref[9 * EY + 4 * EMY : 9 * EY + 5 * EMY, :]
         filter_middle(middle, edge, my_ref[...], mzh_ref, mzl_ref, small_ref, index * MX)
 
-    top = top_ref[0]
-    for source in range(1, GX):
-        top = top + top_ref[source]
-    top = exact(exact(rows_ref[...], top), spread_ref[...])
-
     for tile in range(MY // 8):
         sl = slice(tile * 8, tile * 8 + 8)
-        acc = [top[sl, (x // 2) * 128 : (x // 2 + 1) * 128] for x in range(MX)]
+        acc = [None] * MX
         for term in range(TERMS):
             for place in range(3 * MX):
                 if place < MX:
@@ -329,7 +325,8 @@
                 for x in range(MX):
                     offset = place - x - RADIUS
                     if abs(offset) <= RADIUS:
-                        acc[x] = acc[x] + cx_ref[(TERMS + term) * TAPS + abs(offset)] * value
+                        part = cx_ref[(TERMS + term) * TAPS + abs(offset)] * value
+                        acc[x] = part if acc[x] is None else acc[x] + part
         for x in range(MX):
             add_ref[x, pl.ds(tile * 16, 8, stride=2), :] = acc[x]
             add_ref[x, pl.ds(tile * 16 + 1, 8, stride=2), :] = acc[x]
@@ -356,9 +353,32 @@
     lax.fori_loop(0, BY // 8, tile_step, 0)
 
 
-def call(kernel, outs, args, scratch=(), flops=0, smem=0):
+def add_kernel(near_ref, top_ref, out_ref, wide_ref):
+    top = top_ref[0]
+    for source in range(1, GX):
+        top = top + top_ref[source]
+    shape = (BZ, 4 * BZ)
+    row, column = lax.broadcasted_iota(jnp.int32, shape, 0), lanes(shape)
+    spread = jnp.where(row == (column >> 7) * 32 + ((column & 127) >> 2), 1.0, 0.0).astype(BF16)
+    high, rest = halves(top)
+    rest = top - high.astype(F32)
+    mid, low = halves(rest)
+    parts = dot(jnp.concatenate([high.astype(F32), mid.astype(F32), low.astype(F32)], axis=0).astype(BF16), spread)
+    wide = parts[0:8] + parts[8:16] + parts[16:24]
+    for row in range(4):
+        wide_ref[pl.ds(row, 8, stride=4), :] = wide[:, :128]
+        wide_ref[pl.ds(BY + row, 8, stride=4), :] = wide[:, 128:256]
+        wide_ref[pl.ds(2 * BY + row, 8, stride=4), :] = wide[:, 256:384]
+        wide_ref[pl.ds(3 * BY + row, 8, stride=4), :] = wide[:, 384:512]
+    for x in range(BX):
+        out_ref[x] = near_ref[x] + wide_ref[(x // 4) * BY : (x // 4 + 1) * BY, :]
+
+
+def call(kernel, outs, args, scratch=(), flops=0, hbm=False, limit=4):
     vmem = pl.BlockSpec(memory_space=pltpu.VMEM)
-    specs = [pl.BlockSpec(memory_space=pltpu.SMEM)] * smem + [vmem] * (len(args) - smem)
+    specs = [pl.BlockSpec(memory_space=pltpu.HBM) if hbm else vmem] * len(args)
+    if hbm:
+        args = [pltpu.with_memory_space_constraint(a, pltpu.HBM) for a in args]
     size = sum(a.size * a.dtype.itemsize for a in args)
     return pl.pallas_call(
         kernel,
@@ -367,7 +387,7 @@
         out_specs=[vmem] * len(outs),
         scratch_shapes=list(scratch),
         cost_estimate=pl.CostEstimate(flops=flops, bytes_accessed=size, transcendentals=0),
-        compiler_params=pltpu.CompilerParams(vmem_limit_bytes=32 * 1024 * 1024),
+        compiler_params=pltpu.CompilerParams(vmem_limit_bytes=limit * 1024 * 1024),
     )(*args)
 
 
@@ -376,17 +396,24 @@
     return lax.ppermute(value, axis, [(i, (i + step) % count) for i in range(count)])
 
 
-def shards(charges, term_width, term_weight):
-    cas_y, cas_z, along_x, own_z, pairs, spread, rows = [jnp.asarray(t) for t in constant_tables()]
-    coarse, mid, zmsg = call(
+def exchange(value, axis):
+    return lax.all_to_all(value, axis, 0, 0, tiled=True)
+
+
+def potential(charges, term_width, term_weight):
+    sources = [charges, term_width, term_weight] + [jnp.asarray(t) for t in constant_tables()]
+    coarse, mid, z_up, z_down, charges, term_width, term_weight, cas_y, cas_z, along_x, own_z = call(
         restrict_kernel,
-        [((GY * GZ, 8, 128), F32), ((4, MY, 128), F32), ((GZ, 2 * BY + MY, 128), F32)],
-        [charges, pairs],
-        [pltpu.VMEM((MX * MY, 128), F32)],
+        [((GY * GZ, 8, 128), F32), ((4, MY, 128), F32), ((ZROWS, 128), F32), ((ZROWS, 128), F32)]
+        + [(a.shape, a.dtype) for a in sources],
+        sources,
+        [pltpu.VMEM((MX * MY, 128), F32), pltpu.SemaphoreType.DMA((FETCHED,))],
         flops=10**7,
-    )
-    slab = lax.all_to_all(coarse, ("gy", "gz"), 0, 0, tiled=True)
-    zrecv = lax.all_to_all(zmsg, "gz", 0, 0, tiled=True)
+        hbm=True,
+        limit=4,
+    )
+    slab = exchange(coarse, ("gy", "gz"))
+    z_low, z_high = ring(z_up, "gz", 1), ring(z_down, "gz", -1)
     gy, gzh, gzl, my, mzh, mzl, cx = call(
         weights_kernel,
         [
@@ -400,48 +427,46 @@
         ],
         [term_width, term_weight],
         flops=10**7,
-        smem=2,
-    )
-    (partial,) = call(
-        modes_kernel, [((GX, 8, 128), F32)], [slab, cas_y, cas_z, along_x, own_z], flops=5 * 10**7
-    )
-    top = lax.all_to_all(partial, "gx", 0, 0, tiled=True)
+    )
+    bands = [gy, gzh, gzl, my, mzh, mzl]
     halo, y_up, y_down = call(
         y_message_kernel,
-        [((2 * BY + MY, 128), F32), ((YROWS, 128), F32), ((YROWS, 128), F32)],
-        [charges, mid, zrecv],
+        [((ZROWS, 128), F32), ((YROWS, 128), F32), ((YROWS, 128), F32)],
+        [charges, mid, z_low, z_high],
         flops=10**6,
     )
     low, high = ring(y_up, "gy", 1), ring(y_down, "gy", -1)
+    (partial,) = call(
+        modes_kernel, [((GX, 8, 128), F32)], [slab, cas_y, cas_z, along_x, own_z], flops=5 * 10**7, limit=8
+    )
+    top = exchange(partial, "gx")
     x_up, x_down = call(
-        x_message_kernel,
-        [((XROWS, 128), F32), ((XROWS, 128), F32)],
-        [charges, mid, halo, low, high],
-        flops=10**6,
+        x_message_kernel, [((XROWS, 128), F32), ((XROWS, 128), F32)], [charges, mid, halo, low, high], flops=10**6
     )
     x_low, x_high = ring(x_up, "gx", 1), ring(x_down, "gx", -1)
     fine, middle = call(
         own_kernel,
         [((TERMS, BX, BY, 128), F32), ((TERMS, MX, MY, 128), F32)],
-        [charges, mid, halo, low, high, gy, gzh, gzl, my, mzh, mzl],
+        [charges, mid, halo, low, high] + bands,
         flops=10**8,
-    )
-    (result,) = call(
-        final_kernel,
+        limit=8,
+    )
+    (near,) = call(
+        near_kernel,
         [((BX, BY, BZ), F32)],
-        [x_low, x_high, fine, middle, top, gy, gzh, gzl, my, mzh, mzl, cx, spread, rows],
+        [x_low, x_high, fine, middle] + bands + [cx],
         [
             pltpu.VMEM((TERMS, 16, BY, 128), F32),
             pltpu.VMEM((TERMS, 16, MY, 128), F32),
             pltpu.VMEM((MX, BY, 128), F32),
         ],
         flops=10**8,
-    )
+        limit=10,
+    )
+    (result,) = call(add_kernel, [((BX, BY, BZ), F32)], [near, top], [pltpu.VMEM((4 * BY, 128), F32)], flops=10**6)
     return result
 
 
 def solution(mesh):
     placed = (P("gx", "gy", "gz"), P(), P())
-    return jax.shard_map(
-        shards, mesh=mesh, in_specs=placed, out_specs=P("gx", "gy", "gz"), check_vma=False
-    )
+    return jax.shard_map(potential, mesh=mesh, in_specs=placed, out_specs=P("gx", "gy", "gz"), check_vma=False)

time: 68.6 us -> 63.2 us (0.921)
  blocking collectives: 9.62 us -> 0 us
  starting transfers between devices: 32.8 us -> 41.7 us
  local copies, waits for them, and re-layouts: 4.42 us -> 0 us
  waiting for transfers between devices: 8.93 us -> 7.92 us
  Pallas kernels: 12.2 us -> 13.1 us
    all_to_all x1 -> x0, blocking collectives: 9.62 us -> none  [shards(): zrecv = lax.all_to_all(zmsg, 'gz', 0, 0, tiled=True)]
    ppermute x4 -> x6, starting transfers between devices: 16.5 us -> 23.9 us  [ring(): lax.ppermute(value, axis, [(i, (i + step) % count) for i in range(count)])]
    unnamed x26 -> x0, local copies, waits for them, and re-layouts: 4.42 us -> none
    all_to_all x2, waiting for transfers between devices: 8.92 us -> 6.37 us  [exchange(): return lax.all_to_all(value, axis, 0, 0, tiled=True)]
    ppermute x4 -> x6, waiting for transfers between devices: 0.01 us -> 1.55 us  [ring(): lax.ppermute(value, axis, [(i, (i + step) % count) for i in range(count)])]
    all_to_all x2, starting transfers between devices: 16.3 us -> 17.8 us  [exchange(): return lax.all_to_all(value, axis, 0, 0, tiled=True)]
    pallas_call x7 -> x8, Pallas kernels: 12.2 us -> 13.1 us  [call(): pl.pallas_call(kernel, out_shape=[jax.ShapeDtypeStruct(shape, dtype) for...]
  transfers between devices with their start and end apart: 6 -> 8, of which waited for: 2 -> 3; matrix products, arithmetic and copies ran while one was open for 0% -> 0% of each run, Pallas kernels for 10% -> 16%
where the time goes in v2:
time: 63.2 us; the launch traced here: 62.8 us
  starting transfers between devices  41.7 us (66%)
  Pallas kernels  13.1 us (21%)
  waiting for transfers between devices  7.92 us (13%)
    ppermute x6, starting transfers between devices, ring(): lax.ppermute(value, axis, [(i, (i + step) % count) for i in range(count)])  23.9 us
    all_to_all x2, starting transfers between devices, exchange(): return lax.all_to_all(value, axis, 0, 0, tiled=True)  17.8 us
    pallas_call x8, Pallas kernels, call(): pl.pallas_call(kernel, out_shape=[jax.ShapeDtypeStruct(shape, dtype) for...  13.1 us
    all_to_all x2, waiting for transfers between devices, exchange(): return lax.all_to_all(value, axis, 0, 0, tiled=True)  6.37 us
    ppermute x6, waiting for transfers between devices, ring(): lax.ppermute(value, axis, [(i, (i + step) % count) for i in range(count)])  1.55 us
  transfers between devices with their start and end apart: 8, of which 3 were waited for; matrix products, arithmetic and copies ran while one was open for 0% of the time, Pallas kernels for 16%

profile of v2, /device:TPU:1, one launch (start us, length us, event | category | flops | bytes accessed | tf_op | source)
XLA Modules:
  0.0 62.8 jit_solution(11271187512922476413)
XLA Ops:
  0.0 2.2 %shard_map.73 = (f32[32,8,128]{2,1,0:T(8,128)}, f32[4,16,128]{2,1,0:T(8,128)S(1)}, f32[80,128]{1,0:T(8,128)S(1)}, f32[80,128]{1,0:T(8,128)S(1)}, f32[16,32,128]{...) custom-call(f32[16,32,128]{2,1,0:T(8,128)} %refs_0_.1, ...), custom_call_target="tpu_custom_call" | custom-call | flops 10000000 | bytes 1687616 | tf_op jit(solution)/shard_map/pallas_call | solution.py:383
  2.2 3.9 %collective-permute-start = (f32[80,128]{1,0:T(8,128)S(1)}, f32[80,128]{1,0:T(8,128)S(1)}, u32[]{:S(2)}, u32[]{:S(2)}) collective-permute-start(f32[80,128]{1,0:T(8,128)S(1)} %get-tuple-element.32), channel_id=1, source_target_pairs={{0,1},{1,2},{2,3},{3,0},{4,5},{5,6},{6,7},{7,4},{8,9},{9,10},{10,1... | collective-permute-start | bytes 122888 | tf_op jit(solution)/shard_map/ppermute | solution.py:396
  6.1 3.2 %collective-permute-start.1 = (f32[80,128]{1,0:T(8,128)S(1)}, f32[80,128]{1,0:T(8,128)S(1)}, u32[]{:S(2)}, u32[]{:S(2)}) collective-permute-start(f32[80,128]{1,0:T(8,128)S(1)} %get-tuple-element.33), channel_id=1, source_target_pairs={{0,3},{1,0},{2,1},{3,2},{4,7},{5,4},{6,5},{7,6},{8,11},{9,8},{10,9... | collective-permute-start | bytes 122888 | tf_op jit(solution)/shard_map/ppermute | solution.py:396
  9.3 0.0 collective-permute-done.zlow_ref
  9.3 1.5 %collective-permute-done.1.zhigh_ref = f32[80,128]{1,0:T(8,128)S(1)} collective-permute-done((f32[80,128]{1,0:T(8,128)S(1)}, f32[80,128]{1,0:T(8,128)S(1)}, u32[]{:S(2)}, u32[]{:S(2)}) %collective-permute-start.1) | collective-permute-done | bytes 40992 | tf_op jit(solution)/shard_map/ppermute | solution.py:396
  10.9 4.0 %collective-permute-start.2 = (f32[184,128]{1,0:T(8,128)S(1)}, f32[184,128]{1,0:T(8,128)S(1)}, u32[]{:S(2)}, u32[]{:S(2)}) collective-permute-start(f32[184,128]{1,0:T(8,128)S(1)} %get-tuple-element.35), channel_id=1, source_target_pairs={{0,4},{4,8},{8,12},{12,16},{16,20},{20,24},{24,28},{28,0},{1,5},{5... | collective-permute-start | bytes 282632 | tf_op jit(solution)/shard_map/ppermute | solution.py:396
  14.9 8.6 %collective-permute-start.3 = (f32[184,128]{1,0:T(8,128)S(1)}, f32[184,128]{1,0:T(8,128)S(1)}, u32[]{:S(2)}, u32[]{:S(2)}) collective-permute-start(f32[184,128]{1,0:T(8,128)S(1)} %get-tuple-element.36), channel_id=1, source_target_pairs={{0,28},{4,0},{8,4},{12,8},{16,12},{20,16},{24,20},{28,24},{1,29},{... | collective-permute-start | bytes 282632 | tf_op jit(solution)/shard_map/ppermute | solution.py:396
  23.5 6.7 %all-to-all-start = ((f32[32,8,128]{2,1,0:T(8,128)}), f32[32,8,128]{2,1,0:T(8,128)S(1)}, u32[]{:S(2)}, u32[]{:S(2)}) async-start(f32[32,8,128]{2,1,0:T(8,128)} %get-tuple-element.50), calls=%async_computation | async-start | bytes 262144 | tf_op jit(solution)/shard_map/all_to_all | solution.py:400
  30.2 0.0 collective-permute-done.2.low_ref
  30.2 0.0 collective-permute-done.3.high_ref
  30.3 4.1 %collective-permute-start.4 = (f32[592,128]{1,0:T(8,128)S(1)}, f32[592,128]{1,0:T(8,128)S(1)}, u32[]{:S(2)}, u32[]{:S(2)}) collective-permute-start(f32[592,128]{1,0:T(8,128)S(1)} %get-tuple-element.37), channel_id=1, source_target_pairs={{0,32},{32,64},{64,96},{96,128},{128,160},{160,192},{192,224},{224... | collective-permute-start | bytes 909320 | tf_op jit(solution)/shard_map/ppermute | solution.py:396
  34.4 0.0 collective-permute-start.5
  34.4 5.2 %all-to-all-done.slab_ref = f32[32,8,128]{2,1,0:T(8,128)S(1)} async-done(((f32[32,8,128]{2,1,0:T(8,128)}), f32[32,8,128]{2,1,0:T(8,128)S(1)}, u32[]{:S(2)}, u32[]{:S(2)}) %all-to-all-start) | async-done | bytes 131104 | tf_op jit(solution)/shard_map/all_to_all | solution.py:400
  39.6 3.5 %shard_map.79 = f32[16,8,128]{2,1,0:T(8,128)} custom-call(f32[32,8,128]{2,1,0:T(8,128)S(1)} %all-to-all-done.slab_ref, f32[64,64]{1,0:T(8,128)S(1)} %get-tuple-element.51.cas_y_ref, f32[128,128]{1,0:T(8,128)S(1)} %get-tuple-element.52.cas_z_ref, f32[33,64,128]{2,1,0:T(8,128)S(1)} %get-tuple-element.53.along_ref, f32[4,128,128]{2,1,0:T(8,128)S(1)} %get-tuple-element.54.own_z_ref), custom_call_target="tpu_custom_call" | custom-call | flops 50000000 | bytes 1556480 | tf_op jit(solution)/shard_map/pallas_call | solution.py:383
  43.1 11.1 %all-to-all-start.1 = ((f32[16,8,128]{2,1,0:T(8,128)}), f32[16,8,128]{2,1,0:T(8,128)S(1)}, u32[]{:S(2)}, u32[]{:S(2)}) async-start(f32[16,8,128]{2,1,0:T(8,128)} %shard_map.79), calls=%async_computation.1 | async-start | bytes 131072 | tf_op jit(solution)/shard_map/all_to_all | solution.py:400
  54.2 1.7 %shard_map.76 = (bf16[128,144]{1,0:T(8,128)(2,1)S(1)}, bf16[4,256,128]{2,1,0:T(8,128)(2,1)S(1)}, bf16[4,256,128]{2,1,0:T(8,128)(2,1)S(1)}, bf16[64,96]{1,0:T(8,1...) custom-call(f32[2,4]{1,0:T(2,128)S(1)} %get-tuple-element.39.width_ref, ...), custom_call_target="tpu_custom_call" | custom-call | flops 10000000 | bytes 64 | tf_op jit(solution)/shard_map/pallas_call | solution.py:383
  55.9 1.7 %shard_map.77 = (f32[4,16,32,128]{3,2,1,0:T(8,128)S(1)}, f32[4,8,16,128]{3,2,1,0:T(8,128)S(1)}) custom-call(f32[16,32,128]{2,1,0:T(8,128)S(1)} %get-tuple-element.30.f_ref, f32[4,16,128]{2,1,0:T(8,128)S(1)} %get-tuple-element.31.mid_ref, f32[80,128]{1,0:T(8,128)S(1)} %get-tuple-element.34.halo_ref, f32[184,128]{1,0:T(8,128)S(1)} %collective-permute-done.2.low_ref, ...), custom_call_target="tpu_custom_call" | custom-call | flops 100000000 | bytes 1359872 | tf_op jit(solution)/shard_map/pallas_call | solution.py:383
  57.6 0.0 collective-permute-done.4.low_ref
  57.6 0.0 collective-permute-done.5.high_ref
  57.6 3.2 %shard_map.78.near_ref = f32[16,32,128]{2,1,0:T(8,128)S(1)} custom-call(f32[592,128]{1,0:T(8,128)S(1)} %collective-permute-done.4.low_ref, f32[592,128]{1,0:T(8,128)S(1)} %collective-permute-done.5.high_ref, f32[4,16,32,128]{3,2,1,0:T(8,128)S(1)} %get-tuple-element.47.fine_ref, f32[4,8,16,128]{3,2,1,0:T(8,128)S(1)} %get-tuple-element.48.middle_ref, ...), custom_call_target="tpu_custom_call" | custom-call | flops 100000000 | bytes 3047424 | tf_op jit(solution)/shard_map/pallas_call | solution.py:383
  60.8 1.1 %all-to-all-done.1.top_ref = f32[16,8,128]{2,1,0:T(8,128)S(1)} async-done(((f32[16,8,128]{2,1,0:T(8,128)}), f32[16,8,128]{2,1,0:T(8,128)S(1)}, u32[]{:S(2)}, u32[]{:S(2)}) %all-to-all-start.1) | async-done | bytes 65568 | tf_op jit(solution)/shard_map/all_to_all | solution.py:400
  62.0 0.9 %shard_map.80 = f32[16,32,128]{2,1,0:T(8,128)} custom-call(f32[16,32,128]{2,1,0:T(8,128)S(1)} %shard_map.78.near_ref, f32[16,8,128]{2,1,0:T(8,128)S(1)} %all-to-all-done.1.top_ref), custom_call_target="tpu_custom_call" | custom-call | flops 1000000 | bytes 327680 | tf_op jit(solution)/shard_map/pallas_call | solution.py:383
  (2 shorter events, 0.1 us)
Async XLA Ops:
  2.2 7.1 %collective-permute-start = (f32[80,128]{1,0:T(8,128)S(1)}, f32[80,128]{1,0:T(8,128)S(1)}, u32[]{:S(2)}, u32[]{:S(2)}) collective-permute-start(f32[80,128]{1,0:T(8,128)S(1)} %get-tuple-element.32), channel_id=1, source_target_pairs={{0,1},{1,2},{2,3},{3,0},{4,5},{5,6},{6,7},{7,4},{8,9},{9,10},{10,1... | collective-permute-start | bytes 122888 | tf_op jit(solution)/shard_map/ppermute | solution.py:396
  6.1 4.7 %collective-permute-start.1 = (f32[80,128]{1,0:T(8,128)S(1)}, f32[80,128]{1,0:T(8,128)S(1)}, u32[]{:S(2)}, u32[]{:S(2)}) collective-permute-start(f32[80,128]{1,0:T(8,128)S(1)} %get-tuple-element.33), channel_id=1, source_target_pairs={{0,3},{1,0},{2,1},{3,2},{4,7},{5,4},{6,5},{7,6},{8,11},{9,8},{10,9... | collective-permute-start | bytes 122888 | tf_op jit(solution)/shard_map/ppermute | solution.py:396
  10.9 19.3 %collective-permute-start.2 = (f32[184,128]{1,0:T(8,128)S(1)}, f32[184,128]{1,0:T(8,128)S(1)}, u32[]{:S(2)}, u32[]{:S(2)}) collective-permute-start(f32[184,128]{1,0:T(8,128)S(1)} %get-tuple-element.35), channel_id=1, source_target_pairs={{0,4},{4,8},{8,12},{12,16},{16,20},{20,24},{24,28},{28,0},{1,5},{5... | collective-permute-start | bytes 282632 | tf_op jit(solution)/shard_map/ppermute | solution.py:396
  14.9 15.3 %collective-permute-start.3 = (f32[184,128]{1,0:T(8,128)S(1)}, f32[184,128]{1,0:T(8,128)S(1)}, u32[]{:S(2)}, u32[]{:S(2)}) collective-permute-start(f32[184,128]{1,0:T(8,128)S(1)} %get-tuple-element.36), channel_id=1, source_target_pairs={{0,28},{4,0},{8,4},{12,8},{16,12},{20,16},{24,20},{28,24},{1,29},{... | collective-permute-start | bytes 282632 | tf_op jit(solution)/shard_map/ppermute | solution.py:396
  23.5 16.2 %all-to-all-start = ((f32[32,8,128]{2,1,0:T(8,128)}), f32[32,8,128]{2,1,0:T(8,128)S(1)}, u32[]{:S(2)}, u32[]{:S(2)}) async-start(f32[32,8,128]{2,1,0:T(8,128)} %get-tuple-element.50), calls=%async_computation | async-start | bytes 262144 | tf_op jit(solution)/shard_map/all_to_all | solution.py:400
  30.3 27.4 %collective-permute-start.4 = (f32[592,128]{1,0:T(8,128)S(1)}, f32[592,128]{1,0:T(8,128)S(1)}, u32[]{:S(2)}, u32[]{:S(2)}) collective-permute-start(f32[592,128]{1,0:T(8,128)S(1)} %get-tuple-element.37), channel_id=1, source_target_pairs={{0,32},{32,64},{64,96},{96,128},{128,160},{160,192},{192,224},{224... | collective-permute-start | bytes 909320 | tf_op jit(solution)/shard_map/ppermute | solution.py:396
  34.4 23.2 %collective-permute-start.5 = (f32[592,128]{1,0:T(8,128)S(1)}, f32[592,128]{1,0:T(8,128)S(1)}, u32[]{:S(2)}, u32[]{:S(2)}) collective-permute-start(f32[592,128]{1,0:T(8,128)S(1)} %get-tuple-element.38), channel_id=1, source_target_pairs={{0,480},{32,0},{64,32},{96,64},{128,96},{160,128},{192,160},{224,1... | collective-permute-start | bytes 909320 | tf_op jit(solution)/shard_map/ppermute | solution.py:396
  43.1 18.9 %all-to-all-start.1 = ((f32[16,8,128]{2,1,0:T(8,128)}), f32[16,8,128]{2,1,0:T(8,128)S(1)}, u32[]{:S(2)}, u32[]{:S(2)}) async-start(f32[16,8,128]{2,1,0:T(8,128)} %shard_map.79), calls=%async_computation.1 | async-start | bytes 131072 | tf_op jit(solution)/shard_map/all_to_all | solution.py:400

commit v3 on v2

--- a/solution.py
+++ b/solution.py
@@ -24,7 +24,7 @@
 CX, CY, CZ = 64, 64, 128
 EY, EMY = BY + 2 * RADIUS, MY + 2 * RADIUS
 GX, GY, GZ = 16, 8, 4
-FETCHED = 7
+FETCHED, TABLES = 3, 5
 ZROWS = 2 * BY + MY
 YROWS = BX * 8 + 2 * 8 + 5 * 8
 XROWS = 8 * EY + EY + 5 * EMY
@@ -49,7 +49,21 @@
     cosine = np.cos(2.0 * math.pi / CX * (np.outer(shifts, np.arange(CX)) % CX))
     along_x = np.einsum("dm,myz->dyz", cosine, mult) / (CX * CY * CZ)
     own_z = np.stack([np.tile(cas_z[:, 32 * g : 32 * g + 32], (1, 4)) for g in range(GZ)])
-    return [np.asarray(t, np.float32) for t in (cas_y, cas_z, along_x, own_z)]
+
+    def split(table):
+        table = np.asarray(table, np.float32)
+        high = table.astype(BF16)
+        return high, (table - high.astype(np.float32)).astype(BF16)
+
+    high, low = split(cas_y)
+    tables = [
+        np.concatenate([high, high, low], axis=1),
+        np.asarray(np.concatenate([cas_y, cas_y], axis=1), np.float32),
+        np.stack(split(cas_z)),
+        np.stack(split(own_z), axis=1),
+        np.asarray(along_x, np.float32),
+    ]
+    return [jnp.asarray(table) for table in tables]
 
 
 def lanes(shape):
@@ -74,7 +88,14 @@
     return high, (value - high.astype(F32)).astype(BF16)
 
 
-def weights_kernel(width_ref, weight_ref, gy_ref, gzh_ref, gzl_ref, my_ref, mzh_ref, mzl_ref, cx_ref):
+def weights_kernel(width_ref, weight_ref, *refs):
+    fetches = [
+        pltpu.make_async_copy(refs[i], refs[TABLES + 7 + i], refs[-1].at[i]) for i in range(TABLES)
+    ]
+    for fetch in fetches:
+        fetch.start()
+    gy_ref, gzh_ref, gzl_ref, my_ref, mzh_ref, mzl_ref, cx_ref = refs[TABLES : TABLES + 7]
+
     def scale(level, term):
         width = jnp.broadcast_to(width_ref[level : level + 1, term : term + 1], (8, 128))
         inverse = 1.0 / (2.0 * width * width)
@@ -122,6 +143,8 @@
         for offset in range(TAPS):
             value = jnp.exp(-float(offset * offset) * inverse) * norm * weight_ref[1:2, term : term + 1]
             cx_ref[(TERMS + term) * TAPS + offset] = jnp.broadcast_to(value, (8, 128))
+    for fetch in fetches:
+        fetch.wait()
 
 
 def restrict_kernel(*refs):
@@ -181,9 +204,10 @@
         fetch.wait()
 
 
-def modes_kernel(slab_ref, cas_y_ref, cas_z_ref, along_ref, own_z_ref, out_ref):
+def modes_kernel(slab_ref, cas_y_ref, twice_y_ref, cas_z_ref, own_z_ref, along_ref, out_ref, modes_ref, wide_ref):
     rows = [jnp.concatenate([slab_ref[gy * GZ + gz] for gz in range(GZ)], axis=1) for gy in range(GY)]
-    by_y = exact(cas_y_ref[...], jnp.concatenate(rows, axis=0))
+    high, low = halves(jnp.concatenate(rows, axis=0))
+    by_y = dot(cas_y_ref[...], jnp.concatenate([high, low, high], axis=0))
     lane = lanes((CY, 128)) >> 5
     planes = []
     for x in range(4):
@@ -191,28 +215,40 @@
         for gz in range(GZ):
             plane = jnp.where(lane == gz, roll(by_y[:, gz * 128 : (gz + 1) * 128], (gz - x) * 32), plane)
         planes.append(plane)
-    by_z = exact(jnp.concatenate(planes, axis=0), cas_z_ref[...])
-    source = [by_z[x * CY : (x + 1) * CY, :] for x in range(4)]
-    own_y = cas_y_ref[pl.ds(pl.multiple_of(lax.axis_index("gy") * 8, 8), 8), :]
-    own_z = own_z_ref[lax.axis_index("gz")]
+    high, low = halves(jnp.concatenate(planes, axis=0))
+    modes_ref[...] = dot(high, cas_z_ref[0]) + dot(low, cas_z_ref[0]) + dot(high, cas_z_ref[1])
+
+    def tile_step(tile, carry):
+        start = pl.multiple_of(tile * 16, 16)
+        source = [modes_ref[pl.ds(x * CY + start, 16), :] for x in range(4)]
+        table = [along_ref[abs(shift), pl.ds(start, 16), :] for shift in (0, -1, -2, -3)]
+        for place in range(CX):
+            if place:
+                table = [along_ref[min(place, CX - place), pl.ds(start, 16), :]] + table[:3]
+            total = table[0] * source[0]
+            for x in range(1, 4):
+                total = total + table[x] * source[x]
+            high, low = halves(total)
+            wide_ref[pl.ds(start, 16), place * 128 : (place + 1) * 128] = high
+            wide_ref[pl.ds(CY + start, 16), place * 128 : (place + 1) * 128] = low
+        return carry
+
+    lax.fori_loop(0, CY // 16, tile_step, 0)
+    own_y = twice_y_ref[pl.ds(pl.multiple_of(lax.axis_index("gy") * 8, 8), 8), :]
+    high, low = halves(own_y)
+    low = jnp.where(lanes((8, 128)) < CY, low.astype(F32), 0.0)
+    own_y = jnp.concatenate([high.astype(F32), low], axis=0).astype(BF16)
+    back_y = dot(own_y, wide_ref[...])
+    back_y = back_y[0:8] + back_y[8:16]
+    high, low = halves(jnp.concatenate([back_y[:, x * 128 : (x + 1) * 128] for x in range(CX)], axis=0))
+    own_z = own_z_ref.at[lax.axis_index("gz")]
+    back_z = dot(high, own_z[0]) + dot(low, own_z[0]) + dot(high, own_z[1])
     me = lax.axis_index("gx")
     lane = lanes((8, 128)) >> 5
     for block in range(GX):
-        outs = []
-        for x in range(4):
-            total = None
-            for other in range(4):
-                shift = (block * 4 + x - other) % CX
-                part = along_ref[min(shift, CX - shift)] * source[other]
-                total = part if total is None else total + part
-            outs.append(total)
-        back_y = exact(own_y, jnp.concatenate(outs, axis=1))
-        back_z = exact(
-            jnp.concatenate([back_y[:, x * 128 : (x + 1) * 128] for x in range(4)], axis=0), own_z
-        )
-        result = back_z[0:8]
+        result = back_z[block * 32 : block * 32 + 8]
         for x in range(1, 4):
-            result = jnp.where(lane == x, back_z[x * 8 : (x + 1) * 8], result)
+            result = jnp.where(lane == x, back_z[block * 32 + x * 8 : block * 32 + (x + 1) * 8], result)
         out_ref[lax.rem(me + block, GX)] = result
 
 
@@ -374,11 +410,11 @@
         out_ref[x] = near_ref[x] + wide_ref[(x // 4) * BY : (x // 4 + 1) * BY, :]
 
 
-def call(kernel, outs, args, scratch=(), flops=0, hbm=False, limit=4):
+def call(kernel, outs, args, scratch=(), flops=0, hbm=0, limit=4):
     vmem = pl.BlockSpec(memory_space=pltpu.VMEM)
-    specs = [pl.BlockSpec(memory_space=pltpu.HBM) if hbm else vmem] * len(args)
-    if hbm:
-        args = [pltpu.with_memory_space_constraint(a, pltpu.HBM) for a in args]
+    near = len(args) - hbm
+    specs = [vmem] * near + [pl.BlockSpec(memory_space=pltpu.HBM)] * hbm
+    args = args[:near] + [pltpu.with_memory_space_constraint(a, pltpu.HBM) for a in args[near:]]
     size = sum(a.size * a.dtype.itemsize for a in args)
     return pl.pallas_call(
         kernel,
@@ -401,20 +437,20 @@
 
 
 def potential(charges, term_width, term_weight):
-    sources = [charges, term_width, term_weight] + [jnp.asarray(t) for t in constant_tables()]
-    coarse, mid, z_up, z_down, charges, term_width, term_weight, cas_y, cas_z, along_x, own_z = call(
+    sources = [charges, term_width, term_weight]
+    coarse, mid, z_up, z_down, charges, term_width, term_weight = call(
         restrict_kernel,
         [((GY * GZ, 8, 128), F32), ((4, MY, 128), F32), ((ZROWS, 128), F32), ((ZROWS, 128), F32)]
         + [(a.shape, a.dtype) for a in sources],
         sources,
         [pltpu.VMEM((MX * MY, 128), F32), pltpu.SemaphoreType.DMA((FETCHED,))],
         flops=10**7,
-        hbm=True,
-        limit=4,
+        hbm=3,
     )
     slab = exchange(coarse, ("gy", "gz"))
     z_low, z_high = ring(z_up, "gz", 1), ring(z_down, "gz", -1)
-    gy, gzh, gzl, my, mzh, mzl, cx = call(
+    tables = constant_tables()
+    gy, gzh, gzl, my, mzh, mzl, cx, *tables = call(
         weights_kernel,
         [
             ((TERMS * BY, 3 * EY), BF16),
@@ -424,9 +460,12 @@
             ((TERMS, 128, 128), BF16),
             ((TERMS, 128, 128), BF16),
             ((2 * TERMS * TAPS, 8, 128), F32),
-        ],
-        [term_width, term_weight],
+        ]
+        + [(a.shape, a.dtype) for a in tables],
+        [term_width, term_weight] + tables,
+        [pltpu.SemaphoreType.DMA((TABLES,))],
         flops=10**7,
+        hbm=TABLES,
     )
     bands = [gy, gzh, gzl, my, mzh, mzl]
     halo, y_up, y_down = call(
@@ -437,7 +476,12 @@
     )
     low, high = ring(y_up, "gy", 1), ring(y_down, "gy", -1)
     (partial,) = call(
-        modes_kernel, [((GX, 8, 128), F32)], [slab, cas_y, cas_z, along_x, own_z], flops=5 * 10**7, limit=8
+        modes_kernel,
+        [((GX, 8, 128), F32)],
+        [slab] + tables,
+        [pltpu.VMEM((4 * CY, 128), F32), pltpu.VMEM((2 * CY, CX * 128), BF16)],
+        flops=5 * 10**7,
+        limit=8,
     )
     top = exchange(partial, "gx")
     x_up, x_down = call(

time: 63.2 us -> 64.9 us (1.027)
  local copies, waits for them, and re-layouts: 0 us -> 4.48 us
  waiting for transfers between devices: 7.92 us -> 4.42 us
  Pallas kernels: 13.1 us -> 14.1 us
    unnamed x0 -> x12, local copies, waits for them, and re-layouts: none -> 4.48 us
    all_to_all x2, waiting for transfers between devices: 6.37 us -> 2.87 us  [exchange(): return lax.all_to_all(value, axis, 0, 0, tiled=True)]
    pallas_call x8, Pallas kernels: 13.1 us -> 14.1 us  [call(): pl.pallas_call(kernel, out_shape=[jax.ShapeDtypeStruct(shape, dtype) for...]
  transfers between devices with their start and end apart: 8 -> 8, of which waited for: 3 -> 2; matrix products, arithmetic and copies ran while one was open for 0% -> 0% of each run, Pallas kernels for 16% -> 17%
where the time goes in v3:
time: 64.9 us; the launch traced here: 64.3 us
  starting transfers between devices  41.2 us (63%)
  Pallas kernels  14.1 us (22%)
  local copies, waits for them, and re-layouts  4.48 us (7%)
  waiting for transfers between devices  4.42 us (7%)
    ppermute x6, starting transfers between devices, ring(): lax.ppermute(value, axis, [(i, (i + step) % count) for i in range(count)])  23.8 us
    all_to_all x2, starting transfers between devices, exchange(): return lax.all_to_all(value, axis, 0, 0, tiled=True)  17.4 us
    pallas_call x8, Pallas kernels, call(): pl.pallas_call(kernel, out_shape=[jax.ShapeDtypeStruct(shape, dtype) for...  14.1 us
    unnamed x12, local copies, waits for them, and re-layouts  4.48 us
    all_to_all x2, waiting for transfers between devices, exchange(): return lax.all_to_all(value, axis, 0, 0, tiled=True)  2.87 us
    ppermute x6, waiting for transfers between devices, ring(): lax.ppermute(value, axis, [(i, (i + step) % count) for i in range(count)])  1.55 us
  transfers between devices with their start and end apart: 8, of which 2 were waited for; matrix products, arithmetic and copies ran while one was open for 0% of the time, Pallas kernels for 17%

profile of v3, /device:TPU:1, one launch (start us, length us, event | category | flops | bytes accessed | tf_op | source)
XLA Modules:
  0.0 64.3 jit_solution(2030845459382641340)
XLA Ops:
  0.0 2.0 %shard_map.82 = (f32[32,8,128]{2,1,0:T(8,128)}, f32[4,16,128]{2,1,0:T(8,128)S(1)}, f32[80,128]{1,0:T(8,128)S(1)}, f32[80,128]{1,0:T(8,128)S(1)}, f32[16,32,128]{...) custom-call(f32[16,32,128]{2,1,0:T(8,128)} %refs_0_.2, f32[2,4]{1,0:T(2,128)} %refs_1_.2, f32[2,4]{1,0:T(2,128)} %refs_2_.2), custom_call_target="tpu_custom_call" | custom-call | flops 10000000 | bytes 262208 | tf_op jit(solution)/shard_map/pallas_call | solution.py:419
  2.0 3.9 %collective-permute-start = (f32[80,128]{1,0:T(8,128)S(1)}, f32[80,128]{1,0:T(8,128)S(1)}, u32[]{:S(2)}, u32[]{:S(2)}) collective-permute-start(f32[80,128]{1,0:T(8,128)S(1)} %get-tuple-element.33), channel_id=1, source_target_pairs={{0,1},{1,2},{2,3},{3,0},{4,5},{5,6},{6,7},{7,4},{8,9},{9,10},{10,1... | collective-permute-start | bytes 122888 | tf_op jit(solution)/shard_map/ppermute | solution.py:432
  5.9 3.2 %collective-permute-start.1 = (f32[80,128]{1,0:T(8,128)S(1)}, f32[80,128]{1,0:T(8,128)S(1)}, u32[]{:S(2)}, u32[]{:S(2)}) collective-permute-start(f32[80,128]{1,0:T(8,128)S(1)} %get-tuple-element.34), channel_id=1, source_target_pairs={{0,3},{1,0},{2,1},{3,2},{4,7},{5,4},{6,5},{7,6},{8,11},{9,8},{10,9... | collective-permute-start | bytes 122888 | tf_op jit(solution)/shard_map/ppermute | solution.py:432
  9.1 0.0 collective-permute-done.zlow_ref
  9.1 1.5 %collective-permute-done.1.zhigh_ref = f32[80,128]{1,0:T(8,128)S(1)} collective-permute-done((f32[80,128]{1,0:T(8,128)S(1)}, f32[80,128]{1,0:T(8,128)S(1)}, u32[]{:S(2)}, u32[]{:S(2)}) %collective-permute-start.1) | collective-permute-done | bytes 40992 | tf_op jit(solution)/shard_map/ppermute | solution.py:432
  10.7 4.0 %collective-permute-start.2 = (f32[184,128]{1,0:T(8,128)S(1)}, f32[184,128]{1,0:T(8,128)S(1)}, u32[]{:S(2)}, u32[]{:S(2)}) collective-permute-start(f32[184,128]{1,0:T(8,128)S(1)} %get-tuple-element.36), channel_id=1, source_target_pairs={{0,4},{4,8},{8,12},{12,16},{16,20},{20,24},{24,28},{28,0},{1,5},{5... | collective-permute-start | bytes 282632 | tf_op jit(solution)/shard_map/ppermute | solution.py:432
  14.7 8.6 %collective-permute-start.3 = (f32[184,128]{1,0:T(8,128)S(1)}, f32[184,128]{1,0:T(8,128)S(1)}, u32[]{:S(2)}, u32[]{:S(2)}) collective-permute-start(f32[184,128]{1,0:T(8,128)S(1)} %get-tuple-element.37), channel_id=1, source_target_pairs={{0,28},{4,0},{8,4},{12,8},{16,12},{20,16},{24,20},{28,24},{1,29},{... | collective-permute-start | bytes 282632 | tf_op jit(solution)/shard_map/ppermute | solution.py:432
  23.3 6.7 %all-to-all-start = ((f32[32,8,128]{2,1,0:T(8,128)}), f32[32,8,128]{2,1,0:T(8,128)S(1)}, u32[]{:S(2)}, u32[]{:S(2)}) async-start(f32[32,8,128]{2,1,0:T(8,128)} %get-tuple-element.51), calls=%async_computation | async-start | bytes 262144 | tf_op jit(solution)/shard_map/all_to_all | solution.py:436
  30.0 0.0 collective-permute-done.2.low_ref
  30.0 0.0 collective-permute-done.3.high_ref
  30.0 0.9 %shard_map.84 = (f32[592,128]{1,0:T(8,128)}, f32[592,128]{1,0:T(8,128)}) custom-call(f32[16,32,128]{2,1,0:T(8,128)S(1)} %get-tuple-element.31.f_ref, f32[4,16,128]{2,1,0:T(8,128)S(1)} %get-tuple-element.32.mid_ref, f32[80,128]{1,0:T(8,128)S(1)} %get-tuple-element.35.halo_ref, f32[184,128]{1,0:T(8,128)S(1)} %collective-permute-done.2.low_ref, ...), custom_call_target="tpu_custom_call" | custom-call | flops 1000000 | bytes 524288 | tf_op jit(solution)/shard_map/pallas_call | solution.py:419
  30.9 4.1 %collective-permute-start.4 = (f32[592,128]{1,0:T(8,128)}, f32[592,128]{1,0:T(8,128)S(1)}, u32[]{:S(2)}, u32[]{:S(2)}) collective-permute-start(f32[592,128]{1,0:T(8,128)} %get-tuple-element.38), channel_id=1, source_target_pairs={{0,32},{32,64},{64,96},{96,128},{128,160},{160,192},{192,224},{224... | collective-permute-start | bytes 909320 | tf_op jit(solution)/shard_map/ppermute | solution.py:432
  35.0 0.0 collective-permute-start.5
  35.0 2.9 %shard_map.85 = (bf16[128,144]{1,0:T(8,128)(2,1)S(1)}, bf16[4,256,128]{2,1,0:T(8,128)(2,1)S(1)}, bf16[4,256,128]{2,1,0:T(8,128)(2,1)S(1)}, bf16[64,96]{1,0:T(8,1...) custom-call(f32[2,4]{1,0:T(2,128)S(1)} %get-tuple-element.40.width_r, ...), custom_call_target="tpu_custom_call" | custom-call | flops 10000000 | bytes 1466432 | tf_op jit(solution)/shard_map/pallas_call | solution.py:419
  38.0 0.0 copy-start
  38.0 0.7 %copy-done = bf16[4,2,128,128]{3,2,1,0:T(8,128)(2,1)} copy-done((bf16[4,2,128,128]{3,2,1,0:T(8,128)(2,1)}, bf16[4,2,128,128]{3,2,1,0:T(8,128)(2,1)S(1)}, u32[]{:S(2)}) %copy-start) | copy-done | bytes 262168
  38.7 0.0 copy-start.2
  38.7 0.6 copy-done.2
  39.3 0.0 copy-start.4
  39.3 0.6 copy-done.4
  39.9 0.0 all-to-all-done.slab_ref
  39.9 0.0 copy-start.1
  39.9 0.9 %copy-done.1 = bf16[4,2,128,128]{3,2,1,0:T(8,128)(2,1)S(1)} copy-done((bf16[4,2,128,128]{3,2,1,0:T(8,128)(2,1)S(1)}, bf16[4,2,128,128]{3,2,1,0:T(8,128)(2,1)}, u32[]{:S(2)}) %copy-start.1) | copy-done | bytes 262168
  40.9 0.0 copy-start.3
  40.9 0.8 %copy-done.3 = bf16[2,128,128]{2,1,0:T(8,128)(2,1)S(1)} copy-done((bf16[2,128,128]{2,1,0:T(8,128)(2,1)S(1)}, bf16[2,128,128]{2,1,0:T(8,128)(2,1)}, u32[]{:S(2)}) %copy-start.3) | copy-done | bytes 65560
  41.7 0.0 copy-start.5
  41.7 0.8 %copy-done.5 = f32[64,128]{1,0:T(8,128)S(1)} copy-done((f32[64,128]{1,0:T(8,128)S(1)}, f32[64,128]{1,0:T(8,128)}, u32[]{:S(2)}) %copy-start.5) | copy-done | bytes 32792
  42.5 2.6 %shard_map.88 = f32[16,8,128]{2,1,0:T(8,128)} custom-call(f32[32,8,128]{2,1,0:T(8,128)S(1)} %all-to-all-done.slab_ref, bf16[64,192]{1,0:T(8,128)(2,1)S(1)} %get-tuple-element.52.cas_y_ref, f32[64,128]{1,0:T(8,128)S(1)} %copy-done.5, bf16[2,128,128]{2,1,0:T(8,128)(2,1)S(1)} %copy-done.3, bf16[4,2,128,128]{3,2,1,0:T(8,128)(2,1)S(1)} %copy-done.1, ...), custom_call_target="tpu_custom_call" | custom-call | flops 50000000 | bytes 1597440 | tf_op jit(solution)/shard_map/pallas_call | solution.py:419
  45.0 10.7 %all-to-all-start.1 = ((f32[16,8,128]{2,1,0:T(8,128)}), f32[16,8,128]{2,1,0:T(8,128)S(1)}, u32[]{:S(2)}, u32[]{:S(2)}) async-start(f32[16,8,128]{2,1,0:T(8,128)} %shard_map.88), calls=%async_computation.1 | async-start | bytes 131072 | tf_op jit(solution)/shard_map/all_to_all | solution.py:436
  55.7 1.7 %shard_map.86 = (f32[4,16,32,128]{3,2,1,0:T(8,128)S(1)}, f32[4,8,16,128]{3,2,1,0:T(8,128)S(1)}) custom-call(f32[16,32,128]{2,1,0:T(8,128)S(1)} %get-tuple-element.31.f_ref, f32[4,16,128]{2,1,0:T(8,128)S(1)} %get-tuple-element.32.mid_ref, f32[80,128]{1,0:T(8,128)S(1)} %get-tuple-element.35.halo_ref, f32[184,128]{1,0:T(8,128)S(1)} %collective-permute-done.2.low_ref, ...), custom_call_target="tpu_custom_call" | custom-call | flops 100000000 | bytes 1359872 | tf_op jit(solution)/shard_map/pallas_call | solution.py:419
  57.3 0.0 collective-permute-done.4.low_ref
  57.3 0.0 collective-permute-done.5.high_ref
  57.3 3.2 %shard_map.87.near_ref = f32[16,32,128]{2,1,0:T(8,128)S(1)} custom-call(f32[592,128]{1,0:T(8,128)S(1)} %collective-permute-done.4.low_ref, f32[592,128]{1,0:T(8,128)S(1)} %collective-permute-done.5.high_ref, f32[4,16,32,128]{3,2,1,0:T(8,128)S(1)} %get-tuple-element.48.fine_ref, f32[4,8,16,128]{3,2,1,0:T(8,128)S(1)} %get-tuple-element.49.middle_ref, ...), custom_call_target="tpu_custom_call" | custom-call | flops 100000000 | bytes 3047424 | tf_op jit(solution)/shard_map/pallas_call | solution.py:419
  60.6 2.9 %all-to-all-done.1.top_ref = f32[16,8,128]{2,1,0:T(8,128)S(1)} async-done(((f32[16,8,128]{2,1,0:T(8,128)}), f32[16,8,128]{2,1,0:T(8,128)S(1)}, u32[]{:S(2)}, u32[]{:S(2)}) %all-to-all-start.1) | async-done | bytes 65568 | tf_op jit(solution)/shard_map/all_to_all | solution.py:436
  63.4 0.9 %shard_map.89 = f32[16,32,128]{2,1,0:T(8,128)} custom-call(f32[16,32,128]{2,1,0:T(8,128)S(1)} %shard_map.87.near_ref, f32[16,8,128]{2,1,0:T(8,128)S(1)} %all-to-all-done.1.top_ref), custom_call_target="tpu_custom_call" | custom-call | flops 1000000 | bytes 327680 | tf_op jit(solution)/shard_map/pallas_call | solution.py:419
  (1 shorter events, 0.0 us)
Async XLA Ops:
  2.0 7.1 %collective-permute-start = (f32[80,128]{1,0:T(8,128)S(1)}, f32[80,128]{1,0:T(8,128)S(1)}, u32[]{:S(2)}, u32[]{:S(2)}) collective-permute-start(f32[80,128]{1,0:T(8,128)S(1)} %get-tuple-element.33), channel_id=1, source_target_pairs={{0,1},{1,2},{2,3},{3,0},{4,5},{5,6},{6,7},{7,4},{8,9},{9,10},{10,1... | collective-permute-start | bytes 122888 | tf_op jit(solution)/shard_map/ppermute | solution.py:432
  5.9 4.7 %collective-permute-start.1 = (f32[80,128]{1,0:T(8,128)S(1)}, f32[80,128]{1,0:T(8,128)S(1)}, u32[]{:S(2)}, u32[]{:S(2)}) collective-permute-start(f32[80,128]{1,0:T(8,128)S(1)} %get-tuple-element.34), channel_id=1, source_target_pairs={{0,3},{1,0},{2,1},{3,2},{4,7},{5,4},{6,5},{7,6},{8,11},{9,8},{10,9... | collective-permute-start | bytes 122888 | tf_op jit(solution)/shard_map/ppermute | solution.py:432
  10.7 19.3 %collective-permute-start.2 = (f32[184,128]{1,0:T(8,128)S(1)}, f32[184,128]{1,0:T(8,128)S(1)}, u32[]{:S(2)}, u32[]{:S(2)}) collective-permute-start(f32[184,128]{1,0:T(8,128)S(1)} %get-tuple-element.36), channel_id=1, source_target_pairs={{0,4},{4,8},{8,12},{12,16},{16,20},{20,24},{24,28},{28,0},{1,5},{5... | collective-permute-start | bytes 282632 | tf_op jit(solution)/shard_map/ppermute | solution.py:432
  14.7 15.3 %collective-permute-start.3 = (f32[184,128]{1,0:T(8,128)S(1)}, f32[184,128]{1,0:T(8,128)S(1)}, u32[]{:S(2)}, u32[]{:S(2)}) collective-permute-start(f32[184,128]{1,0:T(8,128)S(1)} %get-tuple-element.37), channel_id=1, source_target_pairs={{0,28},{4,0},{8,4},{12,8},{16,12},{20,16},{24,20},{28,24},{1,29},{... | collective-permute-start | bytes 282632 | tf_op jit(solution)/shard_map/ppermute | solution.py:432
  23.3 16.6 %all-to-all-start = ((f32[32,8,128]{2,1,0:T(8,128)}), f32[32,8,128]{2,1,0:T(8,128)S(1)}, u32[]{:S(2)}, u32[]{:S(2)}) async-start(f32[32,8,128]{2,1,0:T(8,128)} %get-tuple-element.51), calls=%async_computation | async-start | bytes 262144 | tf_op jit(solution)/shard_map/all_to_all | solution.py:436
  30.9 26.4 %collective-permute-start.4 = (f32[592,128]{1,0:T(8,128)}, f32[592,128]{1,0:T(8,128)S(1)}, u32[]{:S(2)}, u32[]{:S(2)}) collective-permute-start(f32[592,128]{1,0:T(8,128)} %get-tuple-element.38), channel_id=1, source_target_pairs={{0,32},{32,64},{64,96},{96,128},{128,160},{160,192},{192,224},{224... | collective-permute-start | bytes 909320 | tf_op jit(solution)/shard_map/ppermute | solution.py:432
  35.0 22.3 %collective-permute-start.5 = (f32[592,128]{1,0:T(8,128)}, f32[592,128]{1,0:T(8,128)S(1)}, u32[]{:S(2)}, u32[]{:S(2)}) collective-permute-start(f32[592,128]{1,0:T(8,128)} %get-tuple-element.39), channel_id=1, source_target_pairs={{0,480},{32,0},{64,32},{96,64},{128,96},{160,128},{192,160},{224,1... | collective-permute-start | bytes 909320 | tf_op jit(solution)/shard_map/ppermute | solution.py:432
  38.0 0.7 %copy-start = (bf16[4,2,128,128]{3,2,1,0:T(8,128)(2,1)}, bf16[4,2,128,128]{3,2,1,0:T(8,128)(2,1)S(1)}, u32[]{:S(2)}) copy-start(bf16[4,2,128,128]{3,2,1,0:T(8,128)(2,1)S(1)} %get-tuple-element.55.own_z_ref) | copy-start | bytes 786436
  38.7 0.6 copy-start.2
  39.3 0.6 copy-start.4
  39.9 1.0 %copy-start.1 = (bf16[4,2,128,128]{3,2,1,0:T(8,128)(2,1)S(1)}, bf16[4,2,128,128]{3,2,1,0:T(8,128)(2,1)}, u32[]{:S(2)}) copy-start(bf16[4,2,128,128]{3,2,1,0:T(8,128)(2,1)} %copy-done) | copy-start | bytes 786436
  40.9 0.8 %copy-start.3 = (bf16[2,128,128]{2,1,0:T(8,128)(2,1)S(1)}, bf16[2,128,128]{2,1,0:T(8,128)(2,1)}, u32[]{:S(2)}) copy-start(bf16[2,128,128]{2,1,0:T(8,128)(2,1)} %copy-done.2) | copy-start | bytes 196612
  41.7 0.8 %copy-start.5 = (f32[64,128]{1,0:T(8,128)S(1)}, f32[64,128]{1,0:T(8,128)}, u32[]{:S(2)}) copy-start(f32[64,128]{1,0:T(8,128)} %copy-done.4) | copy-start | bytes 98308
  45.0 18.4 %all-to-all-start.1 = ((f32[16,8,128]{2,1,0:T(8,128)}), f32[16,8,128]{2,1,0:T(8,128)S(1)}, u32[]{:S(2)}, u32[]{:S(2)}) async-start(f32[16,8,128]{2,1,0:T(8,128)} %shard_map.88), calls=%async_computation.1 | async-start | bytes 131072 | tf_op jit(solution)/shard_map/all_to_all | solution.py:436

commit v4 on v3

--- a/solution.py
+++ b/solution.py
@@ -24,7 +24,7 @@
 CX, CY, CZ = 64, 64, 128
 EY, EMY = BY + 2 * RADIUS, MY + 2 * RADIUS
 GX, GY, GZ = 16, 8, 4
-FETCHED, TABLES = 3, 5
+FETCHED, PIECES = 8, 14
 ZROWS = 2 * BY + MY
 YROWS = BX * 8 + 2 * 8 + 5 * 8
 XROWS = 8 * EY + EY + 5 * EMY
@@ -88,34 +88,38 @@
     return high, (value - high.astype(F32)).astype(BF16)
 
 
-def weights_kernel(width_ref, weight_ref, *refs):
-    fetches = [
-        pltpu.make_async_copy(refs[i], refs[TABLES + 7 + i], refs[-1].at[i]) for i in range(TABLES)
-    ]
-    for fetch in fetches:
-        fetch.start()
-    gy_ref, gzh_ref, gzl_ref, my_ref, mzh_ref, mzl_ref, cx_ref = refs[TABLES : TABLES + 7]
+def weights_kernel(width_ref, weight_ref, gy_ref, gzh_ref, gzl_ref, my_ref, mzh_ref, mzl_ref, cx_ref):
+    offset = lanes((8, 128)) - RADIUS
+    squares = (offset * offset).astype(F32)
 
     def scale(level, term):
         width = jnp.broadcast_to(width_ref[level : level + 1, term : term + 1], (8, 128))
-        inverse = 1.0 / (2.0 * width * width)
-        offset = lanes((8, 128)) - RADIUS
-        values = jnp.exp(-(offset * offset).astype(F32) * inverse)
-        values = jnp.where(offset <= RADIUS, values, 0.0)
-        norm = 1.0 / jnp.sum(values, axis=1, keepdims=True)
-        return inverse[0:1, 0:1], norm[0:1, 0:1]
-
-    def taps(offset, inverse, norm):
-        values = jnp.exp(-(offset * offset).astype(F32) * inverse) * norm
-        return jnp.where(jnp.abs(offset) <= RADIUS, values, 0.0)
+        inverse = -1.0 / (2.0 * width * width)
+        values = jnp.where(offset <= RADIUS, jnp.exp(squares * inverse), 0.0)
+        norm = 1.0 / jnp.broadcast_to(jnp.sum(values, axis=1, keepdims=True), (8, 128))
+        weight = jnp.broadcast_to(weight_ref[level : level + 1, term : term + 1], (8, 128))
+        for distance in range(TAPS):
+            value = jnp.exp(float(distance * distance) * inverse) * norm * weight
+            row = (level * TERMS + term) * TAPS + distance
+            cx_ref[row : row + 1, :] = value[0:1, :]
+        return inverse, norm
+
+    def taps(place, inverse, norm):
+        rows, columns = place.shape
+        inverse, norm = [
+            jnp.concatenate([jnp.concatenate([v] * (columns // 128), axis=1)] * (rows // 8), axis=0) for v in (inverse, norm)
+        ]
+        values = jnp.exp((place * place).astype(F32) * inverse) * norm
+        return jnp.where(jnp.abs(place) <= RADIUS, values, 0.0)
 
     def along_y(ref, term, inverse, norm, out, ext):
-        shape = (out, 3 * ext)
+        shape = (out, 256 if 3 * ext > 128 else 128)
         column = lanes(shape)
         row = lax.broadcasted_iota(jnp.int32, shape, 0)
         part = (column >= ext).astype(jnp.int32) + (column >= 2 * ext).astype(jnp.int32)
         high, low = halves(taps(column - part * ext - RADIUS - row, inverse, norm))
-        ref[term * out : (term + 1) * out, :] = jnp.where(part < 2, high.astype(F32), low.astype(F32)).astype(BF16)
+        both = jnp.where(part < 2, high.astype(F32), low.astype(F32))
+        ref[term * out : (term + 1) * out, :] = both[:, : 3 * ext].astype(BF16)
 
     for term in range(TERMS):
         inverse, norm = scale(0, term)
@@ -127,9 +131,6 @@
         high, low = halves(taps(place - lanes(shape), inverse, norm))
         gzh_ref[term] = high
         gzl_ref[term] = low
-        for offset in range(TAPS):
-            value = jnp.exp(-float(offset * offset) * inverse) * norm * weight_ref[0:1, term : term + 1]
-            cx_ref[term * TAPS + offset] = jnp.broadcast_to(value, (8, 128))
 
         inverse, norm = scale(1, term)
         along_y(my_ref, term, inverse, norm, MY, EMY)
@@ -140,23 +141,25 @@
         high, low = halves(jnp.where(row < MZ + 16, values, 0.0))
         mzh_ref[term] = high
         mzl_ref[term] = low
-        for offset in range(TAPS):
-            value = jnp.exp(-float(offset * offset) * inverse) * norm * weight_ref[1:2, term : term + 1]
-            cx_ref[(TERMS + term) * TAPS + offset] = jnp.broadcast_to(value, (8, 128))
-    for fetch in fetches:
-        fetch.wait()
 
 
 def restrict_kernel(*refs):
     sources, (coarse_ref, mid_ref, up_ref, down_ref), copies = refs[:FETCHED], refs[FETCHED : FETCHED + 4], refs[FETCHED + 4 :]
     copies, half_ref, sems = copies[:FETCHED], copies[FETCHED], copies[FETCHED + 1]
-    fetches = [pltpu.make_async_copy(a, b, sems.at[i]) for i, (a, b) in enumerate(zip(sources, copies))]
-    for fetch in fetches:
-        fetch.start()
+    pieces = [(0, x, 4) for x in range(0, BX, 4)] + [(i, 0, None) for i in range(1, FETCHED - 1)]
+    pieces += [(FETCHED - 1, x, min(x + 9, CX // 2 + 1) - x) for x in range(0, CX // 2 + 1, 9)]
+    fetches = []
+    for count, (i, first, size) in enumerate(pieces):
+        source, copy = sources[i], copies[i]
+        if size:
+            source, copy = source.at[pl.ds(first, size)], copy.at[pl.ds(first, size)]
+        fetches.append(pltpu.make_async_copy(source, copy, sems.at[count]))
+        fetches[-1].start()
     f_ref = copies[0]
-    fetches[0].wait()
     planes = []
     for x in range(MX):
+        if x % 2 == 0:
+            fetches[x // 2].wait()
         total = None
         for plane in (2 * x, 2 * x + 1):
             for odd in (0, 1):
@@ -200,7 +203,7 @@
     down_ref[2 * BY : 2 * BY + MY, :] = falling
     for x in range(4):
         mid_ref[x] = jnp.where(slot < 8, middle[x], roll(middle[x + 4], 64))
-    for fetch in fetches[1:]:
+    for fetch in fetches[4:]:
         fetch.wait()
 
 
@@ -347,6 +350,9 @@
         edge = lambda ref=ref: ref[9 * EY + 4 * EMY : 9 * EY + 5 * EMY, :]
         filter_middle(middle, edge, my_ref[...], mzh_ref, mzl_ref, small_ref, index * MX)
 
+    def tap_at(row):
+        return jnp.broadcast_to(cx_ref[row : row + 1, :], (8, 128))
+
     for tile in range(MY // 8):
         sl = slice(tile * 8, tile * 8 + 8)
         acc = [None] * MX
@@ -361,7 +367,7 @@
                 for x in range(MX):
                     offset = place - x - RADIUS
                     if abs(offset) <= RADIUS:
-                        part = cx_ref[(TERMS + term) * TAPS + abs(offset)] * value
+                        part = tap_at((TERMS + term) * TAPS + abs(offset)) * value
                         acc[x] = part if acc[x] is None else acc[x] + part
         for x in range(MX):
             add_ref[x, pl.ds(tile * 16, 8, stride=2), :] = acc[x]
@@ -381,7 +387,7 @@
                 for x in range(BX):
                     offset = place - x - RADIUS
                     if abs(offset) <= RADIUS:
-                        acc[x] = acc[x] + cx_ref[term * TAPS + abs(offset)] * value
+                        acc[x] = acc[x] + tap_at(term * TAPS + abs(offset)) * value
         for x in range(BX):
             out_ref[x, sl, :] = acc[x]
         return carry
@@ -437,20 +443,19 @@
 
 
 def potential(charges, term_width, term_weight):
-    sources = [charges, term_width, term_weight]
-    coarse, mid, z_up, z_down, charges, term_width, term_weight = call(
+    sources = [charges, term_width, term_weight] + constant_tables()
+    coarse, mid, z_up, z_down, charges, term_width, term_weight, *tables = call(
         restrict_kernel,
         [((GY * GZ, 8, 128), F32), ((4, MY, 128), F32), ((ZROWS, 128), F32), ((ZROWS, 128), F32)]
         + [(a.shape, a.dtype) for a in sources],
         sources,
-        [pltpu.VMEM((MX * MY, 128), F32), pltpu.SemaphoreType.DMA((FETCHED,))],
+        [pltpu.VMEM((MX * MY, 128), F32), pltpu.SemaphoreType.DMA((PIECES,))],
         flops=10**7,
-        hbm=3,
+        hbm=FETCHED,
     )
     slab = exchange(coarse, ("gy", "gz"))
     z_low, z_high = ring(z_up, "gz", 1), ring(z_down, "gz", -1)
-    tables = constant_tables()
-    gy, gzh, gzl, my, mzh, mzl, cx, *tables = call(
+    gy, gzh, gzl, my, mzh, mzl, cx = call(
         weights_kernel,
         [
             ((TERMS * BY, 3 * EY), BF16),
@@ -459,13 +464,10 @@
             ((TERMS * MY, 3 * EMY), BF16),
             ((TERMS, 128, 128), BF16),
             ((TERMS, 128, 128), BF16),
-            ((2 * TERMS * TAPS, 8, 128), F32),
-        ]
-        + [(a.shape, a.dtype) for a in tables],
-        [term_width, term_weight] + tables,
-        [pltpu.SemaphoreType.DMA((TABLES,))],
+            ((2 * TERMS * TAPS, 128), F32),
+        ],
+        [term_width, term_weight],
         flops=10**7,
-        hbm=TABLES,
     )
     bands = [gy, gzh, gzl, my, mzh, mzl]
     halo, y_up, y_down = call(

time: 64.9 us -> 62.4 us (0.961)
  waiting for transfers between devices: 4.42 us -> 9.16 us
  local copies, waits for them, and re-layouts: 4.48 us -> 0 us
  Pallas kernels: 14.1 us -> 11.1 us
    all_to_all x2, waiting for transfers between devices: 2.87 us -> 7.6 us  [exchange(): return lax.all_to_all(value, axis, 0, 0, tiled=True)]
    unnamed x12 -> x0, local copies, waits for them, and re-layouts: 4.48 us -> none
    pallas_call x8, Pallas kernels: 14.1 us -> 11.1 us  [call(): pl.pallas_call(kernel, out_shape=[jax.ShapeDtypeStruct(shape, dtype) for...]
  transfers between devices with their start and end apart: 8 -> 8, of which waited for: 2 -> 3; matrix products, arithmetic and copies ran while one was open for 0% -> 0% of each run, Pallas kernels for 17% -> 13%
where the time goes in v4:
time: 62.4 us; the launch traced here: 62.1 us
  starting transfers between devices  41.7 us (67%)
  Pallas kernels  11.1 us (18%)
  waiting for transfers between devices  9.16 us (15%)
    ppermute x6, starting transfers between devices, ring(): lax.ppermute(value, axis, [(i, (i + step) % count) for i in range(count)])  23.9 us
    all_to_all x2, starting transfers between devices, exchange(): return lax.all_to_all(value, axis, 0, 0, tiled=True)  17.8 us
    pallas_call x8, Pallas kernels, call(): pl.pallas_call(kernel, out_shape=[jax.ShapeDtypeStruct(shape, dtype) for...  11.1 us
    all_to_all x2, waiting for transfers between devices, exchange(): return lax.all_to_all(value, axis, 0, 0, tiled=True)  7.6 us
    ppermute x6, waiting for transfers between devices, ring(): lax.ppermute(value, axis, [(i, (i + step) % count) for i in range(count)])  1.55 us
  transfers between devices with their start and end apart: 8, of which 3 were waited for; matrix products, arithmetic and copies ran while one was open for 0% of the time, Pallas kernels for 13%

profile of v4, /device:TPU:1, one launch (start us, length us, event | category | flops | bytes accessed | tf_op | source)
XLA Modules:
  0.0 62.1 jit_solution(4181674118870171718)
XLA Ops:
  0.0 2.3 %shard_map.82 = (f32[32,8,128]{2,1,0:T(8,128)}, f32[4,16,128]{2,1,0:T(8,128)S(1)}, f32[80,128]{1,0:T(8,128)S(1)}, f32[80,128]{1,0:T(8,128)S(1)}, f32[16,32,128]{...) custom-call(f32[16,32,128]{2,1,0:T(8,128)} %refs_0_.1, ...), custom_call_target="tpu_custom_call" | custom-call | flops 10000000 | bytes 1728576 | tf_op jit(solution)/shard_map/pallas_call | solution.py:425
  2.3 3.9 %collective-permute-start = (f32[80,128]{1,0:T(8,128)S(1)}, f32[80,128]{1,0:T(8,128)S(1)}, u32[]{:S(2)}, u32[]{:S(2)}) collective-permute-start(f32[80,128]{1,0:T(8,128)S(1)} %get-tuple-element.33), channel_id=1, source_target_pairs={{0,1},{1,2},{2,3},{3,0},{4,5},{5,6},{6,7},{7,4},{8,9},{9,10},{10,1... | collective-permute-start | bytes 122888 | tf_op jit(solution)/shard_map/ppermute | solution.py:438
  6.2 3.2 %collective-permute-start.1 = (f32[80,128]{1,0:T(8,128)S(1)}, f32[80,128]{1,0:T(8,128)S(1)}, u32[]{:S(2)}, u32[]{:S(2)}) collective-permute-start(f32[80,128]{1,0:T(8,128)S(1)} %get-tuple-element.34), channel_id=1, source_target_pairs={{0,3},{1,0},{2,1},{3,2},{4,7},{5,4},{6,5},{7,6},{8,11},{9,8},{10,9... | collective-permute-start | bytes 122888 | tf_op jit(solution)/shard_map/ppermute | solution.py:438
  9.4 0.0 collective-permute-done.zlow_ref
  9.4 1.5 %collective-permute-done.1.zhigh_ref = f32[80,128]{1,0:T(8,128)S(1)} collective-permute-done((f32[80,128]{1,0:T(8,128)S(1)}, f32[80,128]{1,0:T(8,128)S(1)}, u32[]{:S(2)}, u32[]{:S(2)}) %collective-permute-start.1) | collective-permute-done | bytes 40992 | tf_op jit(solution)/shard_map/ppermute | solution.py:438
  11.0 4.0 %collective-permute-start.2 = (f32[184,128]{1,0:T(8,128)S(1)}, f32[184,128]{1,0:T(8,128)S(1)}, u32[]{:S(2)}, u32[]{:S(2)}) collective-permute-start(f32[184,128]{1,0:T(8,128)S(1)} %get-tuple-element.36), channel_id=1, source_target_pairs={{0,4},{4,8},{8,12},{12,16},{16,20},{20,24},{24,28},{28,0},{1,5},{5... | collective-permute-start | bytes 282632 | tf_op jit(solution)/shard_map/ppermute | solution.py:438
  15.0 8.6 %collective-permute-start.3 = (f32[184,128]{1,0:T(8,128)S(1)}, f32[184,128]{1,0:T(8,128)S(1)}, u32[]{:S(2)}, u32[]{:S(2)}) collective-permute-start(f32[184,128]{1,0:T(8,128)S(1)} %get-tuple-element.37), channel_id=1, source_target_pairs={{0,28},{4,0},{8,4},{12,8},{16,12},{20,16},{24,20},{28,24},{1,29},{... | collective-permute-start | bytes 282632 | tf_op jit(solution)/shard_map/ppermute | solution.py:438
  23.6 6.7 %all-to-all-start = ((f32[32,8,128]{2,1,0:T(8,128)}), f32[32,8,128]{2,1,0:T(8,128)S(1)}, u32[]{:S(2)}, u32[]{:S(2)}) async-start(f32[32,8,128]{2,1,0:T(8,128)} %get-tuple-element.51), calls=%async_computation | async-start | bytes 262144 | tf_op jit(solution)/shard_map/all_to_all | solution.py:442
  30.3 0.0 collective-permute-done.2.low_ref
  30.3 0.0 collective-permute-done.3.high_ref
  30.4 4.1 %collective-permute-start.4 = (f32[592,128]{1,0:T(8,128)S(1)}, f32[592,128]{1,0:T(8,128)S(1)}, u32[]{:S(2)}, u32[]{:S(2)}) collective-permute-start(f32[592,128]{1,0:T(8,128)S(1)} %get-tuple-element.38), channel_id=1, source_target_pairs={{0,32},{32,64},{64,96},{96,128},{128,160},{160,192},{192,224},{224... | collective-permute-start | bytes 909320 | tf_op jit(solution)/shard_map/ppermute | solution.py:438
  34.5 0.0 collective-permute-start.5
  34.5 5.2 %all-to-all-done.slab_ref = f32[32,8,128]{2,1,0:T(8,128)S(1)} async-done(((f32[32,8,128]{2,1,0:T(8,128)}), f32[32,8,128]{2,1,0:T(8,128)S(1)}, u32[]{:S(2)}, u32[]{:S(2)}) %all-to-all-start) | async-done | bytes 131104 | tf_op jit(solution)/shard_map/all_to_all | solution.py:442
  39.8 2.6 %shard_map.88 = f32[16,8,128]{2,1,0:T(8,128)} custom-call(f32[32,8,128]{2,1,0:T(8,128)S(1)} %all-to-all-done.slab_ref, bf16[64,192]{1,0:T(8,128)(2,1)S(1)} %get-tuple-element.52.cas_y_ref, f32[64,128]{1,0:T(8,128)S(1)} %get-tuple-element.53.twice_y_ref, bf16[2,128,128]{2,1,0:T(8,128)(2,1)S(1)} %get-tuple-element.54.cas_z_ref, ...), custom_call_target="tpu_custom_call" | custom-call | flops 50000000 | bytes 1597440 | tf_op jit(solution)/shard_map/pallas_call | solution.py:425
  42.3 11.1 %all-to-all-start.1 = ((f32[16,8,128]{2,1,0:T(8,128)}), f32[16,8,128]{2,1,0:T(8,128)S(1)}, u32[]{:S(2)}, u32[]{:S(2)}) async-start(f32[16,8,128]{2,1,0:T(8,128)} %shard_map.88), calls=%async_computation.1 | async-start | bytes 131072 | tf_op jit(solution)/shard_map/all_to_all | solution.py:442
  53.4 0.5 shard_map.85
  53.9 1.7 %shard_map.86 = (f32[4,16,32,128]{3,2,1,0:T(8,128)S(1)}, f32[4,8,16,128]{3,2,1,0:T(8,128)S(1)}) custom-call(f32[16,32,128]{2,1,0:T(8,128)S(1)} %get-tuple-element.31.f_ref, f32[4,16,128]{2,1,0:T(8,128)S(1)} %get-tuple-element.32.mid_ref, f32[80,128]{1,0:T(8,128)S(1)} %get-tuple-element.35.halo_ref, f32[184,128]{1,0:T(8,128)S(1)} %collective-permute-done.2.low_ref, ...), custom_call_target="tpu_custom_call" | custom-call | flops 100000000 | bytes 1359872 | tf_op jit(solution)/shard_map/pallas_call | solution.py:425
  55.6 0.0 collective-permute-done.4.low_ref
  55.6 0.0 collective-permute-done.5.high_ref
  55.6 3.2 %shard_map.87.near_ref = f32[16,32,128]{2,1,0:T(8,128)S(1)} custom-call(f32[592,128]{1,0:T(8,128)S(1)} %collective-permute-done.4.low_ref, f32[592,128]{1,0:T(8,128)S(1)} %collective-permute-done.5.high_ref, f32[4,16,32,128]{3,2,1,0:T(8,128)S(1)} %get-tuple-element.48.fine_ref, f32[4,8,16,128]{3,2,1,0:T(8,128)S(1)} %get-tuple-element.49.middle_ref, ...), custom_call_target="tpu_custom_call" | custom-call | flops 100000000 | bytes 2789376 | tf_op jit(solution)/shard_map/pallas_call | solution.py:425
  58.8 2.4 %all-to-all-done.1.top_ref = f32[16,8,128]{2,1,0:T(8,128)S(1)} async-done(((f32[16,8,128]{2,1,0:T(8,128)}), f32[16,8,128]{2,1,0:T(8,128)S(1)}, u32[]{:S(2)}, u32[]{:S(2)}) %all-to-all-start.1) | async-done | bytes 65568 | tf_op jit(solution)/shard_map/all_to_all | solution.py:442
  61.2 0.9 %shard_map.89 = f32[16,32,128]{2,1,0:T(8,128)} custom-call(f32[16,32,128]{2,1,0:T(8,128)S(1)} %shard_map.87.near_ref, f32[16,8,128]{2,1,0:T(8,128)S(1)} %all-to-all-done.1.top_ref), custom_call_target="tpu_custom_call" | custom-call | flops 1000000 | bytes 327680 | tf_op jit(solution)/shard_map/pallas_call | solution.py:425
  (2 shorter events, 0.1 us)
Async XLA Ops:
  2.3 7.1 %collective-permute-start = (f32[80,128]{1,0:T(8,128)S(1)}, f32[80,128]{1,0:T(8,128)S(1)}, u32[]{:S(2)}, u32[]{:S(2)}) collective-permute-start(f32[80,128]{1,0:T(8,128)S(1)} %get-tuple-element.33), channel_id=1, source_target_pairs={{0,1},{1,2},{2,3},{3,0},{4,5},{5,6},{6,7},{7,4},{8,9},{9,10},{10,1... | collective-permute-start | bytes 122888 | tf_op jit(solution)/shard_map/ppermute | solution.py:438
  6.2 4.7 %collective-permute-start.1 = (f32[80,128]{1,0:T(8,128)S(1)}, f32[80,128]{1,0:T(8,128)S(1)}, u32[]{:S(2)}, u32[]{:S(2)}) collective-permute-start(f32[80,128]{1,0:T(8,128)S(1)} %get-tuple-element.34), channel_id=1, source_target_pairs={{0,3},{1,0},{2,1},{3,2},{4,7},{5,4},{6,5},{7,6},{8,11},{9,8},{10,9... | collective-permute-start | bytes 122888 | tf_op jit(solution)/shard_map/ppermute | solution.py:438
  11.0 19.3 %collective-permute-start.2 = (f32[184,128]{1,0:T(8,128)S(1)}, f32[184,128]{1,0:T(8,128)S(1)}, u32[]{:S(2)}, u32[]{:S(2)}) collective-permute-start(f32[184,128]{1,0:T(8,128)S(1)} %get-tuple-element.36), channel_id=1, source_target_pairs={{0,4},{4,8},{8,12},{12,16},{16,20},{20,24},{24,28},{28,0},{1,5},{5... | collective-permute-start | bytes 282632 | tf_op jit(solution)/shard_map/ppermute | solution.py:438
  15.0 15.3 %collective-permute-start.3 = (f32[184,128]{1,0:T(8,128)S(1)}, f32[184,128]{1,0:T(8,128)S(1)}, u32[]{:S(2)}, u32[]{:S(2)}) collective-permute-start(f32[184,128]{1,0:T(8,128)S(1)} %get-tuple-element.37), channel_id=1, source_target_pairs={{0,28},{4,0},{8,4},{12,8},{16,12},{20,16},{24,20},{28,24},{1,29},{... | collective-permute-start | bytes 282632 | tf_op jit(solution)/shard_map/ppermute | solution.py:438
  23.6 16.2 %all-to-all-start = ((f32[32,8,128]{2,1,0:T(8,128)}), f32[32,8,128]{2,1,0:T(8,128)S(1)}, u32[]{:S(2)}, u32[]{:S(2)}) async-start(f32[32,8,128]{2,1,0:T(8,128)} %get-tuple-element.51), calls=%async_computation | async-start | bytes 262144 | tf_op jit(solution)/shard_map/all_to_all | solution.py:442
  30.4 25.2 %collective-permute-start.4 = (f32[592,128]{1,0:T(8,128)S(1)}, f32[592,128]{1,0:T(8,128)S(1)}, u32[]{:S(2)}, u32[]{:S(2)}) collective-permute-start(f32[592,128]{1,0:T(8,128)S(1)} %get-tuple-element.38), channel_id=1, source_target_pairs={{0,32},{32,64},{64,96},{96,128},{128,160},{160,192},{192,224},{224... | collective-permute-start | bytes 909320 | tf_op jit(solution)/shard_map/ppermute | solution.py:438
  34.5 21.1 %collective-permute-start.5 = (f32[592,128]{1,0:T(8,128)S(1)}, f32[592,128]{1,0:T(8,128)S(1)}, u32[]{:S(2)}, u32[]{:S(2)}) collective-permute-start(f32[592,128]{1,0:T(8,128)S(1)} %get-tuple-element.39), channel_id=1, source_target_pairs={{0,480},{32,0},{64,32},{96,64},{128,96},{160,128},{192,160},{224,1... | collective-permute-start | bytes 909320 | tf_op jit(solution)/shard_map/ppermute | solution.py:438
  42.3 18.9 %all-to-all-start.1 = ((f32[16,8,128]{2,1,0:T(8,128)}), f32[16,8,128]{2,1,0:T(8,128)S(1)}, u32[]{:S(2)}, u32[]{:S(2)}) async-start(f32[16,8,128]{2,1,0:T(8,128)} %shard_map.88), calls=%async_computation.1 | async-start | bytes 131072 | tf_op jit(solution)/shard_map/all_to_all | solution.py:442

commit v5 on v4

--- a/solution.py
+++ b/solution.py
@@ -145,7 +145,7 @@
 
 def restrict_kernel(*refs):
     sources, (coarse_ref, mid_ref, up_ref, down_ref), copies = refs[:FETCHED], refs[FETCHED : FETCHED + 4], refs[FETCHED + 4 :]
-    copies, half_ref, sems = copies[:FETCHED], copies[FETCHED], copies[FETCHED + 1]
+    copies, half_ref, many_ref, sems = copies[:FETCHED], *copies[FETCHED:]
     pieces = [(0, x, 4) for x in range(0, BX, 4)] + [(i, 0, None) for i in range(1, FETCHED - 1)]
     pieces += [(FETCHED - 1, x, min(x + 9, CX // 2 + 1) - x) for x in range(0, CX // 2 + 1, 9)]
     fetches = []
@@ -178,7 +178,9 @@
             part = piece if part is None else part + piece
         coarse = jnp.where((lane >> 5) == x, roll(part, x * 32 - 64), coarse)
     for target in range(GY * GZ):
-        coarse_ref[target] = coarse
+        many_ref[target] = coarse
+    send = pltpu.make_async_copy(many_ref, coarse_ref, sems.at[PIECES])
+    send.start()
 
     slot = lanes((BY, 128)) >> 3
     for group in range(2):
@@ -205,6 +207,7 @@
         mid_ref[x] = jnp.where(slot < 8, middle[x], roll(middle[x + 4], 64))
     for fetch in fetches[4:]:
         fetch.wait()
+    send.wait()
 
 
 def modes_kernel(slab_ref, cas_y_ref, twice_y_ref, cas_z_ref, own_z_ref, along_ref, out_ref, modes_ref, wide_ref):
@@ -221,29 +224,28 @@
     high, low = halves(jnp.concatenate(planes, axis=0))
     modes_ref[...] = dot(high, cas_z_ref[0]) + dot(low, cas_z_ref[0]) + dot(high, cas_z_ref[1])
 
-    def tile_step(tile, carry):
-        start = pl.multiple_of(tile * 16, 16)
-        source = [modes_ref[pl.ds(x * CY + start, 16), :] for x in range(4)]
-        table = [along_ref[abs(shift), pl.ds(start, 16), :] for shift in (0, -1, -2, -3)]
-        for place in range(CX):
-            if place:
-                table = [along_ref[min(place, CX - place), pl.ds(start, 16), :]] + table[:3]
-            total = table[0] * source[0]
-            for x in range(1, 4):
-                total = total + table[x] * source[x]
-            high, low = halves(total)
-            wide_ref[pl.ds(start, 16), place * 128 : (place + 1) * 128] = high
-            wide_ref[pl.ds(CY + start, 16), place * 128 : (place + 1) * 128] = low
-        return carry
-
-    lax.fori_loop(0, CY // 16, tile_step, 0)
     own_y = twice_y_ref[pl.ds(pl.multiple_of(lax.axis_index("gy") * 8, 8), 8), :]
     high, low = halves(own_y)
     low = jnp.where(lanes((8, 128)) < CY, low.astype(F32), 0.0)
     own_y = jnp.concatenate([high.astype(F32), low], axis=0).astype(BF16)
-    back_y = dot(own_y, wide_ref[...])
-    back_y = back_y[0:8] + back_y[8:16]
-    high, low = halves(jnp.concatenate([back_y[:, x * 128 : (x + 1) * 128] for x in range(CX)], axis=0))
+    parts = []
+    for first in range(0, CX, 16):
+        for start in range(0, CY, 16):
+            rows = slice(start, start + 16)
+            source = [modes_ref[x * CY + start : x * CY + start + 16, :] for x in range(4)]
+            table = [None] + [along_ref[min(abs(first - x), CX - abs(first - x)), rows, :] for x in (1, 2, 3)]
+            for place in range(first, first + 16):
+                table = [along_ref[min(place, CX - place), rows, :]] + (table[1:] if place == first else table[:3])
+                total = table[0] * source[0]
+                for x in range(1, 4):
+                    total = total + table[x] * source[x]
+                high, low = halves(total)
+                wide_ref[rows, place * 128 : (place + 1) * 128] = high
+                wide_ref[CY + start : CY + start + 16, place * 128 : (place + 1) * 128] = low
+        part = dot(own_y, wide_ref[:, first * 128 : (first + 16) * 128])
+        parts.append(part[0:8] + part[8:16])
+    rows = [part[:, x * 128 : (x + 1) * 128] for part in parts for x in range(16)]
+    high, low = halves(jnp.concatenate(rows, axis=0))
     own_z = own_z_ref.at[lax.axis_index("gz")]
     back_z = dot(high, own_z[0]) + dot(low, own_z[0]) + dot(high, own_z[1])
     me = lax.axis_index("gx")
@@ -395,7 +397,7 @@
     lax.fori_loop(0, BY // 8, tile_step, 0)
 
 
-def add_kernel(near_ref, top_ref, out_ref, wide_ref):
+def add_kernel(near_ref, top_ref, out_ref, wide_ref, sum_ref, sems):
     top = top_ref[0]
     for source in range(1, GX):
         top = top + top_ref[source]
@@ -412,11 +414,18 @@
         wide_ref[pl.ds(BY + row, 8, stride=4), :] = wide[:, 128:256]
         wide_ref[pl.ds(2 * BY + row, 8, stride=4), :] = wide[:, 256:384]
         wide_ref[pl.ds(3 * BY + row, 8, stride=4), :] = wide[:, 384:512]
-    for x in range(BX):
-        out_ref[x] = near_ref[x] + wide_ref[(x // 4) * BY : (x // 4 + 1) * BY, :]
-
-
-def call(kernel, outs, args, scratch=(), flops=0, hbm=0, limit=4):
+    sends = []
+    for block in range(4):
+        for x in range(4 * block, 4 * block + 4):
+            sum_ref[x] = near_ref[x] + wide_ref[block * BY : (block + 1) * BY, :]
+        place = pl.ds(4 * block, 4)
+        sends.append(pltpu.make_async_copy(sum_ref.at[place], out_ref.at[place], sems.at[block]))
+        sends[-1].start()
+    for send in sends:
+        send.wait()
+
+
+def call(kernel, outs, args, scratch=(), flops=0, hbm=0, written=0, limit=4):
     vmem = pl.BlockSpec(memory_space=pltpu.VMEM)
     near = len(args) - hbm
     specs = [vmem] * near + [pl.BlockSpec(memory_space=pltpu.HBM)] * hbm
@@ -426,7 +435,7 @@
         kernel,
         out_shape=[jax.ShapeDtypeStruct(shape, dtype) for shape, dtype in outs],
         in_specs=specs,
-        out_specs=[vmem] * len(outs),
+        out_specs=[pl.BlockSpec(memory_space=pl.ANY)] * written + [vmem] * (len(outs) - written),
         scratch_shapes=list(scratch),
         cost_estimate=pl.CostEstimate(flops=flops, bytes_accessed=size, transcendentals=0),
         compiler_params=pltpu.CompilerParams(vmem_limit_bytes=limit * 1024 * 1024),
@@ -449,9 +458,14 @@
         [((GY * GZ, 8, 128), F32), ((4, MY, 128), F32), ((ZROWS, 128), F32), ((ZROWS, 128), F32)]
         + [(a.shape, a.dtype) for a in sources],
         sources,
-        [pltpu.VMEM((MX * MY, 128), F32), pltpu.SemaphoreType.DMA((PIECES,))],
+        [
+            pltpu.VMEM((MX * MY, 128), F32),
+            pltpu.VMEM((GY * GZ, 8, 128), F32),
+            pltpu.SemaphoreType.DMA((PIECES + 1,)),
+        ],
         flops=10**7,
         hbm=FETCHED,
+        written=1,
     )
     slab = exchange(coarse, ("gy", "gz"))
     z_low, z_high = ring(z_up, "gz", 1), ring(z_down, "gz", -1)
@@ -509,7 +523,14 @@
         flops=10**8,
         limit=10,
     )
-    (result,) = call(add_kernel, [((BX, BY, BZ), F32)], [near, top], [pltpu.VMEM((4 * BY, 128), F32)], flops=10**6)
+    (result,) = call(
+        add_kernel,
+        [((BX, BY, BZ), F32)],
+        [near, top],
+        [pltpu.VMEM((4 * BY, 128), F32), pltpu.VMEM((BX, BY, BZ), F32), pltpu.SemaphoreType.DMA((4,))],
+        flops=10**6,
+        written=1,
+    )
     return result
 
 

time: 62.4 us -> 62.3 us (level)
  no operation moved by 1% of the time
where the time goes in v5:
time: 62.3 us; the launch traced here: 61.9 us
  starting transfers between devices  41.7 us (67%)
  Pallas kernels  11 us (18%)
  waiting for transfers between devices  9.15 us (15%)
    ppermute x6, starting transfers between devices, ring(): lax.ppermute(value, axis, [(i, (i + step) % count) for i in range(count)])  23.9 us
    all_to_all x2, starting transfers between devices, exchange(): return lax.all_to_all(value, axis, 0, 0, tiled=True)  17.8 us
    pallas_call x8, Pallas kernels, call(): pl.pallas_call(kernel, out_shape=[jax.ShapeDtypeStruct(shape, dtype) for...  11 us
    all_to_all x2, waiting for transfers between devices, exchange(): return lax.all_to_all(value, axis, 0, 0, tiled=True)  7.6 us
    ppermute x6, waiting for transfers between devices, ring(): lax.ppermute(value, axis, [(i, (i + step) % count) for i in range(count)])  1.55 us
  transfers between devices with their start and end apart: 8, of which 3 were waited for; matrix products, arithmetic and copies ran while one was open for 0% of the time, Pallas kernels for 13%

profile of v5, /device:TPU:1, one launch (start us, length us, event | category | flops | bytes accessed | tf_op | source)
XLA Modules:
  0.0 61.9 jit_solution(17151416959049597273)
XLA Ops:
  0.0 2.0 %shard_map.82 = (f32[32,8,128]{2,1,0:T(8,128)}, f32[4,16,128]{2,1,0:T(8,128)S(1)}, f32[80,128]{1,0:T(8,128)S(1)}, f32[80,128]{1,0:T(8,128)S(1)}, f32[16,32,128]{...) custom-call(f32[16,32,128]{2,1,0:T(8,128)} %refs_0_.1, ...), custom_call_target="tpu_custom_call" | custom-call | flops 10000000 | bytes 1728576 | tf_op jit(solution)/shard_map/pallas_call | solution.py:434
  2.0 3.9 %collective-permute-start = (f32[80,128]{1,0:T(8,128)S(1)}, f32[80,128]{1,0:T(8,128)S(1)}, u32[]{:S(2)}, u32[]{:S(2)}) collective-permute-start(f32[80,128]{1,0:T(8,128)S(1)} %get-tuple-element.33), channel_id=1, source_target_pairs={{0,1},{1,2},{2,3},{3,0},{4,5},{5,6},{6,7},{7,4},{8,9},{9,10},{10,1... | collective-permute-start | bytes 122888 | tf_op jit(solution)/shard_map/ppermute | solution.py:447
  6.0 3.2 %collective-permute-start.1 = (f32[80,128]{1,0:T(8,128)S(1)}, f32[80,128]{1,0:T(8,128)S(1)}, u32[]{:S(2)}, u32[]{:S(2)}) collective-permute-start(f32[80,128]{1,0:T(8,128)S(1)} %get-tuple-element.34), channel_id=1, source_target_pairs={{0,3},{1,0},{2,1},{3,2},{4,7},{5,4},{6,5},{7,6},{8,11},{9,8},{10,9... | collective-permute-start | bytes 122888 | tf_op jit(solution)/shard_map/ppermute | solution.py:447
  9.2 0.0 collective-permute-done.zlow_ref
  9.2 1.5 %collective-permute-done.1.zhigh_ref = f32[80,128]{1,0:T(8,128)S(1)} collective-permute-done((f32[80,128]{1,0:T(8,128)S(1)}, f32[80,128]{1,0:T(8,128)S(1)}, u32[]{:S(2)}, u32[]{:S(2)}) %collective-permute-start.1) | collective-permute-done | bytes 40992 | tf_op jit(solution)/shard_map/ppermute | solution.py:447
  10.8 4.0 %collective-permute-start.2 = (f32[184,128]{1,0:T(8,128)S(1)}, f32[184,128]{1,0:T(8,128)S(1)}, u32[]{:S(2)}, u32[]{:S(2)}) collective-permute-start(f32[184,128]{1,0:T(8,128)S(1)} %get-tuple-element.36), channel_id=1, source_target_pairs={{0,4},{4,8},{8,12},{12,16},{16,20},{20,24},{24,28},{28,0},{1,5},{5... | collective-permute-start | bytes 282632 | tf_op jit(solution)/shard_map/ppermute | solution.py:447
  14.8 8.6 %collective-permute-start.3 = (f32[184,128]{1,0:T(8,128)S(1)}, f32[184,128]{1,0:T(8,128)S(1)}, u32[]{:S(2)}, u32[]{:S(2)}) collective-permute-start(f32[184,128]{1,0:T(8,128)S(1)} %get-tuple-element.37), channel_id=1, source_target_pairs={{0,28},{4,0},{8,4},{12,8},{16,12},{20,16},{24,20},{28,24},{1,29},{... | collective-permute-start | bytes 282632 | tf_op jit(solution)/shard_map/ppermute | solution.py:447
  23.4 6.7 %all-to-all-start = ((f32[32,8,128]{2,1,0:T(8,128)}), f32[32,8,128]{2,1,0:T(8,128)S(1)}, u32[]{:S(2)}, u32[]{:S(2)}) async-start(f32[32,8,128]{2,1,0:T(8,128)} %get-tuple-element.51), calls=%async_computation | async-start | bytes 262144 | tf_op jit(solution)/shard_map/all_to_all | solution.py:451
  30.1 0.0 collective-permute-done.2.low_ref
  30.1 0.0 collective-permute-done.3.high_ref
  30.1 4.1 %collective-permute-start.4 = (f32[592,128]{1,0:T(8,128)S(1)}, f32[592,128]{1,0:T(8,128)S(1)}, u32[]{:S(2)}, u32[]{:S(2)}) collective-permute-start(f32[592,128]{1,0:T(8,128)S(1)} %get-tuple-element.38), channel_id=1, source_target_pairs={{0,32},{32,64},{64,96},{96,128},{128,160},{160,192},{192,224},{224... | collective-permute-start | bytes 909320 | tf_op jit(solution)/shard_map/ppermute | solution.py:447
  34.3 0.0 collective-permute-start.5
  34.3 5.2 %all-to-all-done.slab_ref = f32[32,8,128]{2,1,0:T(8,128)S(1)} async-done(((f32[32,8,128]{2,1,0:T(8,128)}), f32[32,8,128]{2,1,0:T(8,128)S(1)}, u32[]{:S(2)}, u32[]{:S(2)}) %all-to-all-start) | async-done | bytes 131104 | tf_op jit(solution)/shard_map/all_to_all | solution.py:451
  39.5 2.6 %shard_map.88 = f32[16,8,128]{2,1,0:T(8,128)} custom-call(f32[32,8,128]{2,1,0:T(8,128)S(1)} %all-to-all-done.slab_ref, bf16[64,192]{1,0:T(8,128)(2,1)S(1)} %get-tuple-element.52.cas_y_ref, f32[64,128]{1,0:T(8,128)S(1)} %get-tuple-element.53.twice_y_ref, bf16[2,128,128]{2,1,0:T(8,128)(2,1)S(1)} %get-tuple-element.54.cas_z_ref, ...), custom_call_target="tpu_custom_call" | custom-call | flops 50000000 | bytes 1597440 | tf_op jit(solution)/shard_map/pallas_call | solution.py:434
  42.2 11.1 %all-to-all-start.1 = ((f32[16,8,128]{2,1,0:T(8,128)}), f32[16,8,128]{2,1,0:T(8,128)S(1)}, u32[]{:S(2)}, u32[]{:S(2)}) async-start(f32[16,8,128]{2,1,0:T(8,128)} %shard_map.88), calls=%async_computation.1 | async-start | bytes 131072 | tf_op jit(solution)/shard_map/all_to_all | solution.py:451
  53.3 0.5 shard_map.85
  53.7 1.7 %shard_map.86 = (f32[4,16,32,128]{3,2,1,0:T(8,128)S(1)}, f32[4,8,16,128]{3,2,1,0:T(8,128)S(1)}) custom-call(f32[16,32,128]{2,1,0:T(8,128)S(1)} %get-tuple-element.31.f_ref, f32[4,16,128]{2,1,0:T(8,128)S(1)} %get-tuple-element.32.mid_ref, f32[80,128]{1,0:T(8,128)S(1)} %get-tuple-element.35.halo_ref, f32[184,128]{1,0:T(8,128)S(1)} %collective-permute-done.2.low_ref, ...), custom_call_target="tpu_custom_call" | custom-call | flops 100000000 | bytes 1359872 | tf_op jit(solution)/shard_map/pallas_call | solution.py:434
  55.4 0.0 collective-permute-done.4.low_ref
  55.4 0.0 collective-permute-done.5.high_ref
  55.4 3.2 %shard_map.87.near_ref = f32[16,32,128]{2,1,0:T(8,128)S(1)} custom-call(f32[592,128]{1,0:T(8,128)S(1)} %collective-permute-done.4.low_ref, f32[592,128]{1,0:T(8,128)S(1)} %collective-permute-done.5.high_ref, f32[4,16,32,128]{3,2,1,0:T(8,128)S(1)} %get-tuple-element.48.fine_ref, f32[4,8,16,128]{3,2,1,0:T(8,128)S(1)} %get-tuple-element.49.middle_ref, ...), custom_call_target="tpu_custom_call" | custom-call | flops 100000000 | bytes 2789376 | tf_op jit(solution)/shard_map/pallas_call | solution.py:434
  58.7 2.4 %all-to-all-done.1.top_ref = f32[16,8,128]{2,1,0:T(8,128)S(1)} async-done(((f32[16,8,128]{2,1,0:T(8,128)}), f32[16,8,128]{2,1,0:T(8,128)S(1)}, u32[]{:S(2)}, u32[]{:S(2)}) %all-to-all-start.1) | async-done | bytes 65568 | tf_op jit(solution)/shard_map/all_to_all | solution.py:451
  61.0 0.9 %shard_map.89 = f32[16,32,128]{2,1,0:T(8,128)} custom-call(f32[16,32,128]{2,1,0:T(8,128)S(1)} %shard_map.87.near_ref, f32[16,8,128]{2,1,0:T(8,128)S(1)} %all-to-all-done.1.top_ref), custom_call_target="tpu_custom_call" | custom-call | flops 1000000 | bytes 327680 | tf_op jit(solution)/shard_map/pallas_call | solution.py:434
  (2 shorter events, 0.1 us)
Async XLA Ops:
  2.0 7.1 %collective-permute-start = (f32[80,128]{1,0:T(8,128)S(1)}, f32[80,128]{1,0:T(8,128)S(1)}, u32[]{:S(2)}, u32[]{:S(2)}) collective-permute-start(f32[80,128]{1,0:T(8,128)S(1)} %get-tuple-element.33), channel_id=1, source_target_pairs={{0,1},{1,2},{2,3},{3,0},{4,5},{5,6},{6,7},{7,4},{8,9},{9,10},{10,1... | collective-permute-start | bytes 122888 | tf_op jit(solution)/shard_map/ppermute | solution.py:447
  6.0 4.7 %collective-permute-start.1 = (f32[80,128]{1,0:T(8,128)S(1)}, f32[80,128]{1,0:T(8,128)S(1)}, u32[]{:S(2)}, u32[]{:S(2)}) collective-permute-start(f32[80,128]{1,0:T(8,128)S(1)} %get-tuple-element.34), channel_id=1, source_target_pairs={{0,3},{1,0},{2,1},{3,2},{4,7},{5,4},{6,5},{7,6},{8,11},{9,8},{10,9... | collective-permute-start | bytes 122888 | tf_op jit(solution)/shard_map/ppermute | solution.py:447
  10.8 19.3 %collective-permute-start.2 = (f32[184,128]{1,0:T(8,128)S(1)}, f32[184,128]{1,0:T(8,128)S(1)}, u32[]{:S(2)}, u32[]{:S(2)}) collective-permute-start(f32[184,128]{1,0:T(8,128)S(1)} %get-tuple-element.36), channel_id=1, source_target_pairs={{0,4},{4,8},{8,12},{12,16},{16,20},{20,24},{24,28},{28,0},{1,5},{5... | collective-permute-start | bytes 282632 | tf_op jit(solution)/shard_map/ppermute | solution.py:447
  14.8 15.3 %collective-permute-start.3 = (f32[184,128]{1,0:T(8,128)S(1)}, f32[184,128]{1,0:T(8,128)S(1)}, u32[]{:S(2)}, u32[]{:S(2)}) collective-permute-start(f32[184,128]{1,0:T(8,128)S(1)} %get-tuple-element.37), channel_id=1, source_target_pairs={{0,28},{4,0},{8,4},{12,8},{16,12},{20,16},{24,20},{28,24},{1,29},{... | collective-permute-start | bytes 282632 | tf_op jit(solution)/shard_map/ppermute | solution.py:447
  23.4 16.2 %all-to-all-start = ((f32[32,8,128]{2,1,0:T(8,128)}), f32[32,8,128]{2,1,0:T(8,128)S(1)}, u32[]{:S(2)}, u32[]{:S(2)}) async-start(f32[32,8,128]{2,1,0:T(8,128)} %get-tuple-element.51), calls=%async_computation | async-start | bytes 262144 | tf_op jit(solution)/shard_map/all_to_all | solution.py:451
  30.1 25.3 %collective-permute-start.4 = (f32[592,128]{1,0:T(8,128)S(1)}, f32[592,128]{1,0:T(8,128)S(1)}, u32[]{:S(2)}, u32[]{:S(2)}) collective-permute-start(f32[592,128]{1,0:T(8,128)S(1)} %get-tuple-element.38), channel_id=1, source_target_pairs={{0,32},{32,64},{64,96},{96,128},{128,160},{160,192},{192,224},{224... | collective-permute-start | bytes 909320 | tf_op jit(solution)/shard_map/ppermute | solution.py:447
  34.3 21.2 %collective-permute-start.5 = (f32[592,128]{1,0:T(8,128)S(1)}, f32[592,128]{1,0:T(8,128)S(1)}, u32[]{:S(2)}, u32[]{:S(2)}) collective-permute-start(f32[592,128]{1,0:T(8,128)S(1)} %get-tuple-element.39), channel_id=1, source_target_pairs={{0,480},{32,0},{64,32},{96,64},{128,96},{160,128},{192,160},{224,1... | collective-permute-start | bytes 909320 | tf_op jit(solution)/shard_map/ppermute | solution.py:447
  42.2 18.9 %all-to-all-start.1 = ((f32[16,8,128]{2,1,0:T(8,128)}), f32[16,8,128]{2,1,0:T(8,128)S(1)}, u32[]{:S(2)}, u32[]{:S(2)}) async-start(f32[16,8,128]{2,1,0:T(8,128)} %shard_map.88), calls=%async_computation.1 | async-start | bytes 131072 | tf_op jit(solution)/shard_map/all_to_all | solution.py:451

commit v6 on v5

--- a/solution.py
+++ b/solution.py
@@ -48,7 +48,8 @@
     shifts = np.arange(CX // 2 + 1)
     cosine = np.cos(2.0 * math.pi / CX * (np.outer(shifts, np.arange(CX)) % CX))
     along_x = np.einsum("dm,myz->dyz", cosine, mult) / (CX * CY * CZ)
-    own_z = np.stack([np.tile(cas_z[:, 32 * g : 32 * g + 32], (1, 4)) for g in range(GZ)])
+    own_z = np.stack([np.tile(cas_z[32 * g : 32 * g + 32], (4, 1)) for g in range(GZ)])
+    own_y = np.stack([cas_y[:, 8 * g : 8 * g + 8] for g in range(GY)])
 
     def split(table):
         table = np.asarray(table, np.float32)
@@ -56,9 +57,10 @@
         return high, (table - high.astype(np.float32)).astype(BF16)
 
     high, low = split(cas_y)
+    own_high, own_low = split(own_y)
     tables = [
         np.concatenate([high, high, low], axis=1),
-        np.asarray(np.concatenate([cas_y, cas_y], axis=1), np.float32),
+        np.concatenate([own_high, own_high, own_low, np.zeros_like(own_low)], axis=2),
         np.stack(split(cas_z)),
         np.stack(split(own_z), axis=1),
         np.asarray(along_x, np.float32),
@@ -177,7 +179,7 @@
             piece = half_ref[pl.ds(row, 8, stride=2), :]
             part = piece if part is None else part + piece
         coarse = jnp.where((lane >> 5) == x, roll(part, x * 32 - 64), coarse)
-    for target in range(GY * GZ):
+    for target in range(GX):
         many_ref[target] = coarse
     send = pltpu.make_async_copy(many_ref, coarse_ref, sems.at[PIECES])
     send.start()
@@ -210,51 +212,46 @@
     send.wait()
 
 
-def modes_kernel(slab_ref, cas_y_ref, twice_y_ref, cas_z_ref, own_z_ref, along_ref, out_ref, modes_ref, wide_ref):
-    rows = [jnp.concatenate([slab_ref[gy * GZ + gz] for gz in range(GZ)], axis=1) for gy in range(GY)]
-    high, low = halves(jnp.concatenate(rows, axis=0))
-    by_y = dot(cas_y_ref[...], jnp.concatenate([high, low, high], axis=0))
+def modes_kernel(columns_ref, cas_y_ref, own_y_ref, cas_z_ref, own_z_ref, along_ref, out_ref, modes_ref):
+    me = lax.axis_index("gx")
+    rows = jnp.concatenate([columns_ref[lax.rem(me + block, GX)] for block in range(GX)], axis=0)
+    lane = lanes((GX * 8, 128)) >> 5
+    high, low = halves(jnp.concatenate([jnp.where(lane == x, rows, 0.0) for x in range(4)], axis=0))
+    own_z = own_z_ref.at[lax.axis_index("gz")]
+    by_z = dot(high, own_z[0]) + dot(low, own_z[0]) + dot(high, own_z[1])
+    ordered = [by_z[(x * GX + block) * 8 : (x * GX + block + 1) * 8] for block in range(GX) for x in range(4)]
+    own_y = own_y_ref[lax.axis_index("gy")]
+    for first in range(0, CX, 16):
+        data = jnp.concatenate(ordered[first : first + 16], axis=1)
+        high = data.astype(BF16).astype(F32)
+        stacked = jnp.concatenate([high, data - high, high, jnp.zeros_like(high)], axis=0).astype(BF16)
+        modes_ref[:, first * 128 : (first + 16) * 128] = dot(own_y, stacked)
+
+    outs = [[] for _ in range(4)]
+    for start in range(0, CY, 8):
+        rows = slice(start, start + 8)
+        total = [None] * 4
+        table = [along_ref[shift, rows, :] for shift in (0, 1, 2, 3)]
+        for place in range(CX):
+            if place:
+                table = [along_ref[min(place, CX - place), rows, :]] + table[:3]
+            value = modes_ref[rows, place * 128 : (place + 1) * 128]
+            for x in range(4):
+                part = table[x] * value
+                total[x] = part if total[x] is None else total[x] + part
+        for x in range(4):
+            outs[x].append(total[x])
+    high, low = halves(jnp.concatenate([tile for x in range(4) for tile in outs[x]], axis=0))
+    back_z = dot(high, cas_z_ref[0]) + dot(low, cas_z_ref[0]) + dot(high, cas_z_ref[1])
+    high, low = halves(jnp.concatenate([back_z[x * CY : (x + 1) * CY] for x in range(4)], axis=1))
+    back_y = dot(cas_y_ref[...], jnp.concatenate([high, low, high], axis=0))
     lane = lanes((CY, 128)) >> 5
-    planes = []
-    for x in range(4):
-        plane = jnp.zeros((CY, 128), F32)
-        for gz in range(GZ):
-            plane = jnp.where(lane == gz, roll(by_y[:, gz * 128 : (gz + 1) * 128], (gz - x) * 32), plane)
-        planes.append(plane)
-    high, low = halves(jnp.concatenate(planes, axis=0))
-    modes_ref[...] = dot(high, cas_z_ref[0]) + dot(low, cas_z_ref[0]) + dot(high, cas_z_ref[1])
-
-    own_y = twice_y_ref[pl.ds(pl.multiple_of(lax.axis_index("gy") * 8, 8), 8), :]
-    high, low = halves(own_y)
-    low = jnp.where(lanes((8, 128)) < CY, low.astype(F32), 0.0)
-    own_y = jnp.concatenate([high.astype(F32), low], axis=0).astype(BF16)
-    parts = []
-    for first in range(0, CX, 16):
-        for start in range(0, CY, 16):
-            rows = slice(start, start + 16)
-            source = [modes_ref[x * CY + start : x * CY + start + 16, :] for x in range(4)]
-            table = [None] + [along_ref[min(abs(first - x), CX - abs(first - x)), rows, :] for x in (1, 2, 3)]
-            for place in range(first, first + 16):
-                table = [along_ref[min(place, CX - place), rows, :]] + (table[1:] if place == first else table[:3])
-                total = table[0] * source[0]
-                for x in range(1, 4):
-                    total = total + table[x] * source[x]
-                high, low = halves(total)
-                wide_ref[rows, place * 128 : (place + 1) * 128] = high
-                wide_ref[CY + start : CY + start + 16, place * 128 : (place + 1) * 128] = low
-        part = dot(own_y, wide_ref[:, first * 128 : (first + 16) * 128])
-        parts.append(part[0:8] + part[8:16])
-    rows = [part[:, x * 128 : (x + 1) * 128] for part in parts for x in range(16)]
-    high, low = halves(jnp.concatenate(rows, axis=0))
-    own_z = own_z_ref.at[lax.axis_index("gz")]
-    back_z = dot(high, own_z[0]) + dot(low, own_z[0]) + dot(high, own_z[1])
-    me = lax.axis_index("gx")
-    lane = lanes((8, 128)) >> 5
-    for block in range(GX):
-        result = back_z[block * 32 : block * 32 + 8]
-        for x in range(1, 4):
-            result = jnp.where(lane == x, back_z[block * 32 + x * 8 : block * 32 + (x + 1) * 8], result)
-        out_ref[lax.rem(me + block, GX)] = result
+    for gz in range(GZ):
+        result = jnp.zeros((CY, 128), F32)
+        for x in range(4):
+            result = jnp.where(lane == x, roll(back_y[:, x * 128 : (x + 1) * 128], (x - gz) * 32), result)
+        for gy in range(GY):
+            out_ref[gy * GZ + gz] = result[gy * 8 : gy * 8 + 8]
 
 
 def y_message_kernel(f_ref, mid_ref, zlow_ref, zhigh_ref, halo_ref, up_ref, down_ref):
@@ -399,7 +396,7 @@
 
 def add_kernel(near_ref, top_ref, out_ref, wide_ref, sum_ref, sems):
     top = top_ref[0]
-    for source in range(1, GX):
+    for source in range(1, GY * GZ):
         top = top + top_ref[source]
     shape = (BZ, 4 * BZ)
     row, column = lax.broadcasted_iota(jnp.int32, shape, 0), lanes(shape)
@@ -455,19 +452,19 @@
     sources = [charges, term_width, term_weight] + constant_tables()
     coarse, mid, z_up, z_down, charges, term_width, term_weight, *tables = call(
         restrict_kernel,
-        [((GY * GZ, 8, 128), F32), ((4, MY, 128), F32), ((ZROWS, 128), F32), ((ZROWS, 128), F32)]
+        [((GX, 8, 128), F32), ((4, MY, 128), F32), ((ZROWS, 128), F32), ((ZROWS, 128), F32)]
         + [(a.shape, a.dtype) for a in sources],
         sources,
         [
             pltpu.VMEM((MX * MY, 128), F32),
-            pltpu.VMEM((GY * GZ, 8, 128), F32),
+            pltpu.VMEM((GX, 8, 128), F32),
             pltpu.SemaphoreType.DMA((PIECES + 1,)),
         ],
         flops=10**7,
         hbm=FETCHED,
         written=1,
     )
-    slab = exchange(coarse, ("gy", "gz"))
+    columns = exchange(coarse, "gx")
     z_low, z_high = ring(z_up, "gz", 1), ring(z_down, "gz", -1)
     gy, gzh, gzl, my, mzh, mzl, cx = call(
         weights_kernel,
@@ -493,13 +490,13 @@
     low, high = ring(y_up, "gy", 1), ring(y_down, "gy", -1)
     (partial,) = call(
         modes_kernel,
-        [((GX, 8, 128), F32)],
-        [slab] + tables,
-        [pltpu.VMEM((4 * CY, 128), F32), pltpu.VMEM((2 * CY, CX * 128), BF16)],
+        [((GY * GZ, 8, 128), F32)],
+        [columns] + tables,
+        [pltpu.VMEM((CY, CX * 128), F32)],
         flops=5 * 10**7,
         limit=8,
     )
-    top = exchange(partial, "gx")
+    top = exchange(partial, ("gy", "gz"))
     x_up, x_down = call(
         x_message_kernel, [((XROWS, 128), F32), ((XROWS, 128), F32)], [charges, mid, halo, low, high], flops=10**6
     )

time: 62.3 us -> 61 us (0.979)
  starting transfers between devices: 41.7 us -> 37.8 us
  waiting for transfers between devices: 9.15 us -> 12.2 us
    all_to_all x2, waiting for transfers between devices: 7.6 us -> 10.7 us  [exchange(): return lax.all_to_all(value, axis, 0, 0, tiled=True)]
    ppermute x6, starting transfers between devices: 23.9 us -> 21.4 us  [ring(): lax.ppermute(value, axis, [(i, (i + step) % count) for i in range(count)])]
    all_to_all x2, starting transfers between devices: 17.8 us -> 16.5 us  [exchange(): return lax.all_to_all(value, axis, 0, 0, tiled=True)]
where the time goes in v6:
time: 61 us; the launch traced here: 60.7 us
  starting transfers between devices  37.8 us (62%)
  waiting for transfers between devices  12.2 us (20%)
  Pallas kernels  10.5 us (17%)
    ppermute x6, starting transfers between devices, ring(): lax.ppermute(value, axis, [(i, (i + step) % count) for i in range(count)])  21.4 us
    all_to_all x2, starting transfers between devices, exchange(): return lax.all_to_all(value, axis, 0, 0, tiled=True)  16.5 us
    all_to_all x2, waiting for transfers between devices, exchange(): return lax.all_to_all(value, axis, 0, 0, tiled=True)  10.7 us
    pallas_call x8, Pallas kernels, call(): pl.pallas_call(kernel, out_shape=[jax.ShapeDtypeStruct(shape, dtype) for...  10.5 us
    ppermute x6, waiting for transfers between devices, ring(): lax.ppermute(value, axis, [(i, (i + step) % count) for i in range(count)])  1.55 us
  transfers between devices with their start and end apart: 8, of which 3 were waited for; matrix products, arithmetic and copies ran while one was open for 0% of the time, Pallas kernels for 13%

profile of v6, /device:TPU:1, one launch (start us, length us, event | category | flops | bytes accessed | tf_op | source)
XLA Modules:
  0.0 60.7 jit_solution(13592713831532082098)
XLA Ops:
  0.0 2.0 %shard_map.82 = (f32[16,8,128]{2,1,0:T(8,128)}, f32[4,16,128]{2,1,0:T(8,128)S(1)}, f32[80,128]{1,0:T(8,128)S(1)}, f32[80,128]{1,0:T(8,128)S(1)}, f32[16,32,128]{...) custom-call(f32[16,32,128]{2,1,0:T(8,128)} %refs_0_.1, ...), custom_call_target="tpu_custom_call" | custom-call | flops 10000000 | bytes 1728576 | tf_op jit(solution)/shard_map/pallas_call | solution.py:431
  2.0 3.9 %collective-permute-start = (f32[80,128]{1,0:T(8,128)S(1)}, f32[80,128]{1,0:T(8,128)S(1)}, u32[]{:S(2)}, u32[]{:S(2)}) collective-permute-start(f32[80,128]{1,0:T(8,128)S(1)} %get-tuple-element.33), channel_id=1, source_target_pairs={{0,1},{1,2},{2,3},{3,0},{4,5},{5,6},{6,7},{7,4},{8,9},{9,10},{10,1... | collective-permute-start | bytes 122888 | tf_op jit(solution)/shard_map/ppermute | solution.py:444
  6.0 3.2 %collective-permute-start.1 = (f32[80,128]{1,0:T(8,128)S(1)}, f32[80,128]{1,0:T(8,128)S(1)}, u32[]{:S(2)}, u32[]{:S(2)}) collective-permute-start(f32[80,128]{1,0:T(8,128)S(1)} %get-tuple-element.34), channel_id=1, source_target_pairs={{0,3},{1,0},{2,1},{3,2},{4,7},{5,4},{6,5},{7,6},{8,11},{9,8},{10,9... | collective-permute-start | bytes 122888 | tf_op jit(solution)/shard_map/ppermute | solution.py:444
  9.2 0.0 collective-permute-done.zlow_ref
  9.2 1.5 %collective-permute-done.1.zhigh_ref = f32[80,128]{1,0:T(8,128)S(1)} collective-permute-done((f32[80,128]{1,0:T(8,128)S(1)}, f32[80,128]{1,0:T(8,128)S(1)}, u32[]{:S(2)}, u32[]{:S(2)}) %collective-permute-start.1) | collective-permute-done | bytes 40992 | tf_op jit(solution)/shard_map/ppermute | solution.py:444
  10.7 4.0 %collective-permute-start.2 = (f32[184,128]{1,0:T(8,128)S(1)}, f32[184,128]{1,0:T(8,128)S(1)}, u32[]{:S(2)}, u32[]{:S(2)}) collective-permute-start(f32[184,128]{1,0:T(8,128)S(1)} %get-tuple-element.36), channel_id=1, source_target_pairs={{0,4},{4,8},{8,12},{12,16},{16,20},{20,24},{24,28},{28,0},{1,5},{5... | collective-permute-start | bytes 282632 | tf_op jit(solution)/shard_map/ppermute | solution.py:444
  14.7 8.6 %collective-permute-start.3 = (f32[184,128]{1,0:T(8,128)S(1)}, f32[184,128]{1,0:T(8,128)S(1)}, u32[]{:S(2)}, u32[]{:S(2)}) collective-permute-start(f32[184,128]{1,0:T(8,128)S(1)} %get-tuple-element.37), channel_id=1, source_target_pairs={{0,28},{4,0},{8,4},{12,8},{16,12},{20,16},{24,20},{28,24},{1,29},{... | collective-permute-start | bytes 282632 | tf_op jit(solution)/shard_map/ppermute | solution.py:444
  23.3 9.5 %all-to-all-start = ((f32[16,8,128]{2,1,0:T(8,128)}), f32[16,8,128]{2,1,0:T(8,128)S(1)}, u32[]{:S(2)}, u32[]{:S(2)}) async-start(f32[16,8,128]{2,1,0:T(8,128)} %get-tuple-element.51), calls=%async_computation | async-start | bytes 131072 | tf_op jit(solution)/shard_map/all_to_all | solution.py:448
  32.8 0.0 collective-permute-done.2.low_ref
  32.8 0.0 collective-permute-done.3.high_ref
  32.9 1.6 %collective-permute-start.4 = (f32[592,128]{1,0:T(8,128)S(1)}, f32[592,128]{1,0:T(8,128)S(1)}, u32[]{:S(2)}, u32[]{:S(2)}) collective-permute-start(f32[592,128]{1,0:T(8,128)S(1)} %get-tuple-element.38), channel_id=1, source_target_pairs={{0,32},{32,64},{64,96},{96,128},{128,160},{160,192},{192,224},{224... | collective-permute-start | bytes 909320 | tf_op jit(solution)/shard_map/ppermute | solution.py:444
  34.6 0.0 collective-permute-start.5
  34.6 6.3 %all-to-all-done.columns_ref = f32[16,8,128]{2,1,0:T(8,128)S(1)} async-done(((f32[16,8,128]{2,1,0:T(8,128)}), f32[16,8,128]{2,1,0:T(8,128)S(1)}, u32[]{:S(2)}, u32[]{:S(2)}) %all-to-all-start) | async-done | bytes 65568 | tf_op jit(solution)/shard_map/all_to_all | solution.py:448
  40.9 2.2 %shard_map.88 = f32[32,8,128]{2,1,0:T(8,128)} custom-call(f32[16,8,128]{2,1,0:T(8,128)S(1)} %all-to-all-done.columns_ref, bf16[64,192]{1,0:T(8,128)(2,1)S(1)} %get-tuple-element.52.cas_y_ref, bf16[8,64,32]{2,1,0:T(8,128)(2,1)S(1)} %get-tuple-element.53.own_y_ref, bf16[2,128,128]{2,1,0:T(8,128)(2,1)S(1)} %get-tuple-element.54.cas_z_ref, ...), custom_call_target="tpu_custom_call" | custom-call | flops 50000000 | bytes 1531904 | tf_op jit(solution)/shard_map/pallas_call | solution.py:431
  43.1 7.0 %all-to-all-start.1 = ((f32[32,8,128]{2,1,0:T(8,128)}), f32[32,8,128]{2,1,0:T(8,128)S(1)}, u32[]{:S(2)}, u32[]{:S(2)}) async-start(f32[32,8,128]{2,1,0:T(8,128)} %shard_map.88), calls=%async_computation.1 | async-start | bytes 262144 | tf_op jit(solution)/shard_map/all_to_all | solution.py:448
  50.0 0.5 shard_map.85
  50.5 1.7 %shard_map.86 = (f32[4,16,32,128]{3,2,1,0:T(8,128)S(1)}, f32[4,8,16,128]{3,2,1,0:T(8,128)S(1)}) custom-call(f32[16,32,128]{2,1,0:T(8,128)S(1)} %get-tuple-element.31.f_ref, f32[4,16,128]{2,1,0:T(8,128)S(1)} %get-tuple-element.32.mid_ref, f32[80,128]{1,0:T(8,128)S(1)} %get-tuple-element.35.halo_ref, f32[184,128]{1,0:T(8,128)S(1)} %collective-permute-done.2.low_ref, ...), custom_call_target="tpu_custom_call" | custom-call | flops 100000000 | bytes 1359872 | tf_op jit(solution)/shard_map/pallas_call | solution.py:431
  52.2 0.0 collective-permute-done.4.low_ref
  52.2 0.0 collective-permute-done.5.high_ref
  52.2 3.2 %shard_map.87.near_ref = f32[16,32,128]{2,1,0:T(8,128)S(1)} custom-call(f32[592,128]{1,0:T(8,128)S(1)} %collective-permute-done.4.low_ref, f32[592,128]{1,0:T(8,128)S(1)} %collective-permute-done.5.high_ref, f32[4,16,32,128]{3,2,1,0:T(8,128)S(1)} %get-tuple-element.48.fine_ref, f32[4,8,16,128]{3,2,1,0:T(8,128)S(1)} %get-tuple-element.49.middle_ref, ...), custom_call_target="tpu_custom_call" | custom-call | flops 100000000 | bytes 2789376 | tf_op jit(solution)/shard_map/pallas_call | solution.py:431
  55.4 4.3 %all-to-all-done.1.top_ref = f32[32,8,128]{2,1,0:T(8,128)S(1)} async-done(((f32[32,8,128]{2,1,0:T(8,128)}), f32[32,8,128]{2,1,0:T(8,128)S(1)}, u32[]{:S(2)}, u32[]{:S(2)}) %all-to-all-start.1) | async-done | bytes 131104 | tf_op jit(solution)/shard_map/all_to_all | solution.py:448
  59.8 0.9 %shard_map.89 = f32[16,32,128]{2,1,0:T(8,128)} custom-call(f32[16,32,128]{2,1,0:T(8,128)S(1)} %shard_map.87.near_ref, f32[32,8,128]{2,1,0:T(8,128)S(1)} %all-to-all-done.1.top_ref), custom_call_target="tpu_custom_call" | custom-call | flops 1000000 | bytes 393216 | tf_op jit(solution)/shard_map/pallas_call | solution.py:431
  (2 shorter events, 0.1 us)
Async XLA Ops:
  2.0 7.1 %collective-permute-start = (f32[80,128]{1,0:T(8,128)S(1)}, f32[80,128]{1,0:T(8,128)S(1)}, u32[]{:S(2)}, u32[]{:S(2)}) collective-permute-start(f32[80,128]{1,0:T(8,128)S(1)} %get-tuple-element.33), channel_id=1, source_target_pairs={{0,1},{1,2},{2,3},{3,0},{4,5},{5,6},{6,7},{7,4},{8,9},{9,10},{10,1... | collective-permute-start | bytes 122888 | tf_op jit(solution)/shard_map/ppermute | solution.py:444
  6.0 4.7 %collective-permute-start.1 = (f32[80,128]{1,0:T(8,128)S(1)}, f32[80,128]{1,0:T(8,128)S(1)}, u32[]{:S(2)}, u32[]{:S(2)}) collective-permute-start(f32[80,128]{1,0:T(8,128)S(1)} %get-tuple-element.34), channel_id=1, source_target_pairs={{0,3},{1,0},{2,1},{3,2},{4,7},{5,4},{6,5},{7,6},{8,11},{9,8},{10,9... | collective-permute-start | bytes 122888 | tf_op jit(solution)/shard_map/ppermute | solution.py:444
  10.7 22.1 %collective-permute-start.2 = (f32[184,128]{1,0:T(8,128)S(1)}, f32[184,128]{1,0:T(8,128)S(1)}, u32[]{:S(2)}, u32[]{:S(2)}) collective-permute-start(f32[184,128]{1,0:T(8,128)S(1)} %get-tuple-element.36), channel_id=1, source_target_pairs={{0,4},{4,8},{8,12},{12,16},{16,20},{20,24},{24,28},{28,0},{1,5},{5... | collective-permute-start | bytes 282632 | tf_op jit(solution)/shard_map/ppermute | solution.py:444
  14.7 18.1 %collective-permute-start.3 = (f32[184,128]{1,0:T(8,128)S(1)}, f32[184,128]{1,0:T(8,128)S(1)}, u32[]{:S(2)}, u32[]{:S(2)}) collective-permute-start(f32[184,128]{1,0:T(8,128)S(1)} %get-tuple-element.37), channel_id=1, source_target_pairs={{0,28},{4,0},{8,4},{12,8},{16,12},{20,16},{24,20},{28,24},{1,29},{... | collective-permute-start | bytes 282632 | tf_op jit(solution)/shard_map/ppermute | solution.py:444
  23.3 17.6 %all-to-all-start = ((f32[16,8,128]{2,1,0:T(8,128)}), f32[16,8,128]{2,1,0:T(8,128)S(1)}, u32[]{:S(2)}, u32[]{:S(2)}) async-start(f32[16,8,128]{2,1,0:T(8,128)} %get-tuple-element.51), calls=%async_computation | async-start | bytes 131072 | tf_op jit(solution)/shard_map/all_to_all | solution.py:448
  32.9 19.3 %collective-permute-start.4 = (f32[592,128]{1,0:T(8,128)S(1)}, f32[592,128]{1,0:T(8,128)S(1)}, u32[]{:S(2)}, u32[]{:S(2)}) collective-permute-start(f32[592,128]{1,0:T(8,128)S(1)} %get-tuple-element.38), channel_id=1, source_target_pairs={{0,32},{32,64},{64,96},{96,128},{128,160},{160,192},{192,224},{224... | collective-permute-start | bytes 909320 | tf_op jit(solution)/shard_map/ppermute | solution.py:444
  34.6 17.7 %collective-permute-start.5 = (f32[592,128]{1,0:T(8,128)S(1)}, f32[592,128]{1,0:T(8,128)S(1)}, u32[]{:S(2)}, u32[]{:S(2)}) collective-permute-start(f32[592,128]{1,0:T(8,128)S(1)} %get-tuple-element.39), channel_id=1, source_target_pairs={{0,480},{32,0},{64,32},{96,64},{128,96},{160,128},{192,160},{224,1... | collective-permute-start | bytes 909320 | tf_op jit(solution)/shard_map/ppermute | solution.py:444
  43.1 16.7 %all-to-all-start.1 = ((f32[32,8,128]{2,1,0:T(8,128)}), f32[32,8,128]{2,1,0:T(8,128)S(1)}, u32[]{:S(2)}, u32[]{:S(2)}) async-start(f32[32,8,128]{2,1,0:T(8,128)} %shard_map.88), calls=%async_computation.1 | async-start | bytes 262144 | tf_op jit(solution)/shard_map/all_to_all | solution.py:448

commit v7 on v6

--- a/solution.py
+++ b/solution.py
@@ -327,12 +327,45 @@
             out_ref[term, place + x] = result[x * MY : (x + 1) * MY]
 
 
+def tap_rows(cx_ref):
+    return lambda row: jnp.broadcast_to(cx_ref[row : row + 1, :], (8, 128))
+
+
+def along_x(acc, tap_at, level, places, load):
+    for term in range(TERMS):
+        for index, place in places:
+            value = load(term, index)
+            for x in range(len(acc)):
+                if abs(place - x) <= RADIUS:
+                    part = tap_at((level * TERMS + term) * TAPS + abs(place - x)) * value
+                    acc[x] = part if acc[x] is None else acc[x] + part
+    return acc
+
+
 def own_kernel(
-    f_ref, mid_ref, halo_ref, low_ref, high_ref, gy_ref, gzh_ref, gzl_ref, my_ref, mzh_ref, mzl_ref, fine_ref, middle_ref
+    f_ref, mid_ref, halo_ref, low_ref, high_ref, gy_ref, gzh_ref, gzl_ref, my_ref, mzh_ref, mzl_ref, cx_ref,
+    fine_ref, middle_ref, planes_ref, small_ref,
 ):
     planes, sides, middle, edge = own_extended(f_ref, mid_ref, halo_ref, low_ref, high_ref)
-    filter_yz(planes, sides, gy_ref[...], gzh_ref, gzl_ref, fine_ref, list(range(BX)))
-    filter_middle(middle, edge, my_ref[...], mzh_ref, mzl_ref, middle_ref, 0)
+    filter_yz(planes, sides, gy_ref[...], gzh_ref, gzl_ref, planes_ref, list(range(BX)))
+    filter_middle(middle, edge, my_ref[...], mzh_ref, mzl_ref, small_ref, 0)
+    tap_at = tap_rows(cx_ref)
+    for tile in range(MY // 8):
+        sl = slice(tile * 8, tile * 8 + 8)
+        places = [(x, x) for x in range(MX)]
+        acc = along_x([None] * MX, tap_at, 1, places, lambda term, i, sl=sl: small_ref[term, i, sl, :])
+        for x in range(MX):
+            middle_ref[x, sl, :] = acc[x]
+
+    def tile_step(tile, carry):
+        sl = pl.ds(pl.multiple_of(tile * 8, 8), 8)
+        places = [(x, x) for x in range(BX)]
+        acc = along_x([None] * BX, tap_at, 0, places, lambda term, i: planes_ref[term, i, sl, :])
+        for x in range(BX):
+            fine_ref[x, sl, :] = acc[x]
+        return carry
+
+    lax.fori_loop(0, BY // 8, tile_step, 0)
 
 
 def near_kernel(
@@ -349,44 +382,21 @@
         edge = lambda ref=ref: ref[9 * EY + 4 * EMY : 9 * EY + 5 * EMY, :]
         filter_middle(middle, edge, my_ref[...], mzh_ref, mzl_ref, small_ref, index * MX)
 
-    def tap_at(row):
-        return jnp.broadcast_to(cx_ref[row : row + 1, :], (8, 128))
-
+    tap_at = tap_rows(cx_ref)
     for tile in range(MY // 8):
         sl = slice(tile * 8, tile * 8 + 8)
-        acc = [None] * MX
-        for term in range(TERMS):
-            for place in range(3 * MX):
-                if place < MX:
-                    value = small_ref[term, place, sl, :]
-                elif place < 2 * MX:
-                    value = middle_ref[term, place - MX, sl, :]
-                else:
-                    value = small_ref[term, place - MX, sl, :]
-                for x in range(MX):
-                    offset = place - x - RADIUS
-                    if abs(offset) <= RADIUS:
-                        part = tap_at((TERMS + term) * TAPS + abs(offset)) * value
-                        acc[x] = part if acc[x] is None else acc[x] + part
+        acc = [middle_ref[x, sl, :] for x in range(MX)]
+        places = [(i, i - MX if i < MX else i) for i in range(2 * MX)]
+        acc = along_x(acc, tap_at, 1, places, lambda term, i, sl=sl: small_ref[term, i, sl, :])
         for x in range(MX):
             add_ref[x, pl.ds(tile * 16, 8, stride=2), :] = acc[x]
             add_ref[x, pl.ds(tile * 16 + 1, 8, stride=2), :] = acc[x]
 
     def tile_step(tile, carry):
         sl = pl.ds(pl.multiple_of(tile * 8, 8), 8)
-        acc = [add_ref[x // 2, sl, :] for x in range(BX)]
-        for term in range(TERMS):
-            for place in range(2 * BX):
-                if place < 8:
-                    value = ring_ref[term, place, sl, :]
-                elif place < 24:
-                    value = fine_ref[term, place - 8, sl, :]
-                else:
-                    value = ring_ref[term, place - 16, sl, :]
-                for x in range(BX):
-                    offset = place - x - RADIUS
-                    if abs(offset) <= RADIUS:
-                        acc[x] = acc[x] + tap_at(term * TAPS + abs(offset)) * value
+        acc = [fine_ref[x, sl, :] + add_ref[x // 2, sl, :] for x in range(BX)]
+        places = [(i, i - 8 if i < 8 else i + 8) for i in range(16)]
+        acc = along_x(acc, tap_at, 0, places, lambda term, i: ring_ref[term, i, sl, :])
         for x in range(BX):
             out_ref[x, sl, :] = acc[x]
         return carry
@@ -503,10 +513,11 @@
     x_low, x_high = ring(x_up, "gx", 1), ring(x_down, "gx", -1)
     fine, middle = call(
         own_kernel,
-        [((TERMS, BX, BY, 128), F32), ((TERMS, MX, MY, 128), F32)],
-        [charges, mid, halo, low, high] + bands,
+        [((BX, BY, BZ), F32), ((MX, MY, 128), F32)],
+        [charges, mid, halo, low, high] + bands + [cx],
+        [pltpu.VMEM((TERMS, BX, BY, 128), F32), pltpu.VMEM((TERMS, MX, MY, 128), F32)],
         flops=10**8,
-        limit=8,
+        limit=10,
     )
     (near,) = call(
         near_kernel,

time: 61 us -> 61 us (level)
  no operation moved by 1% of the time
where the time goes in v7:
time: 61 us; the launch traced here: 60.7 us
  starting transfers between devices  37.8 us (62%)
  waiting for transfers between devices  12.2 us (20%)
  Pallas kernels  10.6 us (17%)
    ppermute x6, starting transfers between devices, ring(): lax.ppermute(value, axis, [(i, (i + step) % count) for i in range(count)])  21.4 us
    all_to_all x2, starting transfers between devices, exchange(): return lax.all_to_all(value, axis, 0, 0, tiled=True)  16.5 us
    all_to_all x2, waiting for transfers between devices, exchange(): return lax.all_to_all(value, axis, 0, 0, tiled=True)  10.6 us
    pallas_call x8, Pallas kernels, call(): pl.pallas_call(kernel, out_shape=[jax.ShapeDtypeStruct(shape, dtype) for...  10.6 us
    ppermute x6, waiting for transfers between devices, ring(): lax.ppermute(value, axis, [(i, (i + step) % count) for i in range(count)])  1.55 us
  transfers between devices with their start and end apart: 8, of which 3 were waited for; matrix products, arithmetic and copies ran while one was open for 0% of the time, Pallas kernels for 13%

profile of v7, /device:TPU:1, one launch (start us, length us, event | category | flops | bytes accessed | tf_op | source)
XLA Modules:
  0.0 60.7 jit_solution(12491720740625958069)
XLA Ops:
  0.0 2.0 %shard_map.82 = (f32[16,8,128]{2,1,0:T(8,128)}, f32[4,16,128]{2,1,0:T(8,128)S(1)}, f32[80,128]{1,0:T(8,128)S(1)}, f32[80,128]{1,0:T(8,128)S(1)}, f32[16,32,128]{...) custom-call(f32[16,32,128]{2,1,0:T(8,128)} %refs_0_.1, ...), custom_call_target="tpu_custom_call" | custom-call | flops 10000000 | bytes 1728576 | tf_op jit(solution)/shard_map/pallas_call | solution.py:441
  2.0 3.9 %collective-permute-start = (f32[80,128]{1,0:T(8,128)S(1)}, f32[80,128]{1,0:T(8,128)S(1)}, u32[]{:S(2)}, u32[]{:S(2)}) collective-permute-start(f32[80,128]{1,0:T(8,128)S(1)} %get-tuple-element.33), channel_id=1, source_target_pairs={{0,1},{1,2},{2,3},{3,0},{4,5},{5,6},{6,7},{7,4},{8,9},{9,10},{10,1... | collective-permute-start | bytes 122888 | tf_op jit(solution)/shard_map/ppermute | solution.py:454
  6.0 3.2 %collective-permute-start.1 = (f32[80,128]{1,0:T(8,128)S(1)}, f32[80,128]{1,0:T(8,128)S(1)}, u32[]{:S(2)}, u32[]{:S(2)}) collective-permute-start(f32[80,128]{1,0:T(8,128)S(1)} %get-tuple-element.34), channel_id=1, source_target_pairs={{0,3},{1,0},{2,1},{3,2},{4,7},{5,4},{6,5},{7,6},{8,11},{9,8},{10,9... | collective-permute-start | bytes 122888 | tf_op jit(solution)/shard_map/ppermute | solution.py:454
  9.2 0.0 collective-permute-done.zlow_ref
  9.2 1.5 %collective-permute-done.1.zhigh_ref = f32[80,128]{1,0:T(8,128)S(1)} collective-permute-done((f32[80,128]{1,0:T(8,128)S(1)}, f32[80,128]{1,0:T(8,128)S(1)}, u32[]{:S(2)}, u32[]{:S(2)}) %collective-permute-start.1) | collective-permute-done | bytes 40992 | tf_op jit(solution)/shard_map/ppermute | solution.py:454
  10.7 4.0 %collective-permute-start.2 = (f32[184,128]{1,0:T(8,128)S(1)}, f32[184,128]{1,0:T(8,128)S(1)}, u32[]{:S(2)}, u32[]{:S(2)}) collective-permute-start(f32[184,128]{1,0:T(8,128)S(1)} %get-tuple-element.36), channel_id=1, source_target_pairs={{0,4},{4,8},{8,12},{12,16},{16,20},{20,24},{24,28},{28,0},{1,5},{5... | collective-permute-start | bytes 282632 | tf_op jit(solution)/shard_map/ppermute | solution.py:454
  14.7 8.6 %collective-permute-start.3 = (f32[184,128]{1,0:T(8,128)S(1)}, f32[184,128]{1,0:T(8,128)S(1)}, u32[]{:S(2)}, u32[]{:S(2)}) collective-permute-start(f32[184,128]{1,0:T(8,128)S(1)} %get-tuple-element.37), channel_id=1, source_target_pairs={{0,28},{4,0},{8,4},{12,8},{16,12},{20,16},{24,20},{28,24},{1,29},{... | collective-permute-start | bytes 282632 | tf_op jit(solution)/shard_map/ppermute | solution.py:454
  23.3 9.5 %all-to-all-start = ((f32[16,8,128]{2,1,0:T(8,128)}), f32[16,8,128]{2,1,0:T(8,128)S(1)}, u32[]{:S(2)}, u32[]{:S(2)}) async-start(f32[16,8,128]{2,1,0:T(8,128)} %get-tuple-element.51), calls=%async_computation | async-start | bytes 131072 | tf_op jit(solution)/shard_map/all_to_all | solution.py:458
  32.8 0.0 collective-permute-done.2.low_ref
  32.8 0.0 collective-permute-done.3.high_ref
  32.9 1.6 %collective-permute-start.4 = (f32[592,128]{1,0:T(8,128)S(1)}, f32[592,128]{1,0:T(8,128)S(1)}, u32[]{:S(2)}, u32[]{:S(2)}) collective-permute-start(f32[592,128]{1,0:T(8,128)S(1)} %get-tuple-element.38), channel_id=1, source_target_pairs={{0,32},{32,64},{64,96},{96,128},{128,160},{160,192},{192,224},{224... | collective-permute-start | bytes 909320 | tf_op jit(solution)/shard_map/ppermute | solution.py:454
  34.6 0.0 collective-permute-start.5
  34.6 6.3 %all-to-all-done.columns_ref = f32[16,8,128]{2,1,0:T(8,128)S(1)} async-done(((f32[16,8,128]{2,1,0:T(8,128)}), f32[16,8,128]{2,1,0:T(8,128)S(1)}, u32[]{:S(2)}, u32[]{:S(2)}) %all-to-all-start) | async-done | bytes 65568 | tf_op jit(solution)/shard_map/all_to_all | solution.py:458
  40.9 2.2 %shard_map.88 = f32[32,8,128]{2,1,0:T(8,128)} custom-call(f32[16,8,128]{2,1,0:T(8,128)S(1)} %all-to-all-done.columns_ref, bf16[64,192]{1,0:T(8,128)(2,1)S(1)} %get-tuple-element.52.cas_y_ref, bf16[8,64,32]{2,1,0:T(8,128)(2,1)S(1)} %get-tuple-element.53.own_y_ref, bf16[2,128,128]{2,1,0:T(8,128)(2,1)S(1)} %get-tuple-element.54.cas_z_ref, ...), custom_call_target="tpu_custom_call" | custom-call | flops 50000000 | bytes 1531904 | tf_op jit(solution)/shard_map/pallas_call | solution.py:441
  43.1 7.0 %all-to-all-start.1 = ((f32[32,8,128]{2,1,0:T(8,128)}), f32[32,8,128]{2,1,0:T(8,128)S(1)}, u32[]{:S(2)}, u32[]{:S(2)}) async-start(f32[32,8,128]{2,1,0:T(8,128)} %shard_map.88), calls=%async_computation.1 | async-start | bytes 262144 | tf_op jit(solution)/shard_map/all_to_all | solution.py:458
  50.0 0.5 shard_map.85
  50.5 2.5 %shard_map.86 = (f32[16,32,128]{2,1,0:T(8,128)S(1)}, f32[8,16,128]{2,1,0:T(8,128)S(1)}) custom-call(f32[16,32,128]{2,1,0:T(8,128)S(1)} %get-tuple-element.31.f_ref, f32[4,16,128]{2,1,0:T(8,128)S(1)} %get-tuple-element.32.mid_ref, f32[80,128]{1,0:T(8,128)S(1)} %get-tuple-element.35.halo_ref, f32[184,128]{1,0:T(8,128)S(1)} %collective-permute-done.2.low_ref, ...), custom_call_target="tpu_custom_call" | custom-call | flops 100000000 | bytes 1396736 | tf_op jit(solution)/shard_map/pallas_call | solution.py:441
  53.0 0.0 collective-permute-done.4.low_ref
  53.0 0.0 collective-permute-done.5.high_ref
  53.0 2.4 %shard_map.87.near_ref = f32[16,32,128]{2,1,0:T(8,128)S(1)} custom-call(f32[592,128]{1,0:T(8,128)S(1)} %collective-permute-done.4.low_ref, f32[592,128]{1,0:T(8,128)S(1)} %collective-permute-done.5.high_ref, f32[16,32,128]{2,1,0:T(8,128)S(1)} %get-tuple-element.49.fine_ref, f32[8,16,128]{2,1,0:T(8,128)S(1)} %get-tuple-element.50.middle_ref, ...), custom_call_target="tpu_custom_call" | custom-call | flops 100000000 | bytes 1806336 | tf_op jit(solution)/shard_map/pallas_call | solution.py:441
  55.5 4.3 %all-to-all-done.1.top_ref = f32[32,8,128]{2,1,0:T(8,128)S(1)} async-done(((f32[32,8,128]{2,1,0:T(8,128)}), f32[32,8,128]{2,1,0:T(8,128)S(1)}, u32[]{:S(2)}, u32[]{:S(2)}) %all-to-all-start.1) | async-done | bytes 131104 | tf_op jit(solution)/shard_map/all_to_all | solution.py:458
  59.8 0.9 %shard_map.89 = f32[16,32,128]{2,1,0:T(8,128)} custom-call(f32[16,32,128]{2,1,0:T(8,128)S(1)} %shard_map.87.near_ref, f32[32,8,128]{2,1,0:T(8,128)S(1)} %all-to-all-done.1.top_ref), custom_call_target="tpu_custom_call" | custom-call | flops 1000000 | bytes 393216 | tf_op jit(solution)/shard_map/pallas_call | solution.py:441
  (2 shorter events, 0.1 us)
Async XLA Ops:
  2.0 7.1 %collective-permute-start = (f32[80,128]{1,0:T(8,128)S(1)}, f32[80,128]{1,0:T(8,128)S(1)}, u32[]{:S(2)}, u32[]{:S(2)}) collective-permute-start(f32[80,128]{1,0:T(8,128)S(1)} %get-tuple-element.33), channel_id=1, source_target_pairs={{0,1},{1,2},{2,3},{3,0},{4,5},{5,6},{6,7},{7,4},{8,9},{9,10},{10,1... | collective-permute-start | bytes 122888 | tf_op jit(solution)/shard_map/ppermute | solution.py:454
  6.0 4.7 %collective-permute-start.1 = (f32[80,128]{1,0:T(8,128)S(1)}, f32[80,128]{1,0:T(8,128)S(1)}, u32[]{:S(2)}, u32[]{:S(2)}) collective-permute-start(f32[80,128]{1,0:T(8,128)S(1)} %get-tuple-element.34), channel_id=1, source_target_pairs={{0,3},{1,0},{2,1},{3,2},{4,7},{5,4},{6,5},{7,6},{8,11},{9,8},{10,9... | collective-permute-start | bytes 122888 | tf_op jit(solution)/shard_map/ppermute | solution.py:454
  10.7 22.1 %collective-permute-start.2 = (f32[184,128]{1,0:T(8,128)S(1)}, f32[184,128]{1,0:T(8,128)S(1)}, u32[]{:S(2)}, u32[]{:S(2)}) collective-permute-start(f32[184,128]{1,0:T(8,128)S(1)} %get-tuple-element.36), channel_id=1, source_target_pairs={{0,4},{4,8},{8,12},{12,16},{16,20},{20,24},{24,28},{28,0},{1,5},{5... | collective-permute-start | bytes 282632 | tf_op jit(solution)/shard_map/ppermute | solution.py:454
  14.7 18.1 %collective-permute-start.3 = (f32[184,128]{1,0:T(8,128)S(1)}, f32[184,128]{1,0:T(8,128)S(1)}, u32[]{:S(2)}, u32[]{:S(2)}) collective-permute-start(f32[184,128]{1,0:T(8,128)S(1)} %get-tuple-element.37), channel_id=1, source_target_pairs={{0,28},{4,0},{8,4},{12,8},{16,12},{20,16},{24,20},{28,24},{1,29},{... | collective-permute-start | bytes 282632 | tf_op jit(solution)/shard_map/ppermute | solution.py:454
  23.3 17.6 %all-to-all-start = ((f32[16,8,128]{2,1,0:T(8,128)}), f32[16,8,128]{2,1,0:T(8,128)S(1)}, u32[]{:S(2)}, u32[]{:S(2)}) async-start(f32[16,8,128]{2,1,0:T(8,128)} %get-tuple-element.51), calls=%async_computation | async-start | bytes 131072 | tf_op jit(solution)/shard_map/all_to_all | solution.py:458
  32.9 20.1 %collective-permute-start.4 = (f32[592,128]{1,0:T(8,128)S(1)}, f32[592,128]{1,0:T(8,128)S(1)}, u32[]{:S(2)}, u32[]{:S(2)}) collective-permute-start(f32[592,128]{1,0:T(8,128)S(1)} %get-tuple-element.38), channel_id=1, source_target_pairs={{0,32},{32,64},{64,96},{96,128},{128,160},{160,192},{192,224},{224... | collective-permute-start | bytes 909320 | tf_op jit(solution)/shard_map/ppermute | solution.py:454
  34.6 18.5 %collective-permute-start.5 = (f32[592,128]{1,0:T(8,128)S(1)}, f32[592,128]{1,0:T(8,128)S(1)}, u32[]{:S(2)}, u32[]{:S(2)}) collective-permute-start(f32[592,128]{1,0:T(8,128)S(1)} %get-tuple-element.39), channel_id=1, source_target_pairs={{0,480},{32,0},{64,32},{96,64},{128,96},{160,128},{192,160},{224,1... | collective-permute-start | bytes 909320 | tf_op jit(solution)/shard_map/ppermute | solution.py:454
  43.1 16.7 %all-to-all-start.1 = ((f32[32,8,128]{2,1,0:T(8,128)}), f32[32,8,128]{2,1,0:T(8,128)S(1)}, u32[]{:S(2)}, u32[]{:S(2)}) async-start(f32[32,8,128]{2,1,0:T(8,128)} %shard_map.88), calls=%async_computation.1 | async-start | bytes 262144 | tf_op jit(solution)/shard_map/all_to_all | solution.py:458

commit v8 on v7

--- a/solution.py
+++ b/solution.py
@@ -290,7 +290,7 @@
 
 
 def filter_yz(planes, sides, gy, gzh_ref, gzl_ref, out_ref, places):
-    for group in range(2):
+    for group in range(len(sides)):
         data = jnp.concatenate([planes[group * 8 + x]() for x in range(8)] + [sides[group]()], axis=1)
         high, low = halves(data)
         by_y = dot(gy, jnp.concatenate([high, low, high], axis=0))
@@ -368,26 +368,53 @@
     lax.fori_loop(0, BY // 8, tile_step, 0)
 
 
-def near_kernel(
-    low_ref, high_ref, fine_ref, middle_ref, gy_ref, gzh_ref, gzl_ref, my_ref, mzh_ref, mzl_ref, cx_ref,
-    out_ref, ring_ref, small_ref, add_ref,
+def ring_planes(ref, high, gy, gzh_ref, gzl_ref, my, mzh_ref, mzl_ref, ring_ref, small_ref):
+    planes = [lambda x=x: ref[x * EY : (x + 1) * EY, :] for x in range(8)]
+    filter_yz(planes, [lambda: ref[8 * EY : 9 * EY, :]], gy, gzh_ref, gzl_ref, ring_ref, list(range(8)))
+    middle = [lambda x=x: ref[9 * EY + x * EMY : 9 * EY + (x + 1) * EMY, :] for x in range(4)]
+    edge = lambda: ref[9 * EY + 4 * EMY : 9 * EY + 5 * EMY, :]
+    filter_middle(middle, edge, my, mzh_ref, mzl_ref, small_ref, 0)
+    return [(i, BX + i if high else i - 8) for i in range(8)], [(i, MX + i if high else i - MX) for i in range(MX)]
+
+
+def low_kernel(
+    low_ref, fine_ref, middle_ref, gy_ref, gzh_ref, gzl_ref, my_ref, mzh_ref, mzl_ref, cx_ref,
+    out_ref, outm_ref, ring_ref, small_ref,
 ):
-    planes, sides = [], []
-    for ref in (low_ref, high_ref):
-        planes += [lambda ref=ref, x=x: ref[x * EY : (x + 1) * EY, :] for x in range(8)]
-        sides.append(lambda ref=ref: ref[8 * EY : 9 * EY, :])
-    filter_yz(planes, sides, gy_ref[...], gzh_ref, gzl_ref, ring_ref, list(range(16)))
-    for index, ref in enumerate((low_ref, high_ref)):
-        middle = [lambda ref=ref, x=x: ref[9 * EY + x * EMY : 9 * EY + (x + 1) * EMY, :] for x in range(4)]
-        edge = lambda ref=ref: ref[9 * EY + 4 * EMY : 9 * EY + 5 * EMY, :]
-        filter_middle(middle, edge, my_ref[...], mzh_ref, mzl_ref, small_ref, index * MX)
-
+    fine, middle = ring_planes(
+        low_ref, False, gy_ref[...], gzh_ref, gzl_ref, my_ref[...], mzh_ref, mzl_ref, ring_ref, small_ref
+    )
     tap_at = tap_rows(cx_ref)
     for tile in range(MY // 8):
         sl = slice(tile * 8, tile * 8 + 8)
         acc = [middle_ref[x, sl, :] for x in range(MX)]
-        places = [(i, i - MX if i < MX else i) for i in range(2 * MX)]
-        acc = along_x(acc, tap_at, 1, places, lambda term, i, sl=sl: small_ref[term, i, sl, :])
+        acc = along_x(acc, tap_at, 1, middle, lambda term, i, sl=sl: small_ref[term, i, sl, :])
+        for x in range(MX):
+            outm_ref[x, sl, :] = acc[x]
+
+    def tile_step(tile, carry):
+        sl = pl.ds(pl.multiple_of(tile * 8, 8), 8)
+        acc = [fine_ref[x, sl, :] for x in range(BX)]
+        acc = along_x(acc, tap_at, 0, fine, lambda term, i: ring_ref[term, i, sl, :])
+        for x in range(BX):
+            out_ref[x, sl, :] = acc[x]
+        return carry
+
+    lax.fori_loop(0, BY // 8, tile_step, 0)
+
+
+def near_kernel(
+    high_ref, fine_ref, middle_ref, gy_ref, gzh_ref, gzl_ref, my_ref, mzh_ref, mzl_ref, cx_ref,
+    out_ref, ring_ref, small_ref, add_ref,
+):
+    fine, middle = ring_planes(
+        high_ref, True, gy_ref[...], gzh_ref, gzl_ref, my_ref[...], mzh_ref, mzl_ref, ring_ref, small_ref
+    )
+    tap_at = tap_rows(cx_ref)
+    for tile in range(MY // 8):
+        sl = slice(tile * 8, tile * 8 + 8)
+        acc = [middle_ref[x, sl, :] for x in range(MX)]
+        acc = along_x(acc, tap_at, 1, middle, lambda term, i, sl=sl: small_ref[term, i, sl, :])
         for x in range(MX):
             add_ref[x, pl.ds(tile * 16, 8, stride=2), :] = acc[x]
             add_ref[x, pl.ds(tile * 16 + 1, 8, stride=2), :] = acc[x]
@@ -395,8 +422,7 @@
     def tile_step(tile, carry):
         sl = pl.ds(pl.multiple_of(tile * 8, 8), 8)
         acc = [fine_ref[x, sl, :] + add_ref[x // 2, sl, :] for x in range(BX)]
-        places = [(i, i - 8 if i < 8 else i + 8) for i in range(16)]
-        acc = along_x(acc, tap_at, 0, places, lambda term, i: ring_ref[term, i, sl, :])
+        acc = along_x(acc, tap_at, 0, fine, lambda term, i: ring_ref[term, i, sl, :])
         for x in range(BX):
             out_ref[x, sl, :] = acc[x]
         return carry
@@ -519,17 +545,22 @@
         flops=10**8,
         limit=10,
     )
+    scratch = [pltpu.VMEM((TERMS, 8, BY, 128), F32), pltpu.VMEM((TERMS, MX, MY, 128), F32)]
+    fine, middle = call(
+        low_kernel,
+        [((BX, BY, BZ), F32), ((MX, MY, 128), F32)],
+        [x_low, fine, middle] + bands + [cx],
+        scratch,
+        flops=10**8,
+        limit=8,
+    )
     (near,) = call(
         near_kernel,
         [((BX, BY, BZ), F32)],
-        [x_low, x_high, fine, middle] + bands + [cx],
-        [
-            pltpu.VMEM((TERMS, 16, BY, 128), F32),
-            pltpu.VMEM((TERMS, 16, MY, 128), F32),
-            pltpu.VMEM((MX, BY, 128), F32),
-        ],
+        [x_high, fine, middle] + bands + [cx],
+        scratch + [pltpu.VMEM((MX, BY, 128), F32)],
         flops=10**8,
-        limit=10,
+        limit=8,
     )
     (result,) = call(
         add_kernel,

time: 61 us -> 61 us (level)
    pallas_call x8 -> x9, Pallas kernels: 10.6 us -> 10.7 us  [call(): pl.pallas_call(kernel, out_shape=[jax.ShapeDtypeStruct(shape, dtype) for...]
where the time goes in v8:
time: 61 us; the launch traced here: 60.7 us
  starting transfers between devices  37.8 us (62%)
  waiting for transfers between devices  12 us (20%)
  Pallas kernels  10.7 us (18%)
    ppermute x6, starting transfers between devices, ring(): lax.ppermute(value, axis, [(i, (i + step) % count) for i in range(count)])  21.4 us
    all_to_all x2, starting transfers between devices, exchange(): return lax.all_to_all(value, axis, 0, 0, tiled=True)  16.5 us
    pallas_call x9, Pallas kernels, call(): pl.pallas_call(kernel, out_shape=[jax.ShapeDtypeStruct(shape, dtype) for...  10.7 us
    all_to_all x2, waiting for transfers between devices, exchange(): return lax.all_to_all(value, axis, 0, 0, tiled=True)  10.5 us
    ppermute x6, waiting for transfers between devices, ring(): lax.ppermute(value, axis, [(i, (i + step) % count) for i in range(count)])  1.55 us
  transfers between devices with their start and end apart: 8, of which 3 were waited for; matrix products, arithmetic and copies ran while one was open for 0% of the time, Pallas kernels for 13%

profile of v8, /device:TPU:1, one launch (start us, length us, event | category | flops | bytes accessed | tf_op | source)
XLA Modules:
  0.0 60.7 jit_solution(15282487538451555484)
XLA Ops:
  0.0 2.0 %shard_map.82 = (f32[16,8,128]{2,1,0:T(8,128)}, f32[4,16,128]{2,1,0:T(8,128)S(1)}, f32[80,128]{1,0:T(8,128)S(1)}, f32[80,128]{1,0:T(8,128)S(1)}, f32[16,32,128]{...) custom-call(f32[16,32,128]{2,1,0:T(8,128)} %refs_0_.1, ...), custom_call_target="tpu_custom_call" | custom-call | flops 10000000 | bytes 1728576 | tf_op jit(solution)/shard_map/pallas_call | solution.py:467
  2.0 3.9 %collective-permute-start = (f32[80,128]{1,0:T(8,128)S(1)}, f32[80,128]{1,0:T(8,128)S(1)}, u32[]{:S(2)}, u32[]{:S(2)}) collective-permute-start(f32[80,128]{1,0:T(8,128)S(1)} %get-tuple-element.35), channel_id=1, source_target_pairs={{0,1},{1,2},{2,3},{3,0},{4,5},{5,6},{6,7},{7,4},{8,9},{9,10},{10,1... | collective-permute-start | bytes 122888 | tf_op jit(solution)/shard_map/ppermute | solution.py:480
  6.0 3.2 %collective-permute-start.1 = (f32[80,128]{1,0:T(8,128)S(1)}, f32[80,128]{1,0:T(8,128)S(1)}, u32[]{:S(2)}, u32[]{:S(2)}) collective-permute-start(f32[80,128]{1,0:T(8,128)S(1)} %get-tuple-element.36), channel_id=1, source_target_pairs={{0,3},{1,0},{2,1},{3,2},{4,7},{5,4},{6,5},{7,6},{8,11},{9,8},{10,9... | collective-permute-start | bytes 122888 | tf_op jit(solution)/shard_map/ppermute | solution.py:480
  9.2 0.0 collective-permute-done.zlow_ref
  9.2 1.5 %collective-permute-done.1.zhigh_ref = f32[80,128]{1,0:T(8,128)S(1)} collective-permute-done((f32[80,128]{1,0:T(8,128)S(1)}, f32[80,128]{1,0:T(8,128)S(1)}, u32[]{:S(2)}, u32[]{:S(2)}) %collective-permute-start.1) | collective-permute-done | bytes 40992 | tf_op jit(solution)/shard_map/ppermute | solution.py:480
  10.7 4.0 %collective-permute-start.2 = (f32[184,128]{1,0:T(8,128)S(1)}, f32[184,128]{1,0:T(8,128)S(1)}, u32[]{:S(2)}, u32[]{:S(2)}) collective-permute-start(f32[184,128]{1,0:T(8,128)S(1)} %get-tuple-element.38), channel_id=1, source_target_pairs={{0,4},{4,8},{8,12},{12,16},{16,20},{20,24},{24,28},{28,0},{1,5},{5... | collective-permute-start | bytes 282632 | tf_op jit(solution)/shard_map/ppermute | solution.py:480
  14.7 8.6 %collective-permute-start.3 = (f32[184,128]{1,0:T(8,128)S(1)}, f32[184,128]{1,0:T(8,128)S(1)}, u32[]{:S(2)}, u32[]{:S(2)}) collective-permute-start(f32[184,128]{1,0:T(8,128)S(1)} %get-tuple-element.39), channel_id=1, source_target_pairs={{0,28},{4,0},{8,4},{12,8},{16,12},{20,16},{24,20},{28,24},{1,29},{... | collective-permute-start | bytes 282632 | tf_op jit(solution)/shard_map/ppermute | solution.py:480
  23.3 9.5 %all-to-all-start = ((f32[16,8,128]{2,1,0:T(8,128)}), f32[16,8,128]{2,1,0:T(8,128)S(1)}, u32[]{:S(2)}, u32[]{:S(2)}) async-start(f32[16,8,128]{2,1,0:T(8,128)} %get-tuple-element.55), calls=%async_computation | async-start | bytes 131072 | tf_op jit(solution)/shard_map/all_to_all | solution.py:484
  32.8 0.0 collective-permute-done.2.low_ref
  32.8 0.0 collective-permute-done.3.high_ref
  32.9 1.6 %collective-permute-start.5 = (f32[592,128]{1,0:T(8,128)S(1)}, f32[592,128]{1,0:T(8,128)S(1)}, u32[]{:S(2)}, u32[]{:S(2)}) collective-permute-start(f32[592,128]{1,0:T(8,128)S(1)} %get-tuple-element.41), channel_id=1, source_target_pairs={{0,32},{32,64},{64,96},{96,128},{128,160},{160,192},{192,224},{224... | collective-permute-start | bytes 909320 | tf_op jit(solution)/shard_map/ppermute | solution.py:480
  34.6 0.0 collective-permute-start.4
  34.6 6.3 %all-to-all-done.columns_ref = f32[16,8,128]{2,1,0:T(8,128)S(1)} async-done(((f32[16,8,128]{2,1,0:T(8,128)}), f32[16,8,128]{2,1,0:T(8,128)S(1)}, u32[]{:S(2)}, u32[]{:S(2)}) %all-to-all-start) | async-done | bytes 65568 | tf_op jit(solution)/shard_map/all_to_all | solution.py:484
  40.9 2.2 %shard_map.89 = f32[32,8,128]{2,1,0:T(8,128)} custom-call(f32[16,8,128]{2,1,0:T(8,128)S(1)} %all-to-all-done.columns_ref, bf16[64,192]{1,0:T(8,128)(2,1)S(1)} %get-tuple-element.56.cas_y_ref, bf16[8,64,32]{2,1,0:T(8,128)(2,1)S(1)} %get-tuple-element.57.own_y_ref, bf16[2,128,128]{2,1,0:T(8,128)(2,1)S(1)} %get-tuple-element.58.cas_z_ref, ...), custom_call_target="tpu_custom_call" | custom-call | flops 50000000 | bytes 1531904 | tf_op jit(solution)/shard_map/pallas_call | solution.py:467
  43.1 7.0 %all-to-all-start.1 = ((f32[32,8,128]{2,1,0:T(8,128)}), f32[32,8,128]{2,1,0:T(8,128)S(1)}, u32[]{:S(2)}, u32[]{:S(2)}) async-start(f32[32,8,128]{2,1,0:T(8,128)} %shard_map.89), calls=%async_computation.1 | async-start | bytes 262144 | tf_op jit(solution)/shard_map/all_to_all | solution.py:484
  50.0 0.5 shard_map.85
  50.5 2.5 %shard_map.86 = (f32[16,32,128]{2,1,0:T(8,128)S(1)}, f32[8,16,128]{2,1,0:T(8,128)S(1)}) custom-call(f32[16,32,128]{2,1,0:T(8,128)S(1)} %get-tuple-element.33.f_ref, f32[4,16,128]{2,1,0:T(8,128)S(1)} %get-tuple-element.34.mid_ref, f32[80,128]{1,0:T(8,128)S(1)} %get-tuple-element.37.halo_ref, f32[184,128]{1,0:T(8,128)S(1)} %collective-permute-done.2.low_ref, ...), custom_call_target="tpu_custom_call" | custom-call | flops 100000000 | bytes 1396736 | tf_op jit(solution)/shard_map/pallas_call | solution.py:467
  53.0 0.0 collective-permute-done.5.low_ref
  53.0 1.3 %shard_map.87 = (f32[16,32,128]{2,1,0:T(8,128)S(1)}, f32[8,16,128]{2,1,0:T(8,128)S(1)}) custom-call(f32[592,128]{1,0:T(8,128)S(1)} %collective-permute-done.5.low_ref, f32[16,32,128]{2,1,0:T(8,128)S(1)} %get-tuple-element.51.fine_ref, f32[8,16,128]{2,1,0:T(8,128)S(1)} %get-tuple-element.52.middle_ref, bf16[128,144]{1,0:T(8,128)(2,1)S(1)} %get-tuple-element.44.gy_ref, ...), custom_call_target="tpu_custom_call" | custom-call | flops 100000000 | bytes 1503232 | tf_op jit(solution)/shard_map/pallas_call | solution.py:467
  54.3 0.0 collective-permute-done.4.high_ref
  54.3 1.3 %shard_map.88.near_ref = f32[16,32,128]{2,1,0:T(8,128)S(1)} custom-call(f32[592,128]{1,0:T(8,128)S(1)} %collective-permute-done.4.high_ref, f32[16,32,128]{2,1,0:T(8,128)S(1)} %get-tuple-element.53.fine_ref, f32[8,16,128]{2,1,0:T(8,128)S(1)} %get-tuple-element.54.middle_ref, bf16[128,144]{1,0:T(8,128)(2,1)S(1)} %get-tuple-element.44.gy_ref, ...), custom_call_target="tpu_custom_call" | custom-call | flops 100000000 | bytes 1503232 | tf_op jit(solution)/shard_map/pallas_call | solution.py:467
  55.6 4.1 %all-to-all-done.1.top_ref = f32[32,8,128]{2,1,0:T(8,128)S(1)} async-done(((f32[32,8,128]{2,1,0:T(8,128)}), f32[32,8,128]{2,1,0:T(8,128)S(1)}, u32[]{:S(2)}, u32[]{:S(2)}) %all-to-all-start.1) | async-done | bytes 131104 | tf_op jit(solution)/shard_map/all_to_all | solution.py:484
  59.8 0.9 %shard_map.90 = f32[16,32,128]{2,1,0:T(8,128)} custom-call(f32[16,32,128]{2,1,0:T(8,128)S(1)} %shard_map.88.near_ref, f32[32,8,128]{2,1,0:T(8,128)S(1)} %all-to-all-done.1.top_ref), custom_call_target="tpu_custom_call" | custom-call | flops 1000000 | bytes 393216 | tf_op jit(solution)/shard_map/pallas_call | solution.py:467
  (2 shorter events, 0.1 us)
Async XLA Ops:
  2.0 7.1 %collective-permute-start = (f32[80,128]{1,0:T(8,128)S(1)}, f32[80,128]{1,0:T(8,128)S(1)}, u32[]{:S(2)}, u32[]{:S(2)}) collective-permute-start(f32[80,128]{1,0:T(8,128)S(1)} %get-tuple-element.35), channel_id=1, source_target_pairs={{0,1},{1,2},{2,3},{3,0},{4,5},{5,6},{6,7},{7,4},{8,9},{9,10},{10,1... | collective-permute-start | bytes 122888 | tf_op jit(solution)/shard_map/ppermute | solution.py:480
  6.0 4.7 %collective-permute-start.1 = (f32[80,128]{1,0:T(8,128)S(1)}, f32[80,128]{1,0:T(8,128)S(1)}, u32[]{:S(2)}, u32[]{:S(2)}) collective-permute-start(f32[80,128]{1,0:T(8,128)S(1)} %get-tuple-element.36), channel_id=1, source_target_pairs={{0,3},{1,0},{2,1},{3,2},{4,7},{5,4},{6,5},{7,6},{8,11},{9,8},{10,9... | collective-permute-start | bytes 122888 | tf_op jit(solution)/shard_map/ppermute | solution.py:480
  10.7 22.1 %collective-permute-start.2 = (f32[184,128]{1,0:T(8,128)S(1)}, f32[184,128]{1,0:T(8,128)S(1)}, u32[]{:S(2)}, u32[]{:S(2)}) collective-permute-start(f32[184,128]{1,0:T(8,128)S(1)} %get-tuple-element.38), channel_id=1, source_target_pairs={{0,4},{4,8},{8,12},{12,16},{16,20},{20,24},{24,28},{28,0},{1,5},{5... | collective-permute-start | bytes 282632 | tf_op jit(solution)/shard_map/ppermute | solution.py:480
  14.7 18.1 %collective-permute-start.3 = (f32[184,128]{1,0:T(8,128)S(1)}, f32[184,128]{1,0:T(8,128)S(1)}, u32[]{:S(2)}, u32[]{:S(2)}) collective-permute-start(f32[184,128]{1,0:T(8,128)S(1)} %get-tuple-element.39), channel_id=1, source_target_pairs={{0,28},{4,0},{8,4},{12,8},{16,12},{20,16},{24,20},{28,24},{1,29},{... | collective-permute-start | bytes 282632 | tf_op jit(solution)/shard_map/ppermute | solution.py:480
  23.3 17.6 %all-to-all-start = ((f32[16,8,128]{2,1,0:T(8,128)}), f32[16,8,128]{2,1,0:T(8,128)S(1)}, u32[]{:S(2)}, u32[]{:S(2)}) async-start(f32[16,8,128]{2,1,0:T(8,128)} %get-tuple-element.55), calls=%async_computation | async-start | bytes 131072 | tf_op jit(solution)/shard_map/all_to_all | solution.py:484
  32.9 20.1 %collective-permute-start.5 = (f32[592,128]{1,0:T(8,128)S(1)}, f32[592,128]{1,0:T(8,128)S(1)}, u32[]{:S(2)}, u32[]{:S(2)}) collective-permute-start(f32[592,128]{1,0:T(8,128)S(1)} %get-tuple-element.41), channel_id=1, source_target_pairs={{0,32},{32,64},{64,96},{96,128},{128,160},{160,192},{192,224},{224... | collective-permute-start | bytes 909320 | tf_op jit(solution)/shard_map/ppermute | solution.py:480
  34.6 19.8 %collective-permute-start.4 = (f32[592,128]{1,0:T(8,128)S(1)}, f32[592,128]{1,0:T(8,128)S(1)}, u32[]{:S(2)}, u32[]{:S(2)}) collective-permute-start(f32[592,128]{1,0:T(8,128)S(1)} %get-tuple-element.40), channel_id=1, source_target_pairs={{0,480},{32,0},{64,32},{96,64},{128,96},{160,128},{192,160},{224,1... | collective-permute-start | bytes 909320 | tf_op jit(solution)/shard_map/ppermute | solution.py:480
  43.1 16.7 %all-to-all-start.1 = ((f32[32,8,128]{2,1,0:T(8,128)}), f32[32,8,128]{2,1,0:T(8,128)S(1)}, u32[]{:S(2)}, u32[]{:S(2)}) async-start(f32[32,8,128]{2,1,0:T(8,128)} %shard_map.89), calls=%async_computation.1 | async-start | bytes 262144 | tf_op jit(solution)/shard_map/all_to_all | solution.py:484
